TPU v7x, 32 devices: a whole 2x2x4 slice. The times are simulated.
32 devices in a mesh: dom: 16 (over z, x, core), grp: 2 (over y).
Axes of the slice: x: 2, y: 2, z: 4, core: 2. Of those that a mesh axis runs over, the one named last changes fastest.
Arguments:
- positions: float32 [3, 2, 16384], P(None, 'grp', 'dom'), as said below
- species: int32 [2, 16384], P('grp', 'dom'), may hold values from 0 to 3
- neighbours: int32 [48, 2, 16384], P(None, 'grp', 'dom'), may hold values from 0 to 16383, as said below
- slot_counts: int32 [2, 16384], P('grp', 'dom'), may hold values from 20 to 48, as said below
- structure: int32 [2, 16384], P('grp', 'dom'), may hold values from 0 to 511, as said below
- target_energy: float32 [2, 512], P('grp'), may hold values from -6 to 6
- radial_one: float32 [10, 12], replicated, may hold values from -6 to 6
- coupling_one: bfloat16 [4, 1960, 512], replicated, may hold values from -0.3125 to 0.3125
- coefficient_one: float32 [4, 512], replicated, may hold values from -0.25 to 0.25
- mixing: float32 [512, 4], replicated, may hold values from -0.375 to 0.375
- radial_two: float32 [10, 12], replicated, may hold values from -6 to 6
- coupling_two: bfloat16 [4, 1960, 512], replicated, may hold values from -0.3125 to 0.3125
- coefficient_two: float32 [4, 512], replicated, may hold values from -0.25 to 0.25
Outputs:
- energies: float32 [2, 512], P('grp')
- offsets: float32 [4], replicated
- forces: float32 [3, 2, 16384], P(None, 'grp', 'dom')
- radial_first: float32 [10, 12], replicated
- coefficient_first: float32 [4, 512], replicated
- mixing_gradient: float32 [512, 4], replicated
- radial_second: float32 [10, 12], replicated
- coefficient_second: float32 [4, 512], replicated
Inputs may be any that keep to these rules, and one draw needn't show every extreme that they name: Atoms of one structure are consecutive within a group; structure numbers start at 0 in each group and rise by one, and every group holds exactly 512 structures; each structure holds a multiple of 8 atoms, from 8 to 4096. `neighbours`: each slot names another atom of the same structure; it lies in the same block of 1024 consecutive atoms of the group as the atom or in an adjacent block. An atom may be named in several slots of one atom. Slots k < slot_counts are live, the others are ignored. `positions`: any two atoms of one structure are 0.9 or more apart.
All inputs are finite; a program needn't handle non-finite values.
Results may differ from a plain program's by a relative error of at most 0.0085.
The roundings to bfloat16 on the way count: a program that leaves them out, or rounds other values in their place, can miss the bound.
Values sent between devices are 32-bit elements; how exact they have to be, the bound alone decides.
A program may use at most 320 MiB of HBM per device.

v0:
```python
from functools import partial, reduce
import math

import jax
import jax.numpy as jnp
from jax import lax
from jax.experimental import pallas as pl
from jax.experimental.pallas import tpu as pltpu
from jax.sharding import PartitionSpec as P

NRAD = 12
NMAX = 10
LMAX = 6
LM = 49
SPECIES = 4
CH = SPECIES * NMAX
DENS = CH * LM
NBR = 48
NPAD = 64
TILE = 128
LBLK = 7
WROWS = 4
NVAL = 7
SLOTS = 4

cutoff_radius = 5.0
density_scale = 0.17
norm_eps = 1e-05
ridge_weight = 0.1
highest = lax.Precision.HIGHEST
f32 = jnp.float32
MESH = pl.DeviceIdType.MESH
bf16 = jnp.bfloat16


def log2_of(count):
    steps = count.bit_length() - 1
    assert count == 1 << steps
    return steps


def neighbour_flags(me, count):
    return me > 0, me < count - 1


def greet(partners, flags):
    barrier = pltpu.get_barrier_semaphore()
    for partner, flag in zip(partners, flags):
        if flag is None:
            pl.semaphore_signal(barrier, inc=1, device_id=partner, device_id_type=MESH)
        else:

            @pl.when(flag)
            def _(partner=partner):
                pl.semaphore_signal(barrier, inc=1, device_id=partner, device_id_type=MESH)

    present = sum(1 for flag in flags if flag is None)
    for flag in flags:
        if flag is not None:
            present = present + jnp.where(flag, 1, 0)
    pl.semaphore_wait(barrier, present)


class SidePair:
    def __init__(self, to_left, to_right, got_ref, send_sem, recv_sem):
        count = lax.axis_size("dom")
        me = lax.axis_index("dom")
        self.partners = ({"dom": me - 1}, {"dom": me + 1})
        self.flags = neighbour_flags(me, count)
        self.got = got_ref
        self.copies = [
            pltpu.make_async_remote_copy(
                src_ref=source,
                dst_ref=got_ref.at[1 - side],
                send_sem=send_sem.at[side],
                recv_sem=recv_sem.at[1 - side],
                device_id=self.partners[side],
                device_id_type=MESH,
            )
            for side, source in enumerate((to_left, to_right))
        ]

    def start(self):
        for side in range(2):
            pl.when(self.flags[side])(self.copies[side].start)

    def wait(self):
        for side in range(2):

            @pl.when(self.flags[side])
            def _(side=side):
                self.copies[side].wait_send()
                self.copies[1 - side].wait_recv()

    def received(self, side):
        return jnp.where(self.flags[side], self.got[side], 0.0)


def spread_kernel(values, x_ref, out_ref, got_ref, send_sem, recv_sem):
    pair = SidePair(x_ref, x_ref, got_ref, send_sem, recv_sem)
    greet(pair.partners, pair.flags)
    pair.start()
    rows = x_ref.shape[0] // values
    for value in range(values):
        at = value * 3 * rows
        out_ref[at + rows : at + 2 * rows, :] = x_ref[value * rows : (value + 1) * rows, :]
    pair.wait()
    for side in range(2):
        block = pair.received(side)
        for value in range(values):
            at = value * 3 * rows + 2 * side * rows
            out_ref[at : at + rows, :] = block[value * rows : (value + 1) * rows]


def comm_params(which):
    return pltpu.CompilerParams(collective_id=which, has_side_effects=True)


def vmem_spec():
    return pl.BlockSpec(memory_space=pltpu.VMEM)


def spread_call(which, values, cells):
    rows = cells.shape[0]
    return pl.pallas_call(
        partial(spread_kernel, values),
        out_shape=jax.ShapeDtypeStruct((rows * 3, TILE), f32),
        in_specs=[vmem_spec()],
        out_specs=vmem_spec(),
        scratch_shapes=[
            pltpu.VMEM((2, rows, TILE), f32),
            pltpu.SemaphoreType.DMA((2,)),
            pltpu.SemaphoreType.DMA((2,)),
        ],
        compiler_params=comm_params(which),
        name="spread_%d" % which,
    )(cells)


def collect_kernel(rows, win_ref, out_ref, got_ref, send_sem, recv_sem):
    pair = SidePair(
        win_ref.at[:, 0:rows], win_ref.at[:, 2 * rows : 3 * rows], got_ref, send_sem, recv_sem
    )
    greet(pair.partners, pair.flags)
    pair.start()
    pair.wait()
    out_ref[...] = win_ref[:, rows : 2 * rows] + pair.received(0) + pair.received(1)


def collect_call(which, rows, window):
    values = window.shape[0]
    return pl.pallas_call(
        partial(collect_kernel, rows),
        out_shape=jax.ShapeDtypeStruct((values, rows, TILE), f32),
        in_specs=[vmem_spec()],
        out_specs=vmem_spec(),
        scratch_shapes=[
            pltpu.VMEM((2, values, rows, TILE), f32),
            pltpu.SemaphoreType.DMA((2,)),
            pltpu.SemaphoreType.DMA((2,)),
        ],
        compiler_params=comm_params(which),
        name="collect_%d" % which,
    )(window)


def finish_kernel(rows, sums_at, per_group, win_ref, own_ref, pay_ref, force_ref, sum_ref, energy_ref,
                  offset_ref, got_ref, came_ref, send_sem, recv_sem, step_send, step_recv):
    pair = SidePair(
        win_ref.at[:, 0:rows], win_ref.at[:, 2 * rows : 3 * rows], got_ref, send_sem, recv_sem
    )
    partners = []
    for axis in ("dom", "grp"):
        me = lax.axis_index(axis)
        for bit in range(log2_of(lax.axis_size(axis))):
            half = 1 << bit
            partners.append({axis: me + half - 2 * half * lax.rem(lax.div(me, half), 2)})
    greet(list(pair.partners) + partners, list(pair.flags) + [None] * len(partners))
    pair.start()
    for step, partner in enumerate(partners):
        source = pay_ref if step == 0 else sum_ref
        copy = pltpu.make_async_remote_copy(
            src_ref=source,
            dst_ref=came_ref.at[step],
            send_sem=step_send.at[step],
            recv_sem=step_recv.at[step],
            device_id=partner,
            device_id_type=MESH,
        )
        copy.start()
        copy.wait()
        sum_ref[...] = source[...] + came_ref[step]
    pair.wait()
    force_ref[...] = (
        own_ref[...] - win_ref[:, rows : 2 * rows] - pair.received(0) - pair.received(1)
    )

    groups = lax.axis_size("grp")
    gram = [[None] * SPECIES for _ in range(SPECIES)]
    right = [None] * SPECIES

    def fractions(base):
        counts = [
            sum_ref[pl.ds(base + (1 + c) * per_group, per_group), :] for c in range(SPECIES)
        ]
        size = jnp.maximum(counts[0] + counts[1] + counts[2] + counts[3], 1.0)
        return [count / size for count in counts], size

    def gather_sum(total, value):
        part = jnp.sum(jnp.sum(value, axis=0, keepdims=True), axis=1, keepdims=True)
        return part if total is None else total + part

    stride = (SPECIES + 2) * per_group
    for group in range(groups):
        base = sums_at + group * stride
        frac, _ = fractions(base)
        target = sum_ref[pl.ds(base + (1 + SPECIES) * per_group, per_group), :]
        for c in range(SPECIES):
            right[c] = gather_sum(right[c], frac[c] * target)
            for d in range(c, SPECIES):
                gram[c][d] = gather_sum(gram[c][d], frac[c] * frac[d])
    matrix = [
        [gram[min(c, d)][max(c, d)] + (ridge_weight if c == d else 0.0) for d in range(SPECIES)]
        for c in range(SPECIES)
    ]
    for pivot in range(SPECIES):
        for below in range(pivot + 1, SPECIES):
            ratio = matrix[below][pivot] / matrix[pivot][pivot]
            matrix[below] = [b - ratio * a for a, b in zip(matrix[pivot], matrix[below])]
            right[below] = right[below] - ratio * right[pivot]
    answer = [None] * SPECIES
    for row in range(SPECIES - 1, -1, -1):
        running = right[row]
        for later in range(row + 1, SPECIES):
            running = running - matrix[row][later] * answer[later]
        answer[row] = running / matrix[row][row]
    mine = sums_at + lax.axis_index("grp") * stride
    frac, size = fractions(mine)
    energy = sum_ref[pl.ds(mine, per_group), :] / size
    for c in range(SPECIES):
        energy = energy + frac[c] * answer[c]
    energy_ref[...] = energy
    offset_ref[...] = jnp.concatenate(
        [jnp.broadcast_to(value, (1, TILE)) for value in answer] + [jnp.zeros((4, TILE), f32)], axis=0
    )


def finish_call(which, mesh_steps, rows, sums_at, per_group, window, own, payload):
    size = payload.shape[0]
    return pl.pallas_call(
        partial(finish_kernel, rows, sums_at, per_group),
        out_shape=(
            jax.ShapeDtypeStruct((3, rows, TILE), f32),
            jax.ShapeDtypeStruct((size, TILE), f32),
            jax.ShapeDtypeStruct((per_group, TILE), f32),
            jax.ShapeDtypeStruct((8, TILE), f32),
        ),
        in_specs=[vmem_spec()] * 3,
        out_specs=(vmem_spec(),) * 4,
        scratch_shapes=[
            pltpu.VMEM((2, 3, rows, TILE), f32),
            pltpu.VMEM((mesh_steps, size, TILE), f32),
            pltpu.SemaphoreType.DMA((2,)),
            pltpu.SemaphoreType.DMA((2,)),
            pltpu.SemaphoreType.DMA((mesh_steps,)),
            pltpu.SemaphoreType.DMA((mesh_steps,)),
        ],
        compiler_params=comm_params(which),
        name="finish_%d" % which,
    )(window, own, payload)


def double_factorial(number):
    result = 1.0
    while number > 1:
        result = result * number
        number = number - 2
    return result


def norm_of(degree, azimuth):
    value = math.sqrt(
        (2 * degree + 1)
        / (4 * math.pi)
        * math.factorial(degree - azimuth)
        / math.factorial(degree + azimuth)
    )
    return value * (math.sqrt(2.0) if azimuth else 1.0)


def scaled_legendre(coord_z):
    table = {}
    for azimuth in range(LMAX + 1):
        table[azimuth, azimuth] = norm_of(azimuth, azimuth) * double_factorial(2 * azimuth - 1)
        if azimuth + 1 <= LMAX:
            ratio = norm_of(azimuth + 1, azimuth) / norm_of(azimuth, azimuth)
            table[azimuth + 1, azimuth] = coord_z * (
                (2 * azimuth + 1) * ratio * table[azimuth, azimuth]
            )
        for degree in range(azimuth + 2, LMAX + 1):
            gap = degree - azimuth
            first = (2 * degree - 1) / gap * norm_of(degree, azimuth) / norm_of(degree - 1, azimuth)
            second = (
                (degree + azimuth - 1) / gap * norm_of(degree, azimuth) / norm_of(degree - 2, azimuth)
            )
            table[degree, azimuth] = (first * coord_z) * table[degree - 1, azimuth] - (
                second * table[degree - 2, azimuth]
            )
    return table


def azimuth_powers(coord_x, coord_y):
    cosines = [None, coord_x]
    sines = [None, coord_y]
    for _ in range(2, LMAX + 1):
        cosines.append(cosines[-1] * coord_x - sines[-1] * coord_y)
        sines.append(sines[-1] * coord_x + cosines[-2] * coord_y)
    return cosines, sines


LANE_GATHER = lax.GatherDimensionNumbers(
    offset_dims=(),
    collapsed_slice_dims=(1,),
    start_index_map=(1,),
    operand_batching_dims=(0,),
    start_indices_batching_dims=(0,),
)


def lane_gather(line, lo):
    return lax.gather(
        line,
        lo[..., None],
        LANE_GATHER,
        slice_sizes=(1, 1),
        mode=lax.GatherScatterMode.PROMISE_IN_BOUNDS,
    )


def prepare_kernel(first_ref, cnt_ref, nbr_ref, idx_ref, wt_ref, info_ref, key_ref, pos_ref):
    tile = pl.program_id(0)
    limit = cnt_ref[...]
    iota = lax.broadcasted_iota(jnp.int32, (NBR, TILE), 0)
    live = iota < limit
    index = nbr_ref[...] - first_ref[0]
    key = jnp.where(live, index, -1 - iota)
    key_ref[...] = key
    keys = [key[8 * b : 8 * b + 8] for b in range(NBR // 8)]
    sub = lax.broadcasted_iota(jnp.int32, (8, TILE), 0)
    blocks = NBR // 8
    total = [jnp.zeros((8, TILE), jnp.int32) for _ in range(blocks)]
    early = [jnp.zeros((8, TILE), jnp.int32) for _ in range(blocks)]
    for other in range(NBR):
        line = jnp.broadcast_to(key_ref[other : other + 1, :], (8, TILE))
        for b in range(blocks):
            same = jnp.where(keys[b] == line, 1, 0)
            total[b] = total[b] + same
            if other < 8 * b:
                early[b] = early[b] + same
            elif other < 8 * b + 7:
                early[b] = early[b] + jnp.where(sub > other - 8 * b, same, 0)
    packed, first = [], []
    for b in range(blocks):
        alive = sub + 8 * b < limit
        first.append(jnp.where(alive & (early[b] == 0), 1, 0))
        packed.append(total[b] * 4096 + keys[b])
    for b in range(blocks):
        pos_ref[8 * b : 8 * b + 8, :] = first[b]
    place = [jnp.zeros((8, TILE), jnp.int32) for _ in range(blocks)]
    running = jnp.zeros((1, TILE), jnp.int32)
    lines = []
    for slot in range(NBR):
        flag = pos_ref[slot : slot + 1, :]
        lines.append(jnp.where(flag == 1, running, -1))
        running = running + flag
    for b in range(blocks):
        key_ref[8 * b : 8 * b + 8, :] = packed[b]
    out = place
    for slot in range(NBR):
        where_to = jnp.broadcast_to(lines[slot], (8, TILE))
        line = jnp.broadcast_to(key_ref[slot : slot + 1, :], (8, TILE))
        for b in range(slot // 8 + 1):
            out[b] = jnp.where(where_to == sub + 8 * b, line, out[b])
    zero = jnp.zeros((8, TILE), jnp.int32)
    for b in range(NPAD // 8):
        word = out[b] if b < blocks else zero
        idx_ref[8 * b : 8 * b + 8, :] = lax.bitwise_and(word, 4095)
        wt_ref[8 * b : 8 * b + 8, :] = density_scale * lax.shift_right_logical(word, 12).astype(f32)
    used = jnp.max(running)
    info_ref[0, tile] = lax.div(used + 3, 4) * 4
    row = lax.shift_right_arithmetic(index, 7)
    info_ref[1, tile] = jnp.min(jnp.where(live, row, 1 << 20))
    info_ref[2, tile] = jnp.max(jnp.where(live, row, -1))


def prepare_call(first, limits, neighbours):
    atoms = neighbours.shape[1]
    return pl.pallas_call(
        prepare_kernel,
        out_shape=(
            jax.ShapeDtypeStruct((NPAD, atoms), jnp.int32),
            jax.ShapeDtypeStruct((NPAD, atoms), f32),
            jax.ShapeDtypeStruct((3, atoms // TILE), jnp.int32),
        ),
        grid=(atoms // TILE,),
        in_specs=[smem_spec(), tile_spec(1), tile_spec(NBR)],
        out_specs=(tile_spec(NPAD), tile_spec(NPAD), smem_spec()),
        scratch_shapes=[pltpu.VMEM((NBR, TILE), jnp.int32), pltpu.VMEM((NBR, TILE), jnp.int32)],
        name="prepare",
    )(first, limits, neighbours)


def fetch(tab_ref, names, hi, lo, row_low, row_high):
    def body(row, values):
        hit = hi == row
        out = []
        for name, value in zip(names, values):
            line = jnp.broadcast_to(tab_ref[pl.ds(name * 24 + row, 1), :], (8, TILE))
            got = lane_gather(line, lo)
            out.append(jnp.where(hit, got, value))
        return tuple(out)

    zero = jnp.zeros((8, TILE), f32)
    return lax.fori_loop(row_low, row_high + 1, body, tuple(zero for _ in names))


def edge_block(layer, tab_ref, cen_ref, idx_ref, wt_ref, block_at, row_low, row_high):
    base = pl.multiple_of(block_at * 8, 8)
    index = idx_ref[pl.ds(base, 8), :]
    weight = wt_ref[pl.ds(base, 8), :]
    hi = lax.shift_right_logical(index, 7)
    lo = lax.bitwise_and(index, 127)
    names = (0, 1, 2, 3) if layer == 1 else (0, 1, 2, 3, 4, 5, 6)
    values = fetch(tab_ref, names, hi, lo, row_low, row_high)
    live = weight > 0.0
    deltas = []
    for axis in range(3):
        centre = jnp.broadcast_to(cen_ref[pl.ds(axis, 1), :], (8, TILE))
        deltas.append(jnp.where(live, values[axis] - centre, 1.0))
    dist = jnp.sqrt(deltas[0] * deltas[0] + deltas[1] * deltas[1] + deltas[2] * deltas[2])
    inv = 1.0 / dist
    unit = [delta * inv for delta in deltas]
    if layer == 1:
        chan = [jnp.where(values[3] == float(c), 1.0, 0.0) for c in range(SPECIES)]
    else:
        chan = list(values[3:])
    return hi, lo, weight, dist, inv, unit, chan


def radial_terms(dist, rad_ref, with_slope):
    scaled = dist * (2.0 / cutoff_radius) - 1.0
    inside = dist < cutoff_radius
    angle = dist * (math.pi / cutoff_radius)
    cutoff = jnp.where(inside, 0.5 * (jnp.cos(angle) + 1.0), 0.0)
    cheb = [None, scaled]
    twice = 2.0 * scaled
    cheb.append(twice * scaled - 1.0)
    for _ in range(3, NRAD):
        cheb.append(twice * cheb[-1] - cheb[-2])
    basis = [cutoff] + [cutoff * cheb[p] for p in range(1, NRAD)]
    radial = []
    for n in range(NMAX):
        total = basis[0] * rad_ref[n, 0]
        for p in range(1, NRAD):
            total = total + basis[p] * rad_ref[n, p]
        radial.append(total)
    if not with_slope:
        return basis, radial, None
    slope_cut = jnp.where(inside, (-0.5 * math.pi / cutoff_radius) * jnp.sin(angle), 0.0)
    grad_scaled = cutoff * (2.0 / cutoff_radius)
    second = [None, None, twice]
    second[1] = jnp.ones_like(scaled)
    for _ in range(3, NRAD):
        second.append(twice * second[-1] - second[-2])
    slopes = [slope_cut, slope_cut * scaled + grad_scaled]
    for p in range(2, NRAD):
        slopes.append(slope_cut * cheb[p] + grad_scaled * (float(p) * second[p]))
    return basis, radial, slopes


def harmonic_list(unit):
    table = scaled_legendre(unit[2])
    cosines, sines = azimuth_powers(unit[0], unit[1])
    columns = []
    for degree in range(LMAX + 1):
        for signed in range(-degree, degree + 1):
            azimuth = abs(signed)
            poly = table[degree, azimuth]
            if signed == 0:
                columns.append(poly)
            elif signed > 0:
                columns.append(poly * cosines[azimuth])
            else:
                columns.append(poly * sines[azimuth])
    columns[0] = jnp.full_like(unit[2], columns[0])
    return columns


def density_kernel(layer, info_ref, rad_ref, tab_ref, cen_ref, idx_ref, wt_ref, out_ref,
                   x_ref, y_ref, d_ref):
    tile = pl.program_id(0)
    count = info_ref[0, tile]
    row_low, row_high = info_ref[1, tile], info_ref[2, tile]
    blocks = lax.div(count + 7, 8)

    def edges(block_at, carry):
        base = pl.multiple_of(block_at * 8, 8)
        hi, lo, weight, dist, inv, unit, chan = edge_block(
            layer, tab_ref, cen_ref, idx_ref, wt_ref, block_at, row_low, row_high
        )
        _, radial, _ = radial_terms(dist, rad_ref, False)
        for c in range(SPECIES):
            scale = chan[c] * weight
            for n in range(NMAX):
                x_ref[pl.ds(base * CH + (c * NMAX + n), 8, stride=CH), :] = scale * radial[n]
        for at, column in enumerate(harmonic_list(unit)):
            y_ref[pl.ds(at * NPAD + base, 8), :] = column
        return carry

    lax.fori_loop(0, blocks, edges, 0)
    groups = lax.div(count, SLOTS)

    def lm_block(block_at, carry):
        first = block_at * LBLK

        def slots(group, acc):
            acc = list(acc)
            for part in range(SLOTS):
                slot = group * SLOTS + part
                rows = [
                    x_ref[pl.ds(pl.multiple_of(slot * CH + 8 * j, 8), 8), :] for j in range(CH // 8)
                ]
                for at in range(LBLK):
                    line = jnp.broadcast_to(
                        y_ref[pl.ds((first + at) * NPAD + slot, 1), :], (8, TILE)
                    )
                    for j in range(CH // 8):
                        acc[at * (CH // 8) + j] = acc[at * (CH // 8) + j] + rows[j] * line
            return tuple(acc)

        zero = jnp.zeros((8, TILE), f32)
        acc = lax.fori_loop(0, groups, slots, tuple(zero for _ in range(LBLK * (CH // 8))))
        for at in range(LBLK):
            for j in range(CH // 8):
                d_ref[pl.ds(8 * j * LM + first + at, 8, stride=LM), :] = acc[at * (CH // 8) + j]
        return carry

    lax.fori_loop(0, LM // LBLK, lm_block, 0)
    out_ref[...] = d_ref[...].astype(bf16)


def smem_spec():
    return pl.BlockSpec(memory_space=pltpu.SMEM)


def tile_spec(rows):
    return pl.BlockSpec((rows, TILE), lambda i: (0, i))


def whole_spec(shape):
    return pl.BlockSpec(shape, lambda i: tuple(0 for _ in shape))


def density_call(layer, info, radial, table, centres, index, weight):
    atoms = centres.shape[1]
    return pl.pallas_call(
        partial(density_kernel, layer),
        out_shape=jax.ShapeDtypeStruct((DENS, atoms), bf16),
        grid=(atoms // TILE,),
        in_specs=[
            smem_spec(),
            smem_spec(),
            whole_spec(table.shape),
            tile_spec(8),
            tile_spec(NPAD),
            tile_spec(NPAD),
        ],
        out_specs=tile_spec(DENS),
        scratch_shapes=[
            pltpu.VMEM((NPAD * CH, TILE), f32),
            pltpu.VMEM((LM * NPAD, TILE), f32),
            pltpu.VMEM((DENS, TILE), f32),
        ],
        compiler_params=pltpu.CompilerParams(vmem_limit_bytes=48 << 20),
        name="density_%d" % layer,
    )(info, radial, table, centres, index, weight)


def backward_kernel(layer, info_ref, rad_ref, tab_ref, cen_ref, idx_ref, wt_ref, dd_ref, win_in_ref,
                    own_in_ref, win_ref, own_ref, rgr_ref, x_ref, y_ref, gx_ref, gy_ref, val_ref):
    tile = pl.program_id(0)
    count = info_ref[0, tile]
    row_low, row_high = info_ref[1, tile], info_ref[2, tile]
    blocks = lax.div(count + 7, 8)
    chunks = lax.div(count + 31, 32)

    @pl.when(tile == 0)
    def _():
        if layer == 1:
            win_ref[...] = win_in_ref[...]
        else:
            win_ref[...] = jnp.zeros_like(win_ref)
        rgr_ref[...] = jnp.zeros_like(rgr_ref)

    def edges(block_at, carry):
        base = pl.multiple_of(block_at * 8, 8)
        hi, lo, weight, dist, inv, unit, chan = edge_block(
            layer, tab_ref, cen_ref, idx_ref, wt_ref, block_at, row_low, row_high
        )
        _, radial, _ = radial_terms(dist, rad_ref, False)
        if layer == 1:
            for n in range(NMAX):
                x_ref[pl.ds(n * NPAD + base, 8), :] = weight * radial[n]
            x_ref[pl.ds(NMAX * NPAD + base, 8), :] = chan[1] + chan[3]
            x_ref[pl.ds((NMAX + 1) * NPAD + base, 8), :] = chan[2] + chan[3]
        else:
            for c in range(SPECIES):
                scale = chan[c] * weight
                for n in range(NMAX):
                    x_ref[pl.ds((c * NMAX + n) * NPAD + base, 8), :] = scale * radial[n]
        for at, column in enumerate(harmonic_list(unit)):
            y_ref[pl.ds(at * NPAD + base, 8), :] = column
        return carry

    lax.fori_loop(0, chunks * 4, edges, 0)

    zero = jnp.zeros((8, TILE), f32)

    def chunk_body(chunk, carry):
        start = pl.multiple_of(chunk * 32, 32)

        def m_block(block_at, inner):
            def over_lm(step, acc):
                acc = list(acc)
                for part in range(LBLK):
                    lm = step * LBLK + part
                    cols = [
                        y_ref[pl.ds(pl.multiple_of(lm * NPAD + start + 8 * kb, 8), 8), :]
                        for kb in range(4)
                    ]
                    for i in range(8):
                        line = jnp.broadcast_to(
                            dd_ref[pl.ds((block_at * 8 + i) * LM + lm, 1), :], (8, TILE)
                        )
                        for kb in range(4):
                            acc[i * 4 + kb] = acc[i * 4 + kb] + line * cols[kb]
                return tuple(acc)

            acc = lax.fori_loop(0, LM // LBLK, over_lm, tuple(zero for _ in range(32)))
            for i in range(8):
                for kb in range(4):
                    at = pl.multiple_of((block_at * 8 + i) * NPAD + start + 8 * kb, 8)
                    gx_ref[pl.ds(at, 8), :] = acc[i * 4 + kb]
            return inner

        lax.fori_loop(0, CH // 8, m_block, 0)

        def lm_block(block_at, inner):
            def over_m(step, acc):
                acc = list(acc)
                for part in range(8):
                    m = step * 8 + part
                    cols = [
                        x_ref[pl.ds(pl.multiple_of(m * NPAD + start + 8 * kb, 8), 8), :]
                        for kb in range(4)
                    ]
                    for i in range(LBLK):
                        line = jnp.broadcast_to(
                            dd_ref[pl.ds(m * LM + block_at * LBLK + i, 1), :], (8, TILE)
                        )
                        for kb in range(4):
                            acc[i * 4 + kb] = acc[i * 4 + kb] + line * cols[kb]
                return tuple(acc)

            acc = lax.fori_loop(0, CH // 8, over_m, tuple(zero for _ in range(LBLK * 4)))
            for i in range(LBLK):
                for kb in range(4):
                    at = pl.multiple_of((block_at * LBLK + i) * NPAD + start + 8 * kb, 8)
                    gy_ref[pl.ds(at, 8), :] = acc[i * 4 + kb]
            return inner

        lax.fori_loop(0, LM // LBLK, lm_block, 0)
        return carry

    def species_chunk(chunk, carry):
        start = pl.multiple_of(chunk * 32, 32)
        for n in range(NMAX):
            for kb in range(4):
                gx_ref[pl.ds(pl.multiple_of(n * NPAD + start + 8 * kb, 8), 8), :] = zero

        def lm_block(block_at, inner):
            def over_n(n, acc):
                acc = list(acc)
                bits = []
                for which in range(2):
                    at = (NMAX + which) * NPAD + start
                    bits.append([x_ref[pl.ds(pl.multiple_of(at + 8 * kb, 8), 8), :] > 0.5 for kb in range(4)])
                scaled, sums = [], []
                for kb in range(4):
                    at = pl.multiple_of(n * NPAD + start + 8 * kb, 8)
                    scaled.append(x_ref[pl.ds(at, 8), :])
                    sums.append(gx_ref[pl.ds(at, 8), :])
                for i in range(LBLK):
                    lines = [
                        jnp.broadcast_to(
                            dd_ref[pl.ds((c * NMAX + n) * LM + block_at * LBLK + i, 1), :], (8, TILE)
                        )
                        for c in range(SPECIES)
                    ]
                    for kb in range(4):
                        even = jnp.where(bits[0][kb], lines[1], lines[0])
                        odd = jnp.where(bits[0][kb], lines[3], lines[2])
                        grad = jnp.where(bits[1][kb], odd, even)
                        at = (block_at * LBLK + i) * NPAD + start + 8 * kb
                        col = y_ref[pl.ds(pl.multiple_of(at, 8), 8), :]
                        acc[i * 4 + kb] = acc[i * 4 + kb] + grad * scaled[kb]
                        sums[kb] = sums[kb] + grad * col
                for kb in range(4):
                    at = pl.multiple_of(n * NPAD + start + 8 * kb, 8)
                    gx_ref[pl.ds(at, 8), :] = sums[kb]
                return tuple(acc)

            acc = lax.fori_loop(0, NMAX, over_n, tuple(zero for _ in range(LBLK * 4)))
            for i in range(LBLK):
                for kb in range(4):
                    at = pl.multiple_of((block_at * LBLK + i) * NPAD + start + 8 * kb, 8)
                    gy_ref[pl.ds(at, 8), :] = acc[i * 4 + kb]
            return inner

        lax.fori_loop(0, LM // LBLK, lm_block, 0)
        return carry

    lax.fori_loop(0, chunks, species_chunk if layer == 1 else chunk_body, 0)

    def finish(block_at, own):
        base = pl.multiple_of(block_at * 8, 8)
        hi, lo, weight, dist, inv, unit, chan = edge_block(
            layer, tab_ref, cen_ref, idx_ref, wt_ref, block_at, row_low, row_high
        )
        basis, radial, slopes = radial_terms(dist, rad_ref, True)
        feat_grads = []
        radial_grads = [None] * NMAX
        if layer == 1:
            radial_grads = [gx_ref[pl.ds(n * NPAD + base, 8), :] for n in range(NMAX)]
        for c in range(SPECIES if layer == 2 else 0):
            total = None
            for n in range(NMAX):
                grad = gx_ref[pl.ds((c * NMAX + n) * NPAD + base, 8), :]
                term = grad * radial[n]
                total = term if total is None else total + term
                piece = grad * chan[c]
                radial_grads[n] = piece if c == 0 else radial_grads[n] + piece
            feat_grads.append(total * weight)
        grad_r = None
        radial_grads = [grad * weight for grad in radial_grads]
        for p in range(NRAD):
            total = None
            for n in range(NMAX):
                at = (n * NRAD + p) * 8
                rgr_ref[pl.ds(at, 8), :] = rgr_ref[pl.ds(at, 8), :] + radial_grads[n] * basis[p]
                term = radial_grads[n] * rad_ref[n, p]
                total = term if total is None else total + term
            term = total * slopes[p]
            grad_r = term if grad_r is None else grad_r + term
        table = scaled_legendre(unit[2])
        cosines, sines = azimuth_powers(unit[0], unit[1])
        grad_x = grad_y = grad_z = None

        def plus(total, term):
            return term if total is None else total + term

        for azimuth in range(LMAX + 1):
            grad_cos = grad_sin = None
            for degree in range(azimuth, LMAX + 1):
                at = degree * degree + degree
                up = gy_ref[pl.ds((at + azimuth) * NPAD + base, 8), :]
                poly = table[degree, azimuth]
                if azimuth:
                    down = gy_ref[pl.ds((at - azimuth) * NPAD + base, 8), :]
                    grad_cos = plus(grad_cos, up * poly)
                    grad_sin = plus(grad_sin, down * poly)
                if degree > azimuth:
                    ratio = norm_of(degree, azimuth) / norm_of(degree, azimuth + 1)
                    slope = ratio * table[degree, azimuth + 1]
                    if azimuth:
                        grad_z = plus(grad_z, slope * (up * cosines[azimuth] + down * sines[azimuth]))
                    else:
                        grad_z = plus(grad_z, slope * up)
            if azimuth == 1:
                grad_x, grad_y = grad_cos, grad_sin
            elif azimuth > 1:
                below_cos, below_sin = cosines[azimuth - 1], sines[azimuth - 1]
                grad_x = grad_x + float(azimuth) * (grad_cos * below_cos + grad_sin * below_sin)
                grad_y = grad_y + float(azimuth) * (grad_sin * below_cos - grad_cos * below_sin)
        dot_u = grad_x * unit[0] + grad_y * unit[1] + grad_z * unit[2]
        live = weight > 0.0
        out = []
        for axis, grad in enumerate((grad_x, grad_y, grad_z)):
            value = (grad - dot_u * unit[axis]) * inv + grad_r * unit[axis]
            out.append(jnp.where(live, value, 0.0))
        values = out + feat_grads
        for at, value in enumerate(values):
            val_ref[pl.ds(at * NPAD + base, 8), :] = value
        return tuple(total + value for total, value in zip(own, out))

    own = lax.fori_loop(0, blocks, finish, (zero, zero, zero))
    own = jnp.concatenate(
        [jnp.sum(total, axis=0, keepdims=True) for total in own] + [jnp.zeros((5, TILE), f32)], axis=0
    )
    own_ref[...] = own + own_in_ref[...] if layer == 1 else own

    used = 3 if layer == 1 else NVAL
    sub = lax.broadcasted_iota(jnp.int32, (TILE, TILE), 0)
    windows = lax.div(row_high - row_low + WROWS, WROWS)

    def window(window_at, carry):
        row_base = row_low + window_at * WROWS

        def slot_block(block_at, acc):
            base = pl.multiple_of(block_at * 8, 8)
            index = idx_ref[pl.ds(base, 8), :]
            hi = lax.shift_right_logical(index, 7)
            lo = lax.bitwise_and(index, 127)
            tops, lows = [], []
            for value_at in range(used):
                value = val_ref[pl.ds(value_at * NPAD + base, 8), :]
                for row in range(WROWS):
                    tops.append(jnp.where(hi == row_base + row, value, 0.0))
            stacked = jnp.stack(tops, axis=0)
            ones, left = [], []
            for part in range(8):
                line = jnp.broadcast_to(lo[part : part + 1, :], (TILE, TILE))
                ones.append(jnp.where(line == sub, 1.0, 0.0).astype(bf16))
                left.append(stacked[:, part, :])
            left = jnp.concatenate(left, axis=1)
            ones = jnp.concatenate(ones, axis=1)
            high = left.astype(bf16)
            rest = (left - high.astype(f32)).astype(bf16)
            dims = (((1,), (1,)), ((), ()))
            acc = acc + lax.dot_general(high, ones, dims, preferred_element_type=f32)
            return acc + lax.dot_general(rest, ones, dims, preferred_element_type=f32)

        acc = lax.fori_loop(0, blocks, slot_block, jnp.zeros((used * WROWS, TILE), f32))
        for value_at in range(used):
            at = value_at * 32 + row_base
            win_ref[pl.ds(at, WROWS), :] = (
                win_ref[pl.ds(at, WROWS), :] + acc[value_at * WROWS : (value_at + 1) * WROWS]
            )
        return carry

    lax.fori_loop(0, windows, window, 0)


def backward_call(layer, info, radial, table, centres, index, weight, grad_dens, window_in, own_in):
    atoms = centres.shape[1]
    values = 3 if layer == 1 else NVAL
    return pl.pallas_call(
        partial(backward_kernel, layer),
        out_shape=(
            jax.ShapeDtypeStruct((values * 32, TILE), f32),
            jax.ShapeDtypeStruct((8, atoms), f32),
            jax.ShapeDtypeStruct((NMAX * NRAD * 8, TILE), f32),
        ),
        grid=(atoms // TILE,),
        in_specs=[
            smem_spec(),
            smem_spec(),
            whole_spec(table.shape),
            tile_spec(8),
            tile_spec(NPAD),
            tile_spec(NPAD),
            tile_spec(DENS),
            whole_spec(window_in.shape),
            tile_spec(8),
        ],
        out_specs=(
            whole_spec((values * 32, TILE)),
            tile_spec(8),
            whole_spec((NMAX * NRAD * 8, TILE)),
        ),
        scratch_shapes=[
            pltpu.VMEM((CH * NPAD, TILE), f32),
            pltpu.VMEM((LM * NPAD, TILE), f32),
            pltpu.VMEM((CH * NPAD, TILE), f32),
            pltpu.VMEM((LM * NPAD, TILE), f32),
            pltpu.VMEM((NVAL * NPAD, TILE), f32),
        ],
        compiler_params=pltpu.CompilerParams(vmem_limit_bytes=48 << 20),
        name="backward_%d" % layer,
    )(info, radial, table, centres, index, weight, grad_dens, window_in, own_in)


def feature_map(invariants, mixing):
    inverse_rms = lax.rsqrt(jnp.mean(invariants * invariants, axis=0) + norm_eps)
    return jnp.einsum("qk,qa->ka", mixing, invariants, precision=highest) * inverse_rms


def contract(dens_in, coupling):
    factors = jnp.einsum("vdq,da->vqa", coupling, dens_in, preferred_element_type=f32)
    product = reduce(
        lambda earlier, later: earlier * later,
        [factors[index_v] for index_v in range(factors.shape[0])],
    )
    return (factors, product)


def contract_back(factors, upstream, coupling):
    partials = []
    for factor_at in range(factors.shape[0]):
        others = upstream
        for partner in range(factors.shape[0]):
            if partner != factor_at:
                others = others * factors[partner]
        partials.append(others)
    rounded = jnp.stack(partials).astype(bf16)
    return jnp.einsum("vdq,vqa->da", coupling, rounded, preferred_element_type=f32)


def per_device(
    positions,
    species,
    neighbours,
    slot_counts,
    structure,
    target_energy,
    radial_one,
    coupling_one,
    coefficient_one,
    mixing,
    radial_two,
    coupling_two,
    coefficient_two,
):
    atoms = positions.shape[2]
    tiles = atoms // TILE
    centres = positions[:, 0, :]
    own_species = species[0]
    onehot = (own_species[None, :] == jnp.arange(SPECIES, dtype=jnp.int32)[:, None]).astype(f32)
    site = jnp.concatenate([centres, own_species.astype(f32)[None, :]], axis=0)
    table_one = spread_call(0, 4, site.reshape(4 * tiles, TILE))
    first = ((lax.axis_index("dom") - 1) * atoms).astype(jnp.int32).reshape(1)
    index, weight, info = prepare_call(first, slot_counts, neighbours[:, 0, :])
    centres8 = jnp.pad(centres, ((0, 5), (0, 0)))

    dens_one = density_call(1, info, radial_one, table_one, centres8, index, weight)
    factors_one, invariants_one = contract(dens_one, coupling_one)
    chosen_one = jnp.dot(coefficient_one.T, onehot, precision=highest)
    energy_one = jnp.sum(invariants_one * chosen_one, axis=0)
    features, features_back = jax.vjp(feature_map, invariants_one, mixing)
    feat_table = spread_call(1, SPECIES, features.reshape(SPECIES * tiles, TILE))
    table_two = jnp.concatenate([table_one[: 3 * 3 * tiles], feat_table], axis=0)
    dens_two = density_call(2, info, radial_two, table_two, centres8, index, weight)
    factors_two, invariants_two = contract(dens_two, coupling_two)
    chosen_two = jnp.dot(coefficient_two.T, onehot, precision=highest)
    site_energy = energy_one + jnp.sum(invariants_two * chosen_two, axis=0)
    structures = target_energy.shape[1]
    members = (structure[0][:, None] == jnp.arange(structures, dtype=jnp.int32)[None, :]).astype(f32)
    per_structure = jnp.dot(
        jnp.concatenate([site_energy[None, :], onehot], axis=0), members, precision=highest
    )
    target = jnp.where(lax.axis_index("dom") == 0, target_energy, 0.0)
    per_structure = jnp.concatenate([per_structure, target], axis=0)

    grad_dens_two = contract_back(factors_two, chosen_two, coupling_two)
    blank_window = jnp.zeros((8, TILE), f32)
    blank_own = jnp.zeros((8, atoms), f32)
    window_two, own_two, rgr_two = backward_call(
        2, info, radial_two, table_two, centres8, index, weight, grad_dens_two, blank_window, blank_own
    )
    window_two = window_two.reshape(NVAL, 32, TILE)
    grad_features = collect_call(2, tiles, window_two[3:]).reshape(SPECIES, atoms)
    coefficient_second = jnp.dot(onehot, invariants_two.T, precision=highest)
    grad_invariants, mixing_gradient = features_back(grad_features)
    grad_dens_one = contract_back(factors_one, chosen_one + grad_invariants, coupling_one)
    window_one, own_one, rgr_one = backward_call(
        1,
        info,
        radial_one,
        table_one,
        centres8,
        index,
        weight,
        grad_dens_one,
        window_two[:3].reshape(3 * 32, TILE),
        own_two,
    )
    coefficient_first = jnp.dot(onehot, invariants_one.T, precision=highest)

    def radial_sum(partial_grad):
        return jnp.sum(partial_grad.reshape(NMAX * NRAD, 8 * TILE), axis=1)

    groups = lax.axis_size("grp")
    mine = lax.axis_index("grp") == jnp.arange(groups, dtype=jnp.int32)
    slots = jnp.where(mine[:, None, None], per_structure[None], 0.0)
    quantum = coefficient_first.shape[1]
    wide = SPECIES * quantum
    radials = jnp.zeros((8 * TILE,), f32)
    radials = radials.at[: NMAX * NRAD].set(radial_sum(rgr_one))
    radials = radials.at[TILE : TILE + NMAX * NRAD].set(radial_sum(rgr_two))
    payload = jnp.concatenate(
        [
            radials,
            coefficient_first.reshape(-1),
            coefficient_second.reshape(-1),
            mixing_gradient.T.reshape(-1),
            slots.reshape(-1),
        ]
    )
    sums_at = 8 + 3 * wide // TILE
    steps = log2_of(lax.axis_size("dom")) + log2_of(groups)
    forces, sums, energies, offsets = finish_call(
        3,
        steps,
        tiles,
        sums_at,
        structures // TILE,
        window_one.reshape(3, 32, TILE),
        own_one[:3].reshape(3, tiles, TILE),
        payload.reshape(-1, TILE),
    )
    parts = sums[8:sums_at].reshape(3, SPECIES, quantum)
    return (
        energies.reshape(1, structures),
        offsets[:SPECIES, 0],
        forces.reshape(3, 1, atoms),
        sums[0, : NMAX * NRAD].reshape(NMAX, NRAD),
        parts[0],
        parts[2].T,
        sums[1, : NMAX * NRAD].reshape(NMAX, NRAD),
        parts[1],
    )


def solution(mesh):
    in_specs = (
        P(None, "grp", "dom"),
        P("grp", "dom"),
        P(None, "grp", "dom"),
        P("grp", "dom"),
        P("grp", "dom"),
        P("grp", None),
        P(),
        P(),
        P(),
        P(),
        P(),
        P(),
        P(),
    )
    out_specs = (P("grp", None), P(), P(None, "grp", "dom"), P(), P(), P(), P(), P())
    return jax.shard_map(
        per_device, mesh=mesh, in_specs=in_specs, out_specs=out_specs, check_vma=False
    )
```

profile of v0, /device:TPU:0, one launch (start us, length us, event | category | flops | bytes accessed | tf_op | source)
XLA Modules:
  0.0 335.3 jit_solution(9183209250269662764)
XLA Ops:
  0.6 0.0 copy-start
  0.7 1.6 copy.48
  2.3 5.8 %prepare.1 = (s32[64,1024]{1,0:T(8,128)}, f32[64,1024]{1,0:T(8,128)}, s32[3,8]{1,0:T(4,128)}) custom-call(s32[1]{0:T(128)} %bitcast.first_ref, s32[1,1024]{1,0:T(1,128)} %cnt_ref.1, s32[48,1024]{1,0:T(8,128)} %bitcast.264), custom_call_target="tpu_custom_call" | custom-call | tf_op jit(solution)/shard_map/prepare/pallas_call | solution.py:398
  8.1 0.7 convert_element_type.12
  8.8 0.7 copy.49
  9.6 0.6 reshape.154.x_ref
  10.2 5.1 %spread_0.1.tab_ref = f32[96,128]{1,0:T(8,128)} custom-call(f32[32,128]{1,0:T(8,128)} %reshape.154.x_ref), custom_call_target="tpu_custom_call" | custom-call | tf_op jit(solution)/shard_map/spread_0/pallas_call | solution.py:125
  15.3 0.9 copy-done.2
  16.3 0.9 copy-done.4
  17.2 0.8 copy-done.6
  18.0 0.7 copy-done.10
  18.7 0.7 copy-done.12
  19.4 31.7 %density_1.1 = bf16[1960,1024]{1,0:T(8,128)(2,1)S(1)} custom-call(s32[3,8]{1,0:T(4,128)S(1)} %copy-done.12, f32[10,12]{1,0:T(8,128)S(1)} %copy-done.10, f32[96,128]{1,0:T(8,128)S(1)} %copy-done.6, f32[8,1024]{1,0:T(8,128)S(1)} %pad.9.cen_ref, s32[64,1024]{1,0:T(8,128)S(1)} %copy-done.2, f32[64,1024]{1,0:T(8,128)S(1)} %copy-done.4), custom_call_target="tpu_custom_call" | custom-call | tf_op jit(solution)/shard_map/density_1/pallas_call | solution.py:566
  51.1 0.0 copy-start.17
  51.1 0.0 copy-start.20
  51.1 11.8 %fusion.18 = f32[4,512,1024]{2,1,0:T(8,128)S(1)} fusion(bf16[4,1960,512]{2,1,0:T(8,128)(2,1)} %param.24, bf16[1960,1024]{1,0:T(8,128)(2,1)S(1)} %density_1.1), kind=kOutput, calls=%fused_computation.20 | convolution fusion | flops 8220835840 | bytes 20430848 | tf_op jit(solution)/shard_map/vdq,da->vqa/dot_general | solution.py:899
  62.9 0.0 copy-start.19
  62.9 3.4 %fusion.35 = (f32[1024]{0:T(1024)S(1)}, f32[1024]{0:T(1024)S(1)}, f32[512,1024]{1,0:T(8,128)S(1)}, f32[1024,512]{0,1:T(8,128)}) fusion(f32[4,512,1024]{2,1,0:T(8,128)S(1)} %fusion.18, f32[4,512]{1,0:T(4,128)S(1)} %copy-done.20, s32[1024]{0:T(1024)S(1)} %bitcast.270), kind=kOutput, calls=%fused_computation.54 | convolution fusion | flops 28837888 | bytes 12603392 | tf_op jit(solution)/shard_map/dot_general | solution.py:947
  66.4 0.0 copy-start.9
  66.4 1.3 copy-done.14
  67.7 1.2 broadcast_multiply_fusion
  68.9 0.6 reshape.155.x_ref
  69.5 2.7 spread_1.1
  72.2 0.8 pad_maximum_fusion.tab_ref
  73.1 0.0 slice-start.1
  73.1 32.1 %density_2.1 = bf16[1960,1024]{1,0:T(8,128)(2,1)S(1)} custom-call(s32[3,8]{1,0:T(4,128)S(1)} %copy-done.13, f32[10,12]{1,0:T(8,128)S(1)} %copy-done.9, f32[168,128]{1,0:T(8,128)S(1)} %pad_maximum_fusion.tab_ref, f32[8,1024]{1,0:T(8,128)S(1)} %pad.9.cen_ref, s32[64,1024]{1,0:T(8,128)S(1)} %copy-done.3, f32[64,1024]{1,0:T(8,128)S(1)} %copy-done.5), custom_call_target="tpu_custom_call" | custom-call | tf_op jit(solution)/shard_map/density_2/pallas_call | solution.py:566
  105.2 0.0 slice-start.2
  105.2 12.1 %fusion.21 = f32[4,512,1024]{2,1,0:T(8,128)S(1)} fusion(bf16[4,1960,512]{2,1,0:T(8,128)(2,1)} %param.28, bf16[1960,1024]{1,0:T(8,128)(2,1)S(1)} %density_2.1), kind=kOutput, calls=%fused_computation.21 | convolution fusion | flops 8220835840 | bytes 20430848 | tf_op jit(solution)/shard_map/vdq,da->vqa/dot_general | solution.py:899
  117.2 3.4 %fusion.30 = (f32[1024]{0:T(1024)S(1)}, f32[512,1024]{1,0:T(8,128)}, bf16[1,512,1024]{2,1,0:T(8,128)(2,1)S(1)}, bf16[1,512,1024]{2,1,0:T(8,128)(2,1)S(1)}, bf16[...) fusion(f32[4,512,1024]{2,1,0:T(8,128)S(1)} %fusion.21, f32[4,512]{1,0:T(4,128)S(1)} %copy-done, ...), kind=kOutput, calls=%fused_computation.36 | convolution fusion | flops 34606080 | bytes 14696448 | tf_op jit(solution)/shard_map/dot_general | solution.py:954
  120.7 11.0 %convolution_bitcast_fusion.1.dd_ref = f32[1960,1024]{1,0:T(8,128)} fusion(bf16[4,1960,512]{2,1,0:T(8,128)(2,1)S(1)} %bitcast.285, bf16[1,512,1024]{2,1,0:T(8,128)(2,1)S(1)} %get-tuple-element.85, bf16[1,512,1024]{2,1,0:T(8,128)(2,1)S(1)} %get-tuple-element.84, bf16[1,512,1024]{2,1,0:T(8,128)(2,1)S(1)} %get-tuple-element.86, ...), kind=kOutput, calls=%fused_computation.1 | convolution fusion | flops 8227127296 | bytes 20250624 | tf_op jit(solution)/shard_map/vdq,vqa->da/dot_general | solution.py:916
  131.7 75.1 %backward_2.1 = (f32[224,128]{1,0:T(8,128)S(1)}, f32[8,1024]{1,0:T(8,128)S(1)}, f32[960,128]{1,0:T(8,128)S(1)}) custom-call(s32[3,8]{1,0:T(4,128)S(1)} %copy-done.13, f32[10,12]{1,0:T(8,128)S(1)} %copy-done.9, f32[168,128]{1,0:T(8,128)S(1)} %pad_maximum_fusion.tab_ref, f32[8,1024]{1,0:T(8,128)S(1)} %pad.9.cen_ref, s32[64,1024]{1,0:T(8,128)S(1)} %copy-done.3, ...), custom_call_target="tpu_custom_call" | custom-call | tf_op jit(solution)/shard_map/backward_2/pallas_call | solution.py:857
  206.8 0.6 slice.121
  207.4 3.9 %collect_2.1 = f32[4,8,128]{2,1,0:T(8,128)} custom-call(f32[4,32,128]{2,1,0:T(8,128)} %bitcast.267), custom_call_target="tpu_custom_call" | custom-call | tf_op jit(solution)/shard_map/collect_2/pallas_call | solution.py:152
  211.4 0.7 fusion.63
  212.1 7.2 %fusion.53 = (bf16[1,512,1024]{2,1,0:T(8,128)(2,1)S(1)}, f32[512,1024]{1,0:T(8,128)S(1)}, bf16[1,512,1024]{2,1,0:T(8,128)(2,1)S(1)}) fusion(f32[4,512,1024]{2,1,0:T(8,128)} %copy-done.15, f32[512,1024]{1,0:T(8,128)} %copy-done.14, f32[1024]{0:T(1024)S(1)} %get-tuple-element.94, f32[1024,512]{0,1:T(8,128)} %get-tuple-element.95, ...), kind=kOutput, calls=%fused_computation.79 | convolution fusion | flops 31461376 | bytes 16809984 | tf_op jit(solution)/shard_map/transpose(jvp(qk,qa->ka))/dot_general | solution.py:895
  219.3 3.6 %fusion.52 = (bf16[1,512,1024]{2,1,0:T(8,128)(2,1)S(1)}, bf16[1,512,1024]{2,1,0:T(8,128)(2,1)S(1)}) fusion(f32[4,512,1024]{2,1,0:T(8,128)} %copy-done.15, f32[512,1024]{1,0:T(8,128)S(1)} %get-tuple-element.81), kind=kLoop, calls=%fused_computation.78 | loop fusion | flops 2621440 | bytes 10485760 | tf_op jit(solution)/shard_map/stack | solution.py:915
  223.0 12.9 %convolution_bitcast_fusion.dd_ref = f32[1960,1024]{1,0:T(8,128)} fusion(bf16[4,1960,512]{2,1,0:T(8,128)(2,1)} %param.24, bf16[1,512,1024]{2,1,0:T(8,128)(2,1)S(1)} %get-tuple-element.89, bf16[1,512,1024]{2,1,0:T(8,128)(2,1)S(1)} %get-tuple-element.88, bf16[1,512,1024]{2,1,0:T(8,128)(2,1)S(1)} %get-tuple-element.80, ...), kind=kOutput, calls=%fused_computation | convolution fusion | flops 8227127296 | bytes 20250624 | tf_op jit(solution)/shard_map/vdq,vqa->da/dot_general | solution.py:916
  235.9 53.4 %backward_1.1 = (f32[96,128]{1,0:T(8,128)S(1)}, f32[8,1024]{1,0:T(8,128)S(1)}, f32[960,128]{1,0:T(8,128)S(1)}) custom-call(s32[3,8]{1,0:T(4,128)S(1)} %copy-done.13, f32[10,12]{1,0:T(8,128)S(1)} %copy-done.11, f32[96,128]{1,0:T(8,128)S(1)} %copy-done.7, f32[8,1024]{1,0:T(8,128)S(1)} %pad.9.cen_ref, s32[64,1024]{1,0:T(8,128)S(1)} %copy-done.3, ...), custom_call_target="tpu_custom_call" | custom-call | tf_op jit(solution)/shard_map/backward_1/pallas_call | solution.py:857
  289.3 0.0 copy-start.8
  289.3 0.6 copy-done.8
  289.9 0.6 copy.50
  290.5 0.2 reduce_sum.74
  290.7 0.1 reduce_sum.75
  290.8 0.1 reduce_sum.76
  290.9 0.2 reduce_sum.77
  291.1 0.1 reduce_sum.78
  291.2 0.1 reduce_sum.79
  291.4 2.6 convolution_bitcast_fusion.4
  294.0 2.6 convolution_bitcast_fusion.3
  296.7 5.5 %fusion.45 = f32[1,4,4,128]{3,2,1,0:T(4,128)S(1)} fusion(f32[4,512,1024]{2,1,0:T(8,128)} %copy-done.15, f32[1,4,8,128]{3,2,1,0:T(8,128)S(1)} %multiply_bitcast_fusion), kind=kOutput, calls=%fused_computation.71 | convolution fusion | flops 26738688 | bytes 8413184 | tf_op jit(solution)/shard_map/transpose(jvp(qk,qa->ka))/dot_general | solution.py:895
  302.3 0.8 fusion.39
  303.2 0.1 broadcast_select_fusion
  303.3 0.6 copy-done.18
  303.9 22.9 %finish_3.1 = (f32[3,8,128]{2,1,0:T(8,128)}, f32[104,128]{1,0:T(8,128)}, f32[4,128]{1,0:T(4,128)}, f32[8,128]{1,0:T(8,128)}) custom-call(f32[3,32,128]{2,1,0:T(8,128)} %bitcast.263, f32[3,8,128]{2,1,0:T(8,128)} %bitcast.276, f32[104,128]{1,0:T(8,128)} %bitcast.275), custom_call_target="tpu_custom_call" | custom-call | tf_op jit(solution)/shard_map/finish_3/pallas_call | solution.py:250
  326.8 1.3 slice_reduce_fusion
  328.1 0.8 slice_reduce_fusion.1
  328.8 0.7 reshape_squeeze.6
  329.5 0.7 fusion.78
  330.3 0.6 squeeze.78
  330.9 0.6 squeeze.79
  331.5 0.7 reshape_squeeze.7
  332.1 0.6 squeeze.80
  332.8 1.3 copy.58
  334.0 1.3 copy.59
  (62 shorter events, 0.2 us)
Async XLA Ops:
  0.6 116.6 %copy-start = (f32[4,512]{1,0:T(4,128)S(1)}, f32[4,512]{1,0:T(4,128)}, u32[]{:S(2)}) copy-start(f32[4,512]{1,0:T(4,128)} %param.29) | copy-start | bytes 24580
  15.3 1.0 copy-start.2
  16.3 0.9 copy-start.4
  17.2 0.8 copy-start.6
  18.0 0.7 copy-start.10
  18.7 0.7 copy-start.12
  51.1 11.8 %copy-start.17 = (s32[1,1024]{1,0:T(1,128)S(1)}, s32[1,1024]{1,0:T(1,128)}, u32[]{:S(2)}) copy-start(s32[1,1024]{1,0:T(1,128)} %param.18) | copy-start | bytes 12292
  51.1 11.8 %copy-start.20 = (f32[4,512]{1,0:T(4,128)S(1)}, f32[4,512]{1,0:T(4,128)}, u32[]{:S(2)}) copy-start(f32[4,512]{1,0:T(4,128)} %param.25) | copy-start | bytes 24580
  62.9 6.0 %copy-start.15 = (f32[4,512,1024]{2,1,0:T(8,128)}, f32[4,512,1024]{2,1,0:T(8,128)S(1)}, u32[]{:S(2)}) copy-start(f32[4,512,1024]{2,1,0:T(8,128)S(1)} %fusion.18) | copy-start | bytes 25165828
  62.9 4.8 %copy-start.19 = (f32[512,4]{0,1:T(4,128)S(1)}, f32[512,4]{0,1:T(4,128)}, u32[]{:S(2)}) copy-start(f32[512,4]{0,1:T(4,128)} %param.26) | copy-start | bytes 24580
  66.4 1.3 copy-start.14
  66.4 5.8 %slice-start = ((f32[96,128]{1,0:T(8,128)}), f32[72,128]{1,0:T(8,128)S(1)}, s32[]{:S(2)}) async-start(f32[96,128]{1,0:T(8,128)} %spread_0.1.tab_ref), calls=%async_computation | async-start | bytes 73728 | tf_op jit(solution)/shard_map/slice | solution.py:951
  66.4 6.7 %copy-start.3 = (s32[64,1024]{1,0:T(8,128)S(1)}, s32[64,1024]{1,0:T(8,128)}, u32[]{:S(2)}) copy-start(s32[64,1024]{1,0:T(8,128)} %get-tuple-element.46.idx_ref) | copy-start | bytes 786436
  66.4 6.7 %copy-start.5 = (f32[64,1024]{1,0:T(8,128)S(1)}, f32[64,1024]{1,0:T(8,128)}, u32[]{:S(2)}) copy-start(f32[64,1024]{1,0:T(8,128)} %get-tuple-element.47.wt_ref) | copy-start | bytes 786436
  66.4 6.7 %copy-start.9 = (f32[10,12]{1,0:T(8,128)S(1)}, f32[10,12]{1,0:T(8,128)}, u32[]{:S(2)}) copy-start(f32[10,12]{1,0:T(8,128)} %rad_ref.6) | copy-start | bytes 1444
  66.4 6.7 %copy-start.13 = (s32[3,8]{1,0:T(4,128)S(1)}, s32[3,8]{1,0:T(4,128)}, u32[]{:S(2)}) copy-start(s32[3,8]{1,0:T(4,128)} %get-tuple-element.45.info_ref) | copy-start | bytes 292
  73.1 47.6 %slice-start.1 = ((s8[8028160]{0:T(1024)(128)(4,1)}), s8[4194304]{0:T(1024)(128)(4,1)S(1)}, s32[]{:S(2)}) async-start(s8[8028160]{0:T(1024)(128)(4,1)} %bitcast.284), calls=%async_computation.1 | async-start | bytes 8388608
  105.2 15.5 %slice-start.2 = ((s8[8028160]{0:T(1024)(128)(4,1)}), s8[3833856]{0:T(1024)(128)(4,1)S(1)}, s32[]{:S(2)}) async-start(s8[8028160]{0:T(1024)(128)(4,1)} %bitcast.284), calls=%async_computation.2 | async-start | bytes 7667712
  223.0 12.9 %copy-start.7 = (f32[96,128]{1,0:T(8,128)S(1)}, f32[96,128]{1,0:T(8,128)}, u32[]{:S(2)}) copy-start(f32[96,128]{1,0:T(8,128)} %spread_0.1.tab_ref) | copy-start | bytes 147460
  223.0 12.9 %copy-start.11 = (f32[10,12]{1,0:T(8,128)S(1)}, f32[10,12]{1,0:T(8,128)}, u32[]{:S(2)}) copy-start(f32[10,12]{1,0:T(8,128)} %rad_ref.7) | copy-start | bytes 1444
  289.3 0.6 copy-start.8
  291.4 5.3 %copy-start.16 = (f32[4,8,128]{2,1,0:T(8,128)S(1)}, f32[4,8,128]{2,1,0:T(8,128)}, u32[]{:S(2)}) copy-start(f32[4,8,128]{2,1,0:T(8,128)} %collect_2.1) | copy-start | bytes 49156
  296.7 5.6 %copy-start.21 = (f32[1,512]{1,0:T(1,128)S(1)}, f32[1,512]{1,0:T(1,128)}, u32[]{:S(2)}) copy-start(f32[1,512]{1,0:T(1,128)} %param.22) | copy-start | bytes 6148
  296.7 5.7 %copy-start.22 = (s32[1,1024]{1,0:T(1,128)S(1)}, s32[1,1024]{1,0:T(1,128)}, u32[]{:S(2)}) copy-start(s32[1,1024]{1,0:T(1,128)} %param.21) | copy-start | bytes 12292
  296.7 38.6 %copy-start.1 = (f32[4,512]{1,0:T(4,128)S(1)}, f32[4,512]{1,0:T(4,128)}, u32[]{:S(2)}) copy-start(f32[4,512]{1,0:T(4,128)} %param.29) | copy-start | bytes 24580
  303.3 0.6 copy-start.18
where the time goes:
time: 340 us; the launch traced here: 335 us
  Pallas kernels  233 us (69%)
  matrix products  74.5 us (22%)
  local copies, waits for them, and re-layouts  20.3 us (6%)
  other arithmetic  6.65 us (2%)
    pallas_call x2, Pallas kernels, backward_call(): pl.pallas_call(partial(backward_kernel, layer), out_shape=(jax.ShapeDtype...  129 us
    pallas_call x2, Pallas kernels, density_call(): pl.pallas_call(partial(density_kernel, layer), out_shape=jax.ShapeDtypeSt...  63.8 us
    dot_general x2, matrix products, contract_back(): jnp.einsum('vdq,vqa->da', coupling, rounded, preferred_element_type=f32)  23.9 us
    dot_general x2, matrix products, contract(): jnp.einsum('vdq,da->vqa', coupling, dens_in, preferred_element_type=f32)  23.8 us
    pallas_call x1, Pallas kernels, finish_call(): pl.pallas_call(partial(finish_kernel, rows, sums_at, per_group), out_shap...  22.9 us
    dot_general x3, matrix products, feature_map(): jnp.einsum('qk,qa->ka', mixing, invariants, precision=highest) * inverse_rms  13.9 us
    unnamed x63, local copies, waits for them, and re-layouts  12.3 us
    pallas_call x2, Pallas kernels, spread_call(): pl.pallas_call(partial(spread_kernel, values), out_shape=jax.ShapeDtypeSt...  7.79 us

commit v1 on v0

v1 whole, which is shorter than its diff:
```python
from functools import partial, reduce
import math

import jax
import jax.numpy as jnp
from jax import lax
from jax.experimental import pallas as pl
from jax.experimental.pallas import tpu as pltpu
from jax.sharding import PartitionSpec as P

NRAD = 12
NMAX = 10
LMAX = 6
LM = 49
SPECIES = 4
CH = SPECIES * NMAX
DENS = CH * LM
NBR = 48
NPAD = 64
TILE = 128
LBLK = 7
WROWS = 12
WSTEP = 40
GEO = 5
NVAL = 7
SLOTS = 4
XROW = CH + 1

cutoff_radius = 5.0
density_scale = 0.17
norm_eps = 1e-05
ridge_weight = 0.1
highest = lax.Precision.HIGHEST
f32 = jnp.float32
MESH = pl.DeviceIdType.MESH
bf16 = jnp.bfloat16


def log2_of(count):
    steps = count.bit_length() - 1
    assert count == 1 << steps
    return steps


def neighbour_flags(me, count):
    return me > 0, me < count - 1


def greet(partners, flags):
    barrier = pltpu.get_barrier_semaphore()
    for partner, flag in zip(partners, flags):
        if flag is None:
            pl.semaphore_signal(barrier, inc=1, device_id=partner, device_id_type=MESH)
        else:

            @pl.when(flag)
            def _(partner=partner):
                pl.semaphore_signal(barrier, inc=1, device_id=partner, device_id_type=MESH)

    present = sum(1 for flag in flags if flag is None)
    for flag in flags:
        if flag is not None:
            present = present + jnp.where(flag, 1, 0)
    pl.semaphore_wait(barrier, present)


class SidePair:
    def __init__(self, to_left, to_right, got_ref, send_sem, recv_sem):
        count = lax.axis_size("dom")
        me = lax.axis_index("dom")
        self.partners = ({"dom": me - 1}, {"dom": me + 1})
        self.flags = neighbour_flags(me, count)
        self.got = got_ref
        self.copies = [
            pltpu.make_async_remote_copy(
                src_ref=source,
                dst_ref=got_ref.at[1 - side],
                send_sem=send_sem.at[side],
                recv_sem=recv_sem.at[1 - side],
                device_id=self.partners[side],
                device_id_type=MESH,
            )
            for side, source in enumerate((to_left, to_right))
        ]

    def start(self):
        for side in range(2):
            pl.when(self.flags[side])(self.copies[side].start)

    def wait(self):
        for side in range(2):

            @pl.when(self.flags[side])
            def _(side=side):
                self.copies[side].wait_send()
                self.copies[1 - side].wait_recv()

    def received(self, side):
        return jnp.where(self.flags[side], self.got[side], 0.0)


def split3(value):
    high = value.astype(bf16)
    rest = value - high.astype(f32)
    middle = rest.astype(bf16)
    low = (rest - middle.astype(f32)).astype(bf16)
    return jnp.concatenate([high, middle, low], axis=0)


def reorder(value, perm_ref, contract_at):
    count = value.shape[0]
    out = lax.dot_general(
        split3(value), perm_ref[...], (((1,), (contract_at,)), ((), ())), preferred_element_type=f32
    )
    return out[:count] + (out[count : 2 * count] + out[2 * count :])


def spread_kernel(values, ordered, *refs):
    if ordered:
        x_ref, out_ref, mine_ref, got_ref, send_sem, recv_sem = refs
        flat = x_ref[...]
    else:
        x_ref, perm_ref, out_ref, mine_ref, got_ref, send_sem, recv_sem = refs
        flat = reorder(x_ref[...], perm_ref, 0)
    rows = flat.shape[1] // TILE
    for value in range(values):
        for row in range(rows):
            line = flat[value : value + 1, row * TILE : (row + 1) * TILE]
            at = value * rows + row
            mine_ref[at : at + 1, :] = line
    pair = SidePair(mine_ref, mine_ref, got_ref, send_sem, recv_sem)
    greet(pair.partners, pair.flags)
    pair.start()
    for value in range(values):
        at = value * 3 * rows
        out_ref[at + rows : at + 2 * rows, :] = mine_ref[value * rows : (value + 1) * rows, :]
    pair.wait()
    for side in range(2):
        block = pair.received(side)
        for value in range(values):
            at = value * 3 * rows + 2 * side * rows
            out_ref[at : at + rows, :] = block[value * rows : (value + 1) * rows]


def comm_params(which):
    return pltpu.CompilerParams(collective_id=which, has_side_effects=True)


def vmem_spec():
    return pl.BlockSpec(memory_space=pltpu.VMEM)


def spread_call(which, values, cells, perm=None):
    rows = values * cells.shape[1] // TILE
    operands = (cells,) if perm is None else (cells, perm)
    return pl.pallas_call(
        partial(spread_kernel, values, perm is None),
        out_shape=jax.ShapeDtypeStruct((rows * 3, TILE), f32),
        in_specs=[vmem_spec()] * len(operands),
        out_specs=vmem_spec(),
        scratch_shapes=[
            pltpu.VMEM((rows, TILE), f32),
            pltpu.VMEM((2, rows, TILE), f32),
            pltpu.SemaphoreType.DMA((2,)),
            pltpu.SemaphoreType.DMA((2,)),
        ],
        compiler_params=comm_params(which),
        name="spread_%d" % which,
    )(*operands)


def in_lanes(blocks):
    values, rows = blocks.shape[0], blocks.shape[1]
    flat = [
        jnp.concatenate([blocks[v, r : r + 1, :] for r in range(rows)], axis=1) for v in range(values)
    ]
    return jnp.concatenate(flat + [jnp.zeros((8 - values, rows * TILE), f32)], axis=0)


def collect_kernel(rows, values_at, win_ref, perm_ref, out_ref, got_ref, send_sem, recv_sem):
    pair = SidePair(
        win_ref.at[values_at:, 0:rows],
        win_ref.at[values_at:, 2 * rows : 3 * rows],
        got_ref,
        send_sem,
        recv_sem,
    )
    greet(pair.partners, pair.flags)
    pair.start()
    pair.wait()
    total = win_ref[values_at:, rows : 2 * rows] + pair.received(0) + pair.received(1)
    out_ref[...] = reorder(in_lanes(total), perm_ref, 1)


def collect_call(which, rows, values_at, window, perm):
    values = window.shape[0] - values_at
    return pl.pallas_call(
        partial(collect_kernel, rows, values_at),
        out_shape=jax.ShapeDtypeStruct((8, rows * TILE), f32),
        in_specs=[vmem_spec()] * 2,
        out_specs=vmem_spec(),
        scratch_shapes=[
            pltpu.VMEM((2, values, rows, TILE), f32),
            pltpu.SemaphoreType.DMA((2,)),
            pltpu.SemaphoreType.DMA((2,)),
        ],
        compiler_params=comm_params(which),
        name="collect_%d" % which,
    )(window, perm)


def finish_kernel(rows, sums_at, per_group, win_ref, own_ref, perm_ref, pay_ref, force_ref, sum_ref, energy_ref,
                  offset_ref, got_ref, came_ref, send_sem, recv_sem, step_send, step_recv):
    pair = SidePair(
        win_ref.at[:, 0:rows], win_ref.at[:, 2 * rows : 3 * rows], got_ref, send_sem, recv_sem
    )
    partners = []
    for axis in ("dom", "grp"):
        me = lax.axis_index(axis)
        for bit in range(log2_of(lax.axis_size(axis))):
            half = 1 << bit
            partners.append({axis: me + half - 2 * half * lax.rem(lax.div(me, half), 2)})
    greet(list(pair.partners) + partners, list(pair.flags) + [None] * len(partners))
    pair.start()
    force_ref[...] = reorder(own_ref[...], perm_ref, 0)
    for step, partner in enumerate(partners):
        source = pay_ref if step == 0 else sum_ref
        copy = pltpu.make_async_remote_copy(
            src_ref=source,
            dst_ref=came_ref.at[step],
            send_sem=step_send.at[step],
            recv_sem=step_recv.at[step],
            device_id=partner,
            device_id_type=MESH,
        )
        copy.start()
        copy.wait()
        sum_ref[...] = source[...] + came_ref[step]
    pair.wait()
    total = win_ref[:, rows : 2 * rows] + pair.received(0) + pair.received(1)
    force_ref[...] = force_ref[...] - in_lanes(total)

    groups = lax.axis_size("grp")
    gram = [[None] * SPECIES for _ in range(SPECIES)]
    right = [None] * SPECIES

    def fractions(base):
        counts = [
            sum_ref[pl.ds(base + (1 + c) * per_group, per_group), :] for c in range(SPECIES)
        ]
        size = jnp.maximum(counts[0] + counts[1] + counts[2] + counts[3], 1.0)
        return [count / size for count in counts], size

    def gather_sum(total, value):
        part = jnp.sum(jnp.sum(value, axis=0, keepdims=True), axis=1, keepdims=True)
        return part if total is None else total + part

    stride = (SPECIES + 2) * per_group
    for group in range(groups):
        base = sums_at + group * stride
        frac, _ = fractions(base)
        target = sum_ref[pl.ds(base + (1 + SPECIES) * per_group, per_group), :]
        for c in range(SPECIES):
            right[c] = gather_sum(right[c], frac[c] * target)
            for d in range(c, SPECIES):
                gram[c][d] = gather_sum(gram[c][d], frac[c] * frac[d])
    matrix = [
        [gram[min(c, d)][max(c, d)] + (ridge_weight if c == d else 0.0) for d in range(SPECIES)]
        for c in range(SPECIES)
    ]
    for pivot in range(SPECIES):
        for below in range(pivot + 1, SPECIES):
            ratio = matrix[below][pivot] / matrix[pivot][pivot]
            matrix[below] = [b - ratio * a for a, b in zip(matrix[pivot], matrix[below])]
            right[below] = right[below] - ratio * right[pivot]
    answer = [None] * SPECIES
    for row in range(SPECIES - 1, -1, -1):
        running = right[row]
        for later in range(row + 1, SPECIES):
            running = running - matrix[row][later] * answer[later]
        answer[row] = running / matrix[row][row]
    mine = sums_at + lax.axis_index("grp") * stride
    frac, size = fractions(mine)
    energy = sum_ref[pl.ds(mine, per_group), :] / size
    for c in range(SPECIES):
        energy = energy + frac[c] * answer[c]
    energy_ref[...] = energy
    offset_ref[...] = jnp.concatenate(
        [jnp.broadcast_to(value, (1, TILE)) for value in answer] + [jnp.zeros((4, TILE), f32)], axis=0
    )


def finish_call(which, mesh_steps, rows, sums_at, per_group, window, own, perm, payload):
    size = payload.shape[0]
    return pl.pallas_call(
        partial(finish_kernel, rows, sums_at, per_group),
        out_shape=(
            jax.ShapeDtypeStruct((8, rows * TILE), f32),
            jax.ShapeDtypeStruct((size, TILE), f32),
            jax.ShapeDtypeStruct((per_group, TILE), f32),
            jax.ShapeDtypeStruct((8, TILE), f32),
        ),
        in_specs=[vmem_spec()] * 4,
        out_specs=(vmem_spec(),) * 4,
        scratch_shapes=[
            pltpu.VMEM((2, 3, rows, TILE), f32),
            pltpu.VMEM((mesh_steps, size, TILE), f32),
            pltpu.SemaphoreType.DMA((2,)),
            pltpu.SemaphoreType.DMA((2,)),
            pltpu.SemaphoreType.DMA((mesh_steps,)),
            pltpu.SemaphoreType.DMA((mesh_steps,)),
        ],
        compiler_params=comm_params(which),
        name="finish_%d" % which,
    )(window, own, perm, payload)


def double_factorial(number):
    result = 1.0
    while number > 1:
        result = result * number
        number = number - 2
    return result


def norm_of(degree, azimuth):
    value = math.sqrt(
        (2 * degree + 1)
        / (4 * math.pi)
        * math.factorial(degree - azimuth)
        / math.factorial(degree + azimuth)
    )
    return value * (math.sqrt(2.0) if azimuth else 1.0)


def scaled_legendre(coord_z):
    table = {}
    for azimuth in range(LMAX + 1):
        table[azimuth, azimuth] = norm_of(azimuth, azimuth) * double_factorial(2 * azimuth - 1)
        if azimuth + 1 <= LMAX:
            ratio = norm_of(azimuth + 1, azimuth) / norm_of(azimuth, azimuth)
            table[azimuth + 1, azimuth] = coord_z * (
                (2 * azimuth + 1) * ratio * table[azimuth, azimuth]
            )
        for degree in range(azimuth + 2, LMAX + 1):
            gap = degree - azimuth
            first = (2 * degree - 1) / gap * norm_of(degree, azimuth) / norm_of(degree - 1, azimuth)
            second = (
                (degree + azimuth - 1) / gap * norm_of(degree, azimuth) / norm_of(degree - 2, azimuth)
            )
            table[degree, azimuth] = (first * coord_z) * table[degree - 1, azimuth] - (
                second * table[degree - 2, azimuth]
            )
    return table


def azimuth_powers(coord_x, coord_y):
    cosines = [None, coord_x]
    sines = [None, coord_y]
    for _ in range(2, LMAX + 1):
        cosines.append(cosines[-1] * coord_x - sines[-1] * coord_y)
        sines.append(sines[-1] * coord_x + cosines[-2] * coord_y)
    return cosines, sines


LANE_GATHER = lax.GatherDimensionNumbers(
    offset_dims=(),
    collapsed_slice_dims=(1,),
    start_index_map=(1,),
    operand_batching_dims=(0,),
    start_indices_batching_dims=(0,),
)


def lane_gather(line, lo):
    return lax.gather(
        line,
        lo[..., None],
        LANE_GATHER,
        slice_sizes=(1, 1),
        mode=lax.GatherScatterMode.PROMISE_IN_BOUNDS,
    )


def prepare_kernel(first_ref, cnt_ref, nbr_ref, site_ref, idx_ref, wt_ref, sorted_ref, perm_ref, info_ref,
                   key_ref, pos_ref, word_ref, rank_ref):
    atoms = nbr_ref.shape[1]
    tiles = atoms // TILE
    blocks = NBR // 8
    sub = lax.broadcasted_iota(jnp.int32, (8, TILE), 0)
    lane = lax.broadcasted_iota(jnp.int32, (1, TILE), 1)

    def merge(tile, carry):
        cols = pl.ds(pl.multiple_of(tile * TILE, TILE), TILE)
        limit = cnt_ref[:, cols]
        iota = lax.broadcasted_iota(jnp.int32, (NBR, TILE), 0)
        key = jnp.where(iota < limit, nbr_ref[:, cols] - first_ref[0], -1 - iota)
        key_ref[...] = key
        keys = [key[8 * b : 8 * b + 8] for b in range(blocks)]
        total = [jnp.zeros((8, TILE), jnp.int32) for _ in range(blocks)]
        early = [jnp.zeros((8, TILE), jnp.int32) for _ in range(blocks)]
        for other in range(NBR):
            line = jnp.broadcast_to(key_ref[other : other + 1, :], (8, TILE))
            for b in range(blocks):
                same = jnp.where(keys[b] == line, 1, 0)
                total[b] = total[b] + same
                if other < 8 * b:
                    early[b] = early[b] + same
                elif other < 8 * b + 7:
                    early[b] = early[b] + jnp.where(sub > other - 8 * b, same, 0)
        for b in range(blocks):
            alive = sub + 8 * b < limit
            pos_ref[8 * b : 8 * b + 8, :] = jnp.where(alive & (early[b] == 0), 1, 0)
            key_ref[8 * b : 8 * b + 8, :] = total[b] * 4096 + keys[b]
        running = jnp.zeros((1, TILE), jnp.int32)
        out = [jnp.zeros((8, TILE), jnp.int32) for _ in range(blocks)]
        for slot in range(NBR):
            flag = pos_ref[slot : slot + 1, :]
            place = jnp.broadcast_to(jnp.where(flag == 1, running, -1), (8, TILE))
            running = running + flag
            line = jnp.broadcast_to(key_ref[slot : slot + 1, :], (8, TILE))
            for b in range(slot // 8 + 1):
                out[b] = jnp.where(place == sub + 8 * b, line, out[b])
        for b in range(blocks):
            word_ref[8 * b : 8 * b + 8, cols] = out[b].astype(f32)
        order = running * atoms + (atoms - 1 - tile * TILE) - lane
        rank_ref[pl.ds(tile, 1), :] = order.astype(f32)
        return carry

    lax.fori_loop(0, tiles, merge, 0)
    orders = rank_ref[...]
    upright = jnp.transpose(orders)
    ranks = []
    for tile in range(tiles):
        row = jnp.broadcast_to(orders[tile : tile + 1], (TILE, TILE))
        total = jnp.zeros((TILE, TILE), f32)
        for other in range(tiles):
            col = jnp.broadcast_to(upright[:, other : other + 1], (TILE, TILE))
            total = total + jnp.where(col > row, 1.0, 0.0)
        ranks.append(jnp.sum(total, axis=0, keepdims=True))
    place = lax.broadcasted_iota(jnp.int32, (atoms, TILE), 0).astype(f32)
    for tile in range(tiles):
        line = jnp.broadcast_to(ranks[tile], (atoms, TILE))
        perm_ref[:, tile * TILE : (tile + 1) * TILE] = jnp.where(line == place, 1.0, 0.0).astype(bf16)
    word_ref[NBR : NBR + 8, :] = site_ref[...]
    moved = reorder(word_ref[...], perm_ref, 1)
    sorted_ref[...] = moved[NBR:]
    word = moved[:NBR].astype(jnp.int32)
    index = lax.bitwise_and(word, 4095)
    times = lax.shift_right_logical(word, 12)
    idx_ref[:NBR, :] = index
    idx_ref[NBR:, :] = jnp.zeros((NPAD - NBR, atoms), jnp.int32)
    wt_ref[:NBR, :] = density_scale * times.astype(f32)
    wt_ref[NBR:, :] = jnp.zeros((NPAD - NBR, atoms), f32)
    row = lax.shift_right_logical(index, 7)
    low = jnp.min(jnp.where(times > 0, row, 1 << 20))
    high = jnp.max(jnp.where(times > 0, row, -1))
    slots = lax.broadcasted_iota(jnp.int32, (NBR, TILE), 0) + 1
    for tile in range(tiles):
        used = times[:, tile * TILE : (tile + 1) * TILE] > 0
        info_ref[0, tile] = lax.div(jnp.max(jnp.where(used, slots, 0)) + SLOTS - 1, SLOTS) * SLOTS
        info_ref[1, tile] = low
        info_ref[2, tile] = high


def prepare_call(first, limits, neighbours, site):
    atoms = neighbours.shape[1]
    return pl.pallas_call(
        prepare_kernel,
        out_shape=(
            jax.ShapeDtypeStruct((NPAD, atoms), jnp.int32),
            jax.ShapeDtypeStruct((NPAD, atoms), f32),
            jax.ShapeDtypeStruct((8, atoms), f32),
            jax.ShapeDtypeStruct((atoms, atoms), bf16),
            jax.ShapeDtypeStruct((3, atoms // TILE), jnp.int32),
        ),
        in_specs=[smem_spec(), vmem_spec(), vmem_spec(), vmem_spec()],
        out_specs=(vmem_spec(), vmem_spec(), vmem_spec(), vmem_spec(), smem_spec()),
        scratch_shapes=[
            pltpu.VMEM((NBR, TILE), jnp.int32),
            pltpu.VMEM((NBR, TILE), jnp.int32),
            pltpu.VMEM((NBR + 8, atoms), f32),
            pltpu.VMEM((atoms // TILE, TILE), f32),
        ],
        name="prepare",
    )(first, limits, neighbours, site)


def fetch(tab_ref, values, idx_ref, put_ref, chunk, row_low, row_high):
    start = pl.multiple_of(chunk * 32, 32)
    index = [idx_ref[pl.ds(start + 8 * kb, 8), :] for kb in range(4)]
    hi = [lax.shift_right_logical(word, 7) for word in index]
    lo = [lax.bitwise_and(word, 127) for word in index]

    def body(row, found):
        found = list(found)
        hits = [word == row for word in hi]
        for value in range(values):
            line = jnp.broadcast_to(tab_ref[pl.ds(value * 24 + row, 1), :], (8, TILE))
            for kb in range(4):
                at = value * 4 + kb
                found[at] = jnp.where(hits[kb], lane_gather(line, lo[kb]), found[at])
        return tuple(found)

    zero = jnp.zeros((8, TILE), f32)
    found = lax.fori_loop(row_low, row_high + 1, body, tuple(zero for _ in range(4 * values)))
    for value in range(values):
        for kb in range(4):
            put_ref[pl.ds(pl.multiple_of(value * NPAD + start + 8 * kb, 8), 8), :] = found[value * 4 + kb]


def slot_rows(which, base):
    return pl.ds(pl.multiple_of(which * NPAD + base, 8), 8)


def geometry(layer, geo_ref, feat_ref, wt_ref, base):
    weight = wt_ref[pl.ds(base, 8), :]
    unit = [geo_ref[slot_rows(axis, base), :] for axis in range(3)]
    dist = geo_ref[slot_rows(4, base), :]
    if layer == 1:
        kind = geo_ref[slot_rows(3, base), :]
        chan = [jnp.where(kind == float(c), 1.0, 0.0) for c in range(SPECIES)]
    else:
        chan = [feat_ref[slot_rows(c, base), :] for c in range(SPECIES)]
    return weight, dist, unit, chan


def radial_terms(dist, rad_ref, with_slope):
    scaled = dist * (2.0 / cutoff_radius) - 1.0
    inside = dist < cutoff_radius
    angle = dist * (math.pi / cutoff_radius)
    cutoff = jnp.where(inside, 0.5 * (jnp.cos(angle) + 1.0), 0.0)
    cheb = [None, scaled]
    twice = 2.0 * scaled
    cheb.append(twice * scaled - 1.0)
    for _ in range(3, NRAD):
        cheb.append(twice * cheb[-1] - cheb[-2])
    basis = [cutoff] + [cutoff * cheb[p] for p in range(1, NRAD)]
    radial = []
    for n in range(NMAX):
        total = basis[0] * rad_ref[n, 0]
        for p in range(1, NRAD):
            total = total + basis[p] * rad_ref[n, p]
        radial.append(total)
    if not with_slope:
        return basis, radial, None
    slope_cut = jnp.where(inside, (-0.5 * math.pi / cutoff_radius) * jnp.sin(angle), 0.0)
    grad_scaled = cutoff * (2.0 / cutoff_radius)
    second = [None, None, twice]
    second[1] = jnp.ones_like(scaled)
    for _ in range(3, NRAD):
        second.append(twice * second[-1] - second[-2])
    slopes = [slope_cut, slope_cut * scaled + grad_scaled]
    for p in range(2, NRAD):
        slopes.append(slope_cut * cheb[p] + grad_scaled * (float(p) * second[p]))
    return basis, radial, slopes


def harmonic_list(unit):
    table = scaled_legendre(unit[2])
    cosines, sines = azimuth_powers(unit[0], unit[1])
    columns = []
    for degree in range(LMAX + 1):
        for signed in range(-degree, degree + 1):
            azimuth = abs(signed)
            poly = table[degree, azimuth]
            if signed == 0:
                columns.append(poly)
            elif signed > 0:
                columns.append(poly * cosines[azimuth])
            else:
                columns.append(poly * sines[azimuth])
    columns[0] = jnp.full_like(unit[2], columns[0])
    return columns


def density_kernel(layer, info_ref, rad_ref, tab_ref, cen_ref, idx_ref, wt_ref, *refs):
    if layer == 1:
        out_ref, geo_ref, x_ref, y_ref, d_ref = refs
        feat_ref, put_ref = None, geo_ref
    else:
        geo_ref, out_ref, feat_ref, x_ref, y_ref, d_ref = refs
        put_ref = feat_ref
    tile = pl.program_id(0)
    count = info_ref[0, tile]
    row_low, row_high = info_ref[1, tile], info_ref[2, tile]
    blocks = lax.div(count + 7, 8)

    def gather_chunk(chunk, carry):
        fetch(tab_ref, 4, idx_ref, put_ref, chunk, row_low, row_high)
        return carry

    lax.fori_loop(0, lax.div(count + 31, 32), gather_chunk, 0)

    def edges(block_at, carry):
        base = pl.multiple_of(block_at * 8, 8)
        if layer == 1:
            live = wt_ref[pl.ds(base, 8), :] > 0.0
            deltas = []
            for axis in range(3):
                centre = jnp.broadcast_to(cen_ref[pl.ds(axis, 1), :], (8, TILE))
                delta = geo_ref[slot_rows(axis, base), :] - centre
                deltas.append(jnp.where(live, delta, 1.0))
            dist = jnp.sqrt(deltas[0] * deltas[0] + deltas[1] * deltas[1] + deltas[2] * deltas[2])
            inv = 1.0 / dist
            for axis in range(3):
                geo_ref[slot_rows(axis, base), :] = deltas[axis] * inv
            geo_ref[slot_rows(4, base), :] = dist
        weight, dist, unit, chan = geometry(layer, geo_ref, feat_ref, wt_ref, base)
        _, radial, _ = radial_terms(dist, rad_ref, False)
        for c in range(SPECIES):
            scale = chan[c] * weight
            for n in range(NMAX):
                x_ref[pl.ds(base * XROW + (c * NMAX + n), 8, stride=XROW), :] = scale * radial[n]
        for at, column in enumerate(harmonic_list(unit)):
            y_ref[slot_rows(at, base), :] = column
        return carry

    lax.fori_loop(0, blocks, edges, 0)
    groups = lax.div(count, SLOTS)

    def lm_block(block_at, carry):
        first = block_at * LBLK

        def slots(group, acc):
            acc = list(acc)
            for part in range(SLOTS):
                slot = group * SLOTS + part
                rows = [x_ref[pl.ds(slot * XROW + 8 * j, 8), :] for j in range(CH // 8)]
                for at in range(LBLK):
                    line = jnp.broadcast_to(
                        y_ref[pl.ds((first + at) * NPAD + slot, 1), :], (8, TILE)
                    )
                    for j in range(CH // 8):
                        acc[at * (CH // 8) + j] = acc[at * (CH // 8) + j] + rows[j] * line
            return tuple(acc)

        zero = jnp.zeros((8, TILE), f32)
        acc = lax.fori_loop(0, groups, slots, tuple(zero for _ in range(LBLK * (CH // 8))))
        for at in range(LBLK):
            for j in range(CH // 8):
                d_ref[pl.ds(8 * j * LM + first + at, 8, stride=LM), :] = acc[at * (CH // 8) + j]
        return carry

    lax.fori_loop(0, LM // LBLK, lm_block, 0)
    out_ref[...] = d_ref[...].astype(bf16)


def smem_spec():
    return pl.BlockSpec(memory_space=pltpu.SMEM)


def tile_spec(rows):
    return pl.BlockSpec((rows, TILE), lambda i: (0, i))


def whole_spec(shape):
    return pl.BlockSpec(shape, lambda i: tuple(0 for _ in shape))


def density_call(layer, info, radial, table, centres, index, weight, geo=None):
    atoms = centres.shape[1]
    rows = GEO if layer == 1 else SPECIES
    extra = () if geo is None else (geo,)
    return pl.pallas_call(
        partial(density_kernel, layer),
        out_shape=(
            jax.ShapeDtypeStruct((DENS, atoms), bf16),
            jax.ShapeDtypeStruct((rows * NPAD, atoms), f32),
        ),
        grid=(atoms // TILE,),
        in_specs=[
            smem_spec(),
            smem_spec(),
            whole_spec(table.shape),
            tile_spec(8),
            tile_spec(NPAD),
            tile_spec(NPAD),
        ]
        + [tile_spec(GEO * NPAD)] * len(extra),
        out_specs=(tile_spec(DENS), tile_spec(rows * NPAD)),
        scratch_shapes=[
            pltpu.VMEM((NPAD * XROW + 8, TILE), f32),
            pltpu.VMEM((LM * NPAD, TILE), f32),
            pltpu.VMEM((DENS, TILE), f32),
        ],
        compiler_params=pltpu.CompilerParams(vmem_limit_bytes=48 << 20),
        name="density_%d" % layer,
    )(info, radial, table, centres, index, weight, *extra)


def backward_kernel(layer, info_ref, rad_ref, geo_ref, feat_ref, idx_ref, wt_ref, dd_ref, win_in_ref,
                    own_in_ref, win_ref, own_ref, rgr_ref, x_ref, y_ref, gx_ref, gy_ref, val_ref,
                    left_ref):
    tile = pl.program_id(0)
    count = info_ref[0, tile]
    row_low, row_high = info_ref[1, tile], info_ref[2, tile]
    blocks = lax.div(count + 7, 8)
    zero = jnp.zeros((8, TILE), f32)

    @pl.when(tile == 0)
    def _():
        if layer == 1:
            win_ref[...] = win_in_ref[: 3 * WSTEP]
        else:
            win_ref[...] = jnp.zeros_like(win_ref)
        rgr_ref[...] = jnp.zeros_like(rgr_ref)

    def line_of(at):
        return jnp.broadcast_to(dd_ref[pl.ds(at, 1), :], (8, TILE))

    def contract_slots():
        def over_lm(step, acc):
            acc = list(acc)
            for part in range(LBLK):
                lm = step * LBLK + part
                col = y_ref[pl.ds(pl.multiple_of(lm * 8, 8), 8), :]
                for m in range(CH):
                    acc[m] = acc[m] + line_of(m * LM + lm) * col
            return tuple(acc)

        acc = lax.fori_loop(0, LM // LBLK, over_lm, tuple(zero for _ in range(CH)))
        for m in range(CH):
            gx_ref[8 * m : 8 * m + 8, :] = acc[m]

        def over_m(step, acc):
            acc = list(acc)
            for part in range(4):
                m = step * 4 + part
                col = x_ref[pl.ds(pl.multiple_of(m * 8, 8), 8), :]
                for lm in range(LM):
                    acc[lm] = acc[lm] + line_of(m * LM + lm) * col
            return tuple(acc)

        acc = lax.fori_loop(0, CH // 4, over_m, tuple(zero for _ in range(LM)))
        for lm in range(LM):
            gy_ref[8 * lm : 8 * lm + 8, :] = acc[lm]

    def contract_species(kind):
        odd = (kind == 1.0) | (kind == 3.0)
        upper = kind > 1.5

        def over_n(step, acc):
            acc = list(acc)
            for part in range(2):
                n = step * 2 + part
                at = pl.multiple_of(n * 8, 8)
                scaled = x_ref[pl.ds(at, 8), :]
                sums = [None, None]
                for lm in range(LM):
                    lines = [line_of((c * NMAX + n) * LM + lm) for c in range(SPECIES)]
                    first = jnp.where(odd, lines[1], lines[0])
                    second = jnp.where(odd, lines[3], lines[2])
                    grad = jnp.where(upper, second, first)
                    acc[lm] = acc[lm] + grad * scaled
                    term = grad * y_ref[8 * lm : 8 * lm + 8, :]
                    sums[lm % 2] = term if lm < 2 else sums[lm % 2] + term
                gx_ref[pl.ds(at, 8), :] = sums[0] + sums[1]
            return tuple(acc)

        acc = lax.fori_loop(0, NMAX // 2, over_n, tuple(zero for _ in range(LM)))
        for lm in range(LM):
            gy_ref[8 * lm : 8 * lm + 8, :] = acc[lm]

    def slot_block(block_at, own):
        base = pl.multiple_of(block_at * 8, 8)
        weight, dist, unit, chan = geometry(layer, geo_ref, feat_ref, wt_ref, base)
        _, radial, _ = radial_terms(dist, rad_ref, False)
        for at, column in enumerate(harmonic_list(unit)):
            y_ref[8 * at : 8 * at + 8, :] = column
        if layer == 1:
            for n in range(NMAX):
                x_ref[8 * n : 8 * n + 8, :] = weight * radial[n]
            contract_species(geo_ref[slot_rows(3, base), :])
        else:
            for c in range(SPECIES):
                scale = chan[c] * weight
                for n in range(NMAX):
                    at = 8 * (c * NMAX + n)
                    x_ref[at : at + 8, :] = scale * radial[n]
            contract_slots()
        weight, dist, unit, chan = geometry(layer, geo_ref, feat_ref, wt_ref, base)
        inv = 1.0 / dist
        basis, radial, slopes = radial_terms(dist, rad_ref, True)
        feat_grads = []
        radial_grads = [None] * NMAX
        if layer == 1:
            radial_grads = [gx_ref[8 * n : 8 * n + 8, :] for n in range(NMAX)]
        for c in range(SPECIES if layer == 2 else 0):
            total = None
            for n in range(NMAX):
                grad = gx_ref[8 * (c * NMAX + n) : 8 * (c * NMAX + n) + 8, :]
                term = grad * radial[n]
                total = term if total is None else total + term
                piece = grad * chan[c]
                radial_grads[n] = piece if c == 0 else radial_grads[n] + piece
            feat_grads.append(total * weight)
        grad_r = None
        radial_grads = [grad * weight for grad in radial_grads]
        for p in range(NRAD):
            total = None
            for n in range(NMAX):
                at = (n * NRAD + p) * 8
                rgr_ref[pl.ds(at, 8), :] = rgr_ref[pl.ds(at, 8), :] + radial_grads[n] * basis[p]
                term = radial_grads[n] * rad_ref[n, p]
                total = term if total is None else total + term
            term = total * slopes[p]
            grad_r = term if grad_r is None else grad_r + term
        table = scaled_legendre(unit[2])
        cosines, sines = azimuth_powers(unit[0], unit[1])
        grad_x = grad_y = grad_z = None

        def plus(total, term):
            return term if total is None else total + term

        for azimuth in range(LMAX + 1):
            grad_cos = grad_sin = None
            for degree in range(azimuth, LMAX + 1):
                at = degree * degree + degree
                up = gy_ref[8 * (at + azimuth) : 8 * (at + azimuth) + 8, :]
                poly = table[degree, azimuth]
                if azimuth:
                    down = gy_ref[8 * (at - azimuth) : 8 * (at - azimuth) + 8, :]
                    grad_cos = plus(grad_cos, up * poly)
                    grad_sin = plus(grad_sin, down * poly)
                if degree > azimuth:
                    ratio = norm_of(degree, azimuth) / norm_of(degree, azimuth + 1)
                    slope = ratio * table[degree, azimuth + 1]
                    if azimuth:
                        grad_z = plus(grad_z, slope * (up * cosines[azimuth] + down * sines[azimuth]))
                    else:
                        grad_z = plus(grad_z, slope * up)
            if azimuth == 1:
                grad_x, grad_y = grad_cos, grad_sin
            elif azimuth > 1:
                below_cos, below_sin = cosines[azimuth - 1], sines[azimuth - 1]
                grad_x = grad_x + float(azimuth) * (grad_cos * below_cos + grad_sin * below_sin)
                grad_y = grad_y + float(azimuth) * (grad_sin * below_cos - grad_cos * below_sin)
        dot_u = grad_x * unit[0] + grad_y * unit[1] + grad_z * unit[2]
        live = weight > 0.0
        out = []
        for axis, grad in enumerate((grad_x, grad_y, grad_z)):
            value = (grad - dot_u * unit[axis]) * inv + grad_r * unit[axis]
            out.append(jnp.where(live, value, 0.0))
        values = out + feat_grads
        for at, value in enumerate(values):
            val_ref[slot_rows(at, base), :] = value
        return tuple(total + value for total, value in zip(own, out))


    own = lax.fori_loop(0, blocks, slot_block, (zero, zero, zero))
    own = jnp.concatenate(
        [jnp.sum(total, axis=0, keepdims=True) for total in own] + [jnp.zeros((5, TILE), f32)], axis=0
    )
    own_ref[...] = own + own_in_ref[...] if layer == 1 else own

    used = 3 if layer == 1 else NVAL
    height = used * WROWS
    step_rows = height + 1
    sub = lax.broadcasted_iota(jnp.int32, (TILE, TILE), 0)
    windows = lax.div(row_high - row_low + WROWS, WROWS)

    def window(window_at, carry):
        row_base = row_low + window_at * WROWS

        def scatter(block_at, acc):
            base = pl.multiple_of(block_at * 8, 8)
            index = idx_ref[pl.ds(base, 8), :]
            hi = lax.shift_right_logical(index, 7)
            lo = lax.bitwise_and(index, 127)
            for row in range(WROWS):
                hit = hi == row_base + row
                for value_at in range(used):
                    value = val_ref[slot_rows(value_at, base), :]
                    left_ref[pl.ds(value_at * WROWS + row, 8, stride=step_rows), :] = jnp.where(
                        hit, value, 0.0
                    )
            ones, left = [], []
            for part in range(8):
                line = jnp.broadcast_to(lo[part : part + 1, :], (TILE, TILE))
                ones.append(jnp.where(line == sub, 1.0, 0.0).astype(bf16))
                left.append(left_ref[part * step_rows : part * step_rows + height, :])
            left = jnp.concatenate(left, axis=1)
            ones = jnp.concatenate(ones, axis=1)
            high = left.astype(bf16)
            rest = (left - high.astype(f32)).astype(bf16)
            dims = (((1,), (1,)), ((), ()))
            acc = acc + lax.dot_general(high, ones, dims, preferred_element_type=f32)
            return acc + lax.dot_general(rest, ones, dims, preferred_element_type=f32)

        acc = lax.fori_loop(0, blocks, scatter, jnp.zeros((height, TILE), f32))
        for value_at in range(used):
            at = value_at * WSTEP + row_base
            win_ref[pl.ds(at, WROWS), :] = (
                win_ref[pl.ds(at, WROWS), :] + acc[value_at * WROWS : (value_at + 1) * WROWS]
            )
        return carry

    lax.fori_loop(0, windows, window, 0)


def backward_call(layer, info, radial, geo, feat, index, weight, grad_dens, window_in, own_in):
    atoms = index.shape[1]
    values = 3 if layer == 1 else NVAL
    return pl.pallas_call(
        partial(backward_kernel, layer),
        out_shape=(
            jax.ShapeDtypeStruct((values * WSTEP, TILE), f32),
            jax.ShapeDtypeStruct((8, atoms), f32),
            jax.ShapeDtypeStruct((NMAX * NRAD * 8, TILE), f32),
        ),
        grid=(atoms // TILE,),
        in_specs=[
            smem_spec(),
            smem_spec(),
            tile_spec(GEO * NPAD),
            tile_spec(feat.shape[0]),
            tile_spec(NPAD),
            tile_spec(NPAD),
            tile_spec(DENS),
            whole_spec(window_in.shape),
            tile_spec(8),
        ],
        out_specs=(
            whole_spec((values * WSTEP, TILE)),
            tile_spec(8),
            whole_spec((NMAX * NRAD * 8, TILE)),
        ),
        scratch_shapes=[
            pltpu.VMEM((CH * 8, TILE), f32),
            pltpu.VMEM((LM * 8, TILE), f32),
            pltpu.VMEM((CH * 8, TILE), f32),
            pltpu.VMEM((LM * 8, TILE), f32),
            pltpu.VMEM((NVAL * NPAD, TILE), f32),
            pltpu.VMEM((8 * (NVAL * WROWS + 1), TILE), f32),
        ],
        compiler_params=pltpu.CompilerParams(vmem_limit_bytes=48 << 20),
        name="backward_%d" % layer,
    )(info, radial, geo, feat, index, weight, grad_dens, window_in, own_in)


def feature_map(invariants, mixing):
    inverse_rms = lax.rsqrt(jnp.mean(invariants * invariants, axis=0) + norm_eps)
    return jnp.einsum("qk,qa->ka", mixing, invariants, precision=highest) * inverse_rms


def contract(dens_in, coupling):
    factors = jnp.einsum("vdq,da->vqa", coupling, dens_in, preferred_element_type=f32)
    product = reduce(
        lambda earlier, later: earlier * later,
        [factors[index_v] for index_v in range(factors.shape[0])],
    )
    return (factors, product)


def contract_back(factors, upstream, coupling):
    partials = []
    for factor_at in range(factors.shape[0]):
        others = upstream
        for partner in range(factors.shape[0]):
            if partner != factor_at:
                others = others * factors[partner]
        partials.append(others)
    rounded = jnp.stack(partials).astype(bf16)
    return jnp.einsum("vdq,vqa->da", coupling, rounded, preferred_element_type=f32)


def per_device(
    positions,
    species,
    neighbours,
    slot_counts,
    structure,
    target_energy,
    radial_one,
    coupling_one,
    coefficient_one,
    mixing,
    radial_two,
    coupling_two,
    coefficient_two,
):
    atoms = positions.shape[2]
    tiles = atoms // TILE
    site = jnp.concatenate(
        [
            positions[:, 0, :],
            species.astype(f32),
            structure.astype(f32),
            jnp.zeros((3, atoms), f32),
        ],
        axis=0,
    )
    table_one = spread_call(0, 4, site)
    first = ((lax.axis_index("dom") - 1) * atoms).astype(jnp.int32).reshape(1)
    index, weight, ordered, perm, info = prepare_call(first, slot_counts, neighbours[:, 0, :], site)
    onehot = (ordered[3:4] == jnp.arange(SPECIES, dtype=f32)[:, None]).astype(f32)

    dens_one, geo = density_call(1, info, radial_one, table_one, ordered, index, weight)
    factors_one, invariants_one = contract(dens_one, coupling_one)
    chosen_one = jnp.dot(coefficient_one.T, onehot, precision=highest)
    energy_one = jnp.sum(invariants_one * chosen_one, axis=0)
    features, features_back = jax.vjp(feature_map, invariants_one, mixing)
    features8 = jnp.pad(features, ((0, 8 - SPECIES), (0, 0)))
    table_two = spread_call(1, SPECIES, features8, perm)
    dens_two, feat = density_call(2, info, radial_two, table_two, ordered, index, weight, geo)
    factors_two, invariants_two = contract(dens_two, coupling_two)
    chosen_two = jnp.dot(coefficient_two.T, onehot, precision=highest)
    site_energy = energy_one + jnp.sum(invariants_two * chosen_two, axis=0)
    structures = target_energy.shape[1]
    members = (ordered[4][:, None] == jnp.arange(structures, dtype=f32)[None, :]).astype(f32)
    per_structure = jnp.dot(
        jnp.concatenate([site_energy[None, :], onehot], axis=0), members, precision=highest
    )
    target = jnp.where(lax.axis_index("dom") == 0, target_energy, 0.0)
    per_structure = jnp.concatenate([per_structure, target], axis=0)

    grad_dens_two = contract_back(factors_two, chosen_two, coupling_two)
    blank_window = jnp.zeros((8, TILE), f32)
    blank_own = jnp.zeros((8, atoms), f32)
    window_two, own_two, rgr_two = backward_call(
        2, info, radial_two, geo, feat, index, weight, grad_dens_two, blank_window, blank_own
    )
    grad_features = collect_call(
        2, tiles, 3, window_two.reshape(NVAL, WSTEP, TILE), perm
    )[:SPECIES]
    coefficient_second = jnp.dot(onehot, invariants_two.T, precision=highest)
    grad_invariants, mixing_gradient = features_back(grad_features)
    grad_dens_one = contract_back(factors_one, chosen_one + grad_invariants, coupling_one)
    window_one, own_one, rgr_one = backward_call(
        1, info, radial_one, geo, blank_own, index, weight, grad_dens_one, window_two, own_two
    )
    coefficient_first = jnp.dot(onehot, invariants_one.T, precision=highest)

    def radial_sum(partial_grad):
        return jnp.sum(partial_grad.reshape(NMAX * NRAD, 8 * TILE), axis=1)

    groups = lax.axis_size("grp")
    mine = lax.axis_index("grp") == jnp.arange(groups, dtype=jnp.int32)
    slots = jnp.where(mine[:, None, None], per_structure[None], 0.0)
    quantum = coefficient_first.shape[1]
    wide = SPECIES * quantum
    radials = jnp.zeros((8 * TILE,), f32)
    radials = radials.at[: NMAX * NRAD].set(radial_sum(rgr_one))
    radials = radials.at[TILE : TILE + NMAX * NRAD].set(radial_sum(rgr_two))
    payload = jnp.concatenate(
        [
            radials,
            coefficient_first.reshape(-1),
            coefficient_second.reshape(-1),
            mixing_gradient.T.reshape(-1),
            slots.reshape(-1),
        ]
    )
    sums_at = 8 + 3 * wide // TILE
    steps = log2_of(lax.axis_size("dom")) + log2_of(groups)
    forces, sums, energies, offsets = finish_call(
        3,
        steps,
        tiles,
        sums_at,
        structures // TILE,
        window_one.reshape(3, WSTEP, TILE),
        own_one,
        perm,
        payload.reshape(-1, TILE),
    )
    parts = sums[8:sums_at].reshape(3, SPECIES, quantum)
    return (
        energies.reshape(1, structures),
        offsets[:SPECIES, 0],
        forces[:3].reshape(3, 1, atoms),
        sums[0, : NMAX * NRAD].reshape(NMAX, NRAD),
        parts[0],
        parts[2].T,
        sums[1, : NMAX * NRAD].reshape(NMAX, NRAD),
        parts[1],
    )


def solution(mesh):
    in_specs = (
        P(None, "grp", "dom"),
        P("grp", "dom"),
        P(None, "grp", "dom"),
        P("grp", "dom"),
        P("grp", "dom"),
        P("grp", None),
        P(),
        P(),
        P(),
        P(),
        P(),
        P(),
        P(),
    )
    out_specs = (P("grp", None), P(), P(None, "grp", "dom"), P(), P(), P(), P(), P())
    return jax.shard_map(
        per_device, mesh=mesh, in_specs=in_specs, out_specs=out_specs, check_vma=False
    )
```

time: 340 us -> 287 us (0.84)
  Pallas kernels: 233 us -> 184 us
  other arithmetic: 6.65 us -> 2.83 us
    pallas_call x2, Pallas kernels: 129 us -> 81.8 us  [backward_call(): pl.pallas_call(partial(backward_kernel, layer), out_shape=(jax.ShapeDtype...]
    pallas_call x1, Pallas kernels: 22.9 us -> 17.8 us  [finish_call(): pl.pallas_call(partial(finish_kernel, rows, sums_at, per_group), out_shap...]
    another operation x1 -> x0, other arithmetic: 3.64 us -> none  [contract_back(): rounded = jnp.stack(partials).astype(bf16)]
    dot_general x3, matrix products: 13.9 us -> 10.4 us  [feature_map(): jnp.einsum('qk,qa->ka', mixing, invariants, precision=highest) * inverse_rms]
    unnamed x63 -> x65, local copies, waits for them, and re-layouts: 12.3 us -> 13.8 us
where the time goes in v1:
time: 287 us; the launch traced here: 285 us
  Pallas kernels  184 us (64%)
  matrix products  75.7 us (26%)
  local copies, waits for them, and re-layouts  21.4 us (7%)
    pallas_call x2, Pallas kernels, backward_call(): pl.pallas_call(partial(backward_kernel, layer), out_shape=(jax.ShapeDtype...  81.8 us
    pallas_call x2, Pallas kernels, density_call(): pl.pallas_call(partial(density_kernel, layer), out_shape=(jax.ShapeDtypeS...  59.4 us
    dot_general x2, matrix products, contract_back(): jnp.einsum('vdq,vqa->da', coupling, rounded, preferred_element_type=f32)  26.9 us
    dot_general x2, matrix products, contract(): jnp.einsum('vdq,da->vqa', coupling, dens_in, preferred_element_type=f32)  24.8 us
    pallas_call x1, Pallas kernels, finish_call(): pl.pallas_call(partial(finish_kernel, rows, sums_at, per_group), out_shap...  17.8 us
    unnamed x65, local copies, waits for them, and re-layouts  13.8 us
    pallas_call x2, Pallas kernels, spread_call(): pl.pallas_call(partial(spread_kernel, values, perm is None), out_shape=ja...  12 us
    dot_general x3, matrix products, feature_map(): jnp.einsum('qk,qa->ka', mixing, invariants, precision=highest) * inverse_rms  10.4 us

profile of v1, /device:TPU:0, one launch (start us, length us, event | category | flops | bytes accessed | tf_op | source)
XLA Modules:
  0.0 285.2 jit_solution(14317118325878691259)
XLA Ops:
  0.6 0.0 copy-start
  0.7 0.7 copy.34
  1.4 0.7 convert_element_type.14
  2.1 0.7 convert_element_type.15
  2.8 0.1 pad.25.clone
  2.8 0.7 maximum_maximum_fusion.site_ref.refs_0_
  3.5 1.6 copy.33
  5.2 6.1 %prepare.1 = (s32[64,1024]{1,0:T(8,128)}, f32[64,1024]{1,0:T(8,128)}, f32[8,1024]{1,0:T(8,128)}, bf16[1024,1024]{1,0:T(8,128)(2,1)}, s32[3,8]{1,0:T(4,128)}) custom-call(s32[1]{0:T(128)} %bitcast.first_ref, s32[1,1024]{1,0:T(1,128)} %cnt_ref.1, s32[48,1024]{1,0:T(8,128)} %bitcast.235, f32[8,1024]{1,0:T(8,128)} %maximum_maximum_fusion.site_ref.refs_0_), custom_call_target="tpu_custom_call" | custom-call | tf_op jit(solution)/shard_map/prepare/pallas_call | solution.py:468
  11.2 5.2 %spread_0.1.tab_ref = f32[96,128]{1,0:T(8,128)} custom-call(f32[8,1024]{1,0:T(8,128)} %maximum_maximum_fusion.site_ref.refs_0_), custom_call_target="tpu_custom_call" | custom-call | tf_op jit(solution)/shard_map/spread_0/pallas_call | solution.py:156
  16.4 0.9 copy-done.2
  17.4 0.9 copy-done.4
  18.3 0.8 copy-done.8
  19.1 0.8 copy-done.10
  19.9 0.7 copy-done.15
  20.6 0.7 copy-done.17
  21.3 29.9 %density_1.1 = (bf16[1960,1024]{1,0:T(8,128)(2,1)S(1)}, f32[320,1024]{1,0:T(8,128)S(1)}) custom-call(s32[3,8]{1,0:T(4,128)S(1)} %copy-done.17, f32[10,12]{1,0:T(8,128)S(1)} %copy-done.15, f32[96,128]{1,0:T(8,128)S(1)} %copy-done.8, f32[8,1024]{1,0:T(8,128)S(1)} %copy-done.10, s32[64,1024]{1,0:T(8,128)S(1)} %copy-done.2, f32[64,1024]{1,0:T(8,128)S(1)} %copy-done.4), custom_call_target="tpu_custom_call" | custom-call | tf_op jit(solution)/shard_map/density_1/pallas_call | solution.py:665
  51.2 11.8 %fusion.18 = f32[4,512,1024]{2,1,0:T(8,128)S(1)} fusion(bf16[4,1960,512]{2,1,0:T(8,128)(2,1)} %param.24, bf16[1960,1024]{1,0:T(8,128)(2,1)S(1)} %get-tuple-element.56), kind=kOutput, calls=%fused_computation.20 | convolution fusion | flops 8220835840 | bytes 20430848 | tf_op jit(solution)/shard_map/vdq,da->vqa/dot_general | solution.py:948
  63.0 3.5 %fusion.29 = (f32[1024]{0:T(1024)S(1)}, f32[1024]{0:T(1024)S(1)}, f32[512,1024]{1,0:T(8,128)S(1)}, f32[1024,512]{0,1:T(8,128)}) fusion(f32[4,512,1024]{2,1,0:T(8,128)S(1)} %fusion.18, f32[4,512]{1,0:T(4,128)S(1)} %copy-done.25, f32[1024]{0:T(1024)S(1)} %bitcast.236), kind=kOutput, calls=%fused_computation.40 | convolution fusion | flops 28837888 | bytes 12603392 | tf_op jit(solution)/shard_map/dot_general | solution.py:1001
  66.5 1.3 copy-done.19
  67.9 0.0 copy-start.14
  67.9 0.0 copy-start.18
  67.9 1.2 broadcast_multiply_fusion
  69.1 0.6 pad.9.refs_0_
  69.7 6.8 %spread_1.1.tab_ref = f32[96,128]{1,0:T(8,128)} custom-call(f32[8,1024]{1,0:T(8,128)} %pad.9.refs_0_, bf16[1024,1024]{1,0:T(8,128)(2,1)} %get-tuple-element.57.refs_1_.perm_ref), custom_call_target="tpu_custom_call" | custom-call | tf_op jit(solution)/shard_map/spread_1/pallas_call | solution.py:156
  76.6 0.8 copy-done.9
  77.3 29.5 %density_2.1 = (bf16[1960,1024]{1,0:T(8,128)(2,1)}, f32[256,1024]{1,0:T(8,128)S(1)}) custom-call(s32[3,8]{1,0:T(4,128)S(1)} %copy-done.18, f32[10,12]{1,0:T(8,128)S(1)} %copy-done.14, f32[96,128]{1,0:T(8,128)S(1)} %copy-done.9, f32[8,1024]{1,0:T(8,128)S(1)} %copy-done.11, s32[64,1024]{1,0:T(8,128)S(1)} %copy-done.3, f32[64,1024]{1,0:T(8,128)S(1)} %copy-done.5, ...), custom_call_target="tpu_custom_call" | custom-call | tf_op jit(solution)/shard_map/density_2/pallas_call | solution.py:665
  106.8 13.0 %fusion.21 = f32[4,512,1024]{2,1,0:T(8,128)S(1)} fusion(bf16[4,1960,512]{2,1,0:T(8,128)(2,1)} %param.28, bf16[1960,1024]{1,0:T(8,128)(2,1)} %get-tuple-element.59), kind=kOutput, calls=%fused_computation.21 | convolution fusion | flops 8220835840 | bytes 20430848 | tf_op jit(solution)/shard_map/vdq,da->vqa/dot_general | solution.py:948
  119.9 4.1 %fusion.28 = (f32[1024]{0:T(1024)S(1)}, f32[512,1024]{1,0:T(8,128)}, bf16[1,512,1024]{2,1,0:T(8,128)(2,1)}, bf16[1,512,1024]{2,1,0:T(8,128)(2,1)}, bf16[1,512,10...) fusion(f32[4,512,1024]{2,1,0:T(8,128)S(1)} %fusion.21, f32[4,512]{1,0:T(4,128)S(1)} %copy-done, f32[1024]{0:T(1024)S(1)} %bitcast.237), kind=kOutput, calls=%fused_computation.38 | convolution fusion | flops 34606080 | bytes 14696448 | tf_op jit(solution)/shard_map/dot_general | solution.py:1008
  124.0 0.8 fusion.30
  124.8 0.1 broadcast_select_fusion
  124.9 14.0 %convolution_bitcast_fusion.1.dd_ref = f32[1960,1024]{1,0:T(8,128)} fusion(bf16[4,1960,512]{2,1,0:T(8,128)(2,1)} %param.28, bf16[1,512,1024]{2,1,0:T(8,128)(2,1)} %get-tuple-element.94, bf16[1,512,1024]{2,1,0:T(8,128)(2,1)} %get-tuple-element.93, bf16[1,512,1024]{2,1,0:T(8,128)(2,1)} %get-tuple-element.95, bf16[1,512,1024]{2,1,0:T(8,128)(2,1)} %get-tuple-element.96), kind=kOutput, calls=%fused_computation.1 | convolution fusion | flops 8227127296 | bytes 20250624 | tf_op jit(solution)/shard_map/vdq,vqa->da/dot_general | solution.py:965
  138.9 49.1 %backward_2.1 = (f32[280,128]{1,0:T(8,128)S(1)}, f32[8,1024]{1,0:T(8,128)S(1)}, f32[960,128]{1,0:T(8,128)S(1)}) custom-call(s32[3,8]{1,0:T(4,128)S(1)} %copy-done.18, f32[10,12]{1,0:T(8,128)S(1)} %copy-done.14, f32[320,1024]{1,0:T(8,128)S(1)} %get-tuple-element.55.refs_0_.geo_ref, f32[256,1024]{1,0:T(8,128)S(1)} %get-tuple-element.58.feat_ref, ...), custom_call_target="tpu_custom_call" | custom-call | tf_op jit(solution)/shard_map/backward_2/pallas_call | solution.py:905
  188.1 0.6 copy-done.6
  188.7 7.1 %collect_2.1 = f32[8,1024]{1,0:T(8,128)} custom-call(f32[7,40,128]{2,1,0:T(8,128)} %bitcast.233, bf16[1024,1024]{1,0:T(8,128)(2,1)} %get-tuple-element.57.refs_1_.perm_ref), custom_call_target="tpu_custom_call" | custom-call | tf_op jit(solution)/shard_map/collect_2/pallas_call | solution.py:197
  195.8 3.6 %convolution_bitcast_fusion.3 = f32[1,4,4,128]{3,2,1,0:T(4,128)S(1)} fusion(f32[512,1024]{1,0:T(8,128)} %copy-done.19, f32[8,1024]{1,0:T(8,128)} %collect_2.1, f32[1024]{0:T(1024)S(1)} %fusion.59), kind=kOutput, calls=%fused_computation.57 | convolution fusion | flops 25169920 | bytes 2125824 | tf_op jit(solution)/shard_map/transpose(jvp(qk,qa->ka))/dot_general | solution.py:944
  199.4 0.0 copy-done.22
  199.5 5.6 %fusion.37 = (bf16[1,512,1024]{2,1,0:T(8,128)(2,1)S(1)}, bf16[1,512,1024]{2,1,0:T(8,128)(2,1)S(1)}, bf16[1,512,1024]{2,1,0:T(8,128)(2,1)S(1)}, bf16[1,512,1024]{2,1,0:T(8,128)(2,1)S(1)}) fusion(f32[4,512,1024]{2,1,0:T(8,128)} %copy-done.21, f32[512,1024]{1,0:T(8,128)S(1)} %copy-done.20, f32[1024]{0:T(1024)S(1)} %multiply_multiply_fusion.2, ...), kind=kOutput, calls=%fused_computation.63 | convolution fusion | flops 34082816 | bytes 16809984 | tf_op jit(solution)/shard_map/transpose(jvp(qk,qa->ka))/dot_general | solution.py:944
  205.1 0.0 copy-start.16
  205.1 12.9 %convolution_bitcast_fusion.dd_ref = f32[1960,1024]{1,0:T(8,128)} fusion(bf16[4,1960,512]{2,1,0:T(8,128)(2,1)} %param.24, bf16[1,512,1024]{2,1,0:T(8,128)(2,1)S(1)} %get-tuple-element.98, bf16[1,512,1024]{2,1,0:T(8,128)(2,1)S(1)} %get-tuple-element.99, bf16[1,512,1024]{2,1,0:T(8,128)(2,1)S(1)} %get-tuple-element.100, ...), kind=kOutput, calls=%fused_computation | convolution fusion | flops 8227127296 | bytes 20250624 | tf_op jit(solution)/shard_map/vdq,vqa->da/dot_general | solution.py:965
  218.0 32.7 %backward_1.1 = (f32[120,128]{1,0:T(8,128)S(1)}, f32[8,1024]{1,0:T(8,128)S(1)}, f32[960,128]{1,0:T(8,128)S(1)}) custom-call(s32[3,8]{1,0:T(4,128)S(1)} %copy-done.18, f32[10,12]{1,0:T(8,128)S(1)} %copy-done.16, f32[320,1024]{1,0:T(8,128)S(1)} %get-tuple-element.55.refs_0_.geo_ref, f32[8,1024]{1,0:T(8,128)S(1)} %broadcast_in_dim.44.own_in_ref.feat_ref, ...), custom_call_target="tpu_custom_call" | custom-call | tf_op jit(solution)/shard_map/backward_1/pallas_call | solution.py:905
  250.7 0.6 copy-done.12
  251.3 0.6 copy-done.13
  252.0 0.2 reduce_sum.74
  252.2 0.1 reduce_sum.75
  252.3 0.1 reduce_sum.76
  252.4 0.2 reduce_sum.77
  252.6 0.1 reduce_sum.78
  252.7 0.1 reduce_sum.79
  252.8 2.6 convolution_bitcast_fusion.5
  255.5 0.0 copy-start.1
  255.5 2.6 convolution_bitcast_fusion.4
  258.2 0.6 copy-done.23
  258.8 17.8 %finish_3.1 = (f32[8,1024]{1,0:T(8,128)}, f32[104,128]{1,0:T(8,128)}, f32[4,128]{1,0:T(4,128)}, f32[8,128]{1,0:T(8,128)}) custom-call(f32[3,40,128]{2,1,0:T(8,128)} %bitcast.234, f32[8,1024]{1,0:T(8,128)} %copy-done.13, bf16[1024,1024]{1,0:T(8,128)(2,1)} %get-tuple-element.57.refs_1_.perm_ref, f32[104,128]{1,0:T(8,128)} %bitcast.242), custom_call_target="tpu_custom_call" | custom-call | tf_op jit(solution)/shard_map/finish_3/pallas_call | solution.py:295
  276.5 0.7 fusion.63
  277.3 0.6 squeeze.78
  277.9 0.6 squeeze.77
  278.5 0.6 squeeze.79
  279.1 0.8 slice_bitcast_fusion.8
  279.9 0.6 copy.24
  280.5 0.8 slice_reduce_fusion.1
  281.2 0.7 reshape_squeeze.6
  281.9 0.7 reshape_squeeze.7
  282.6 1.3 slice_reduce_fusion
  283.9 1.3 copy.41
  (59 shorter events, 0.2 us)
Async XLA Ops:
  0.6 119.2 %copy-start = (f32[4,512]{1,0:T(4,128)S(1)}, f32[4,512]{1,0:T(4,128)}, u32[]{:S(2)}) copy-start(f32[4,512]{1,0:T(4,128)} %param.29) | copy-start | bytes 24580
  16.4 1.0 copy-start.2
  17.4 0.9 copy-start.4
  18.3 0.8 copy-start.8
  19.1 0.8 copy-start.10
  19.9 0.7 copy-start.15
  20.6 0.7 copy-start.17
  51.2 11.8 %copy-start.25 = (f32[4,512]{1,0:T(4,128)S(1)}, f32[4,512]{1,0:T(4,128)}, u32[]{:S(2)}) copy-start(f32[4,512]{1,0:T(4,128)} %param.25) | copy-start | bytes 24580
  63.0 6.1 %copy-start.21 = (f32[4,512,1024]{2,1,0:T(8,128)}, f32[4,512,1024]{2,1,0:T(8,128)S(1)}, u32[]{:S(2)}) copy-start(f32[4,512,1024]{2,1,0:T(8,128)S(1)} %fusion.18) | copy-start | bytes 25165828
  63.0 4.8 %copy-start.24 = (f32[512,4]{0,1:T(4,128)S(1)}, f32[512,4]{0,1:T(4,128)}, u32[]{:S(2)}) copy-start(f32[512,4]{0,1:T(4,128)} %param.26) | copy-start | bytes 24580
  66.5 1.3 copy-start.19
  67.8 8.7 %copy-start.3 = (s32[64,1024]{1,0:T(8,128)S(1)}, s32[64,1024]{1,0:T(8,128)}, u32[]{:S(2)}) copy-start(s32[64,1024]{1,0:T(8,128)} %get-tuple-element.53.idx_ref) | copy-start | bytes 786436
  67.9 8.7 %copy-start.5 = (f32[64,1024]{1,0:T(8,128)S(1)}, f32[64,1024]{1,0:T(8,128)}, u32[]{:S(2)}) copy-start(f32[64,1024]{1,0:T(8,128)} %get-tuple-element.54.wt_ref) | copy-start | bytes 786436
  67.9 8.7 %copy-start.11 = (f32[8,1024]{1,0:T(8,128)S(1)}, f32[8,1024]{1,0:T(8,128)}, u32[]{:S(2)}) copy-start(f32[8,1024]{1,0:T(8,128)} %get-tuple-element.52.cen_ref) | copy-start | bytes 98308
  67.9 8.7 %copy-start.14 = (f32[10,12]{1,0:T(8,128)S(1)}, f32[10,12]{1,0:T(8,128)}, u32[]{:S(2)}) copy-start(f32[10,12]{1,0:T(8,128)} %rad_ref.6) | copy-start | bytes 1444
  67.9 8.7 %copy-start.18 = (s32[3,8]{1,0:T(4,128)S(1)}, s32[3,8]{1,0:T(4,128)}, u32[]{:S(2)}) copy-start(s32[3,8]{1,0:T(4,128)} %get-tuple-element.51.info_ref) | copy-start | bytes 292
  76.5 0.8 copy-start.9
  119.9 4.9 %copy-start.26 = (f32[1,512]{1,0:T(1,128)S(1)}, f32[1,512]{1,0:T(1,128)}, u32[]{:S(2)}) copy-start(f32[1,512]{1,0:T(1,128)} %param.22) | copy-start | bytes 6148
  188.1 0.7 copy-start.6
  195.8 3.6 %copy-start.22 = (f32[8,1024]{1,0:T(8,128)S(1)}, f32[8,1024]{1,0:T(8,128)}, u32[]{:S(2)}) copy-start(f32[8,1024]{1,0:T(8,128)} %collect_2.1) | copy-start | bytes 98308
  195.8 3.6 %copy-start.20 = (f32[512,1024]{1,0:T(8,128)S(1)}, f32[512,1024]{1,0:T(8,128)}, u32[]{:S(2)}) copy-start(f32[512,1024]{1,0:T(8,128)} %copy-done.19) | copy-start | bytes 6291460
  205.1 12.9 %copy-start.7 = (f32[280,128]{1,0:T(8,128)S(1)}, f32[280,128]{1,0:T(8,128)}, u32[]{:S(2)}) copy-start(f32[280,128]{1,0:T(8,128)} %copy-done.6) | copy-start | bytes 430084
  205.1 12.9 %copy-start.16 = (f32[10,12]{1,0:T(8,128)S(1)}, f32[10,12]{1,0:T(8,128)}, u32[]{:S(2)}) copy-start(f32[10,12]{1,0:T(8,128)} %rad_ref.7) | copy-start | bytes 1444
  250.7 0.6 copy-start.12
  251.3 0.6 copy-start.13
  255.5 29.7 %copy-start.1 = (f32[4,512]{1,0:T(4,128)S(1)}, f32[4,512]{1,0:T(4,128)}, u32[]{:S(2)}) copy-start(f32[4,512]{1,0:T(4,128)} %param.29) | copy-start | bytes 24580
  258.2 0.6 copy-start.23

commit v2 on v1

--- a/solution.py
+++ b/solution.py
@@ -1,4 +1,4 @@
-from functools import partial, reduce
+from functools import partial
 import math
 
 import jax
@@ -22,6 +22,8 @@
 WROWS = 12
 WSTEP = 40
 GEO = 5
+QB = 128
+DROWS = 400
 NVAL = 7
 SLOTS = 4
 XROW = CH + 1
@@ -939,30 +941,317 @@
     )(info, radial, geo, feat, index, weight, grad_dens, window_in, own_in)
 
 
-def feature_map(invariants, mixing):
-    inverse_rms = lax.rsqrt(jnp.mean(invariants * invariants, axis=0) + norm_eps)
-    return jnp.einsum("qk,qa->ka", mixing, invariants, precision=highest) * inverse_rms
-
-
-def contract(dens_in, coupling):
-    factors = jnp.einsum("vdq,da->vqa", coupling, dens_in, preferred_element_type=f32)
-    product = reduce(
-        lambda earlier, later: earlier * later,
-        [factors[index_v] for index_v in range(factors.shape[0])],
-    )
-    return (factors, product)
-
-
-def contract_back(factors, upstream, coupling):
-    partials = []
-    for factor_at in range(factors.shape[0]):
-        others = upstream
-        for partner in range(factors.shape[0]):
-            if partner != factor_at:
-                others = others * factors[partner]
-        partials.append(others)
-    rounded = jnp.stack(partials).astype(bf16)
-    return jnp.einsum("vdq,vqa->da", coupling, rounded, preferred_element_type=f32)
+def tn_dot(left, right):
+    return lax.dot_general(left, right, (((0,), (0,)), ((), ())), preferred_element_type=f32)
+
+
+def nt_dot(left, right):
+    return lax.dot_general(left, right, (((1,), (1,)), ((), ())), preferred_element_type=f32)
+
+
+def padded_rows(value):
+    return jnp.concatenate([value, jnp.zeros((8 - value.shape[0], value.shape[1]), f32)], axis=0)
+
+
+def onehot_rows(species):
+    kind = lax.broadcasted_iota(jnp.int32, (8, species.shape[1]), 0).astype(f32)
+    return jnp.where(kind == species, 1.0, 0.0).astype(bf16)
+
+
+def combine(parts):
+    total = parts[2][0:8]
+    total = total + (parts[1][8:16] + parts[0][16:24])
+    total = total + (parts[1][0:8] + parts[0][8:16])
+    return total + parts[0][0:8]
+
+
+def by_atoms(rows24, chunk):
+    wide = nt_dot(rows24, split3(chunk))
+    return [wide[:, j * QB : (j + 1) * QB] for j in range(3)]
+
+
+def contract_one_kernel(dens_ref, coup_ref, coef_ref, mix_ref, site_ref, factor_ref, energy_ref, feat_ref,
+                        aux_ref, grad_ref, b_ref, ch_ref, row_ref):
+    factor_at = pl.program_id(0)
+    quantum, atoms = b_ref.shape
+    half = quantum // 2
+    for part in range(2):
+        rows = slice(part * half, (part + 1) * half)
+        value = tn_dot(coup_ref[0, :, rows], dens_ref[...])
+        factor_ref[0, rows, :] = value
+
+        @pl.when(factor_at == 0)
+        def _(value=value, rows=rows):
+            b_ref[rows, :] = value
+
+        @pl.when(factor_at > 0)
+        def _(value=value, rows=rows):
+            b_ref[rows, :] = b_ref[rows, :] * value
+
+    @pl.when(factor_at == pl.num_programs(0) - 1)
+    def _():
+        onehot = onehot_rows(site_ref[3:4, :])
+        row_ref[0:24, :] = split3(padded_rows(coef_ref[...]))
+        row_ref[24:48, :] = split3(mix_ref[...])
+        triple = jnp.concatenate([onehot] * 3, axis=0)
+
+        def chunk_body(chunk, mixed):
+            cols = pl.ds(pl.multiple_of(chunk * QB, QB), QB)
+            ch_ref[...] = tn_dot(row_ref[0:24, cols], triple)
+            pieces = split3(b_ref[cols, :])
+            left = row_ref[24:48, cols]
+            parts = [
+                jnp.dot(left, pieces[j * QB : (j + 1) * QB], preferred_element_type=f32) for j in range(3)
+            ]
+            wide = nt_dot(onehot, pieces)
+            grad_ref[:, cols] = wide[:, 2 * QB :] + wide[:, QB : 2 * QB] + wide[:, :QB]
+
+            def rows_body(step, sums):
+                at = pl.multiple_of(step * 8, 8)
+                value = b_ref[pl.ds(pl.multiple_of(chunk * QB + step * 8, 8), 8), :]
+                return sums[0] + value * ch_ref[pl.ds(at, 8), :], sums[1] + value * value
+
+            energy, square = lax.fori_loop(0, QB // 8, rows_body, mixed[1:])
+            return mixed[0] + combine(parts), energy, square
+
+        zero = jnp.zeros((8, atoms), f32)
+        mixed, energy, square = lax.fori_loop(0, quantum // QB, chunk_body, (zero, zero, zero))
+        energy_ref[...] = jnp.broadcast_to(jnp.sum(energy, axis=0, keepdims=True), (8, atoms))
+        mean = jnp.sum(square, axis=0, keepdims=True) * (1.0 / quantum)
+        scale = lax.rsqrt(mean + norm_eps)
+        feat_ref[...] = mixed * scale
+        aux_ref[0:8, :] = mixed
+        aux_ref[8:16, :] = jnp.broadcast_to(scale, (8, atoms))
+
+
+def contract_one_call(dens, coupling, coefficient, mixing_rows, ordered):
+    factors, depth, quantum = coupling.shape
+    atoms = dens.shape[1]
+    return pl.pallas_call(
+        contract_one_kernel,
+        out_shape=(
+            jax.ShapeDtypeStruct((factors, quantum, atoms), f32),
+            jax.ShapeDtypeStruct((8, atoms), f32),
+            jax.ShapeDtypeStruct((8, atoms), f32),
+            jax.ShapeDtypeStruct((16, atoms), f32),
+            jax.ShapeDtypeStruct((8, quantum), f32),
+        ),
+        grid=(factors,),
+        in_specs=[
+            whole_spec((depth, atoms)),
+            pl.BlockSpec((1, depth, quantum), lambda v: (v, 0, 0)),
+            whole_spec(coefficient.shape),
+            whole_spec(mixing_rows.shape),
+            whole_spec(ordered.shape),
+        ],
+        out_specs=(
+            pl.BlockSpec((1, quantum, atoms), lambda v: (v, 0, 0)),
+            whole_spec((8, atoms)),
+            whole_spec((8, atoms)),
+            whole_spec((16, atoms)),
+            whole_spec((8, quantum)),
+        ),
+        scratch_shapes=[
+            pltpu.VMEM((quantum, atoms), f32),
+            pltpu.VMEM((QB, atoms), f32),
+            pltpu.VMEM((48, quantum), bf16),
+        ],
+        compiler_params=pltpu.CompilerParams(vmem_limit_bytes=48 << 20),
+        name="contract_1",
+    )(dens, coupling, coefficient, mixing_rows, ordered)
+
+
+def factor_grads(values, upstream):
+    low_pair, high_pair = values[0] * values[1], values[2] * values[3]
+    first, second = upstream * high_pair, upstream * low_pair
+    return first * values[1], first * values[0], second * values[3], second * values[2]
+
+
+def contract_two_kernel(dens_ref, coef_ref, site_ref, coup_ref, out_ref, energy_ref, grad_ref,
+                        cv_ref, f_ref, g_ref, ch_ref, row_ref, sem):
+    step = pl.program_id(0)
+    factors, quantum, atoms = f_ref.shape
+    depth = dens_ref.shape[0]
+    half = quantum // 2
+
+    def load(at):
+        return pltpu.make_async_copy(coup_ref.at[at], cv_ref.at[at, 0:depth], sem.at[at])
+
+    @pl.when(step == 0)
+    def _():
+        for at in range(factors):
+            load(at).start()
+        onehot = onehot_rows(site_ref[3:4, :])
+        row_ref[...] = split3(padded_rows(coef_ref[...]))
+        triple = jnp.concatenate([onehot] * 3, axis=0)
+
+        def factor_body(at, carry):
+            load(at).wait()
+            for part in range(2):
+                rows = slice(part * half, (part + 1) * half)
+                f_ref[at, rows, :] = tn_dot(cv_ref[at, 0:depth, rows], dens_ref[...])
+            return carry
+
+        lax.fori_loop(0, factors, factor_body, 0)
+
+        def chunk_body(chunk, energy):
+            cols = pl.ds(pl.multiple_of(chunk * QB, QB), QB)
+            ch_ref[...] = tn_dot(row_ref[:, cols], triple)
+
+            def rows_body(small, total):
+                at = pl.multiple_of(small * 16, 16)
+                rows = pl.ds(pl.multiple_of(chunk * QB + small * 16, 16), 16)
+                values = [f_ref[v, rows, :] for v in range(factors)]
+                upstream = ch_ref[pl.ds(at, 16), :]
+                grads = factor_grads(values, upstream)
+                for v in range(factors):
+                    g_ref[v, rows, :] = grads[v].astype(bf16)
+                product = values[0] * values[1] * values[2] * values[3]
+                f_ref[0, rows, :] = product
+                term = product * upstream
+                return total + term[:8] + term[8:]
+
+            energy = lax.fori_loop(0, QB // 16, rows_body, energy)
+            wide = nt_dot(onehot, split3(f_ref[0, cols, :]))
+            grad_ref[:, cols] = wide[:, 2 * QB :] + wide[:, QB : 2 * QB] + wide[:, :QB]
+            return energy
+
+        energy = lax.fori_loop(0, quantum // QB, chunk_body, jnp.zeros((8, atoms), f32))
+        energy_ref[...] = jnp.broadcast_to(jnp.sum(energy, axis=0, keepdims=True), (8, atoms))
+
+    rows = pl.ds(pl.multiple_of(step * DROWS, 16), DROWS)
+    total = None
+    for at in range(factors):
+        part = jnp.dot(cv_ref[at, rows, :], g_ref[at], preferred_element_type=f32)
+        total = part if total is None else total + part
+    out_ref[...] = total
+
+
+def contract_two_call(dens, coupling, coefficient, ordered):
+    factors, depth, quantum = coupling.shape
+    atoms = dens.shape[1]
+    steps = pl.cdiv(depth, DROWS)
+    return pl.pallas_call(
+        contract_two_kernel,
+        out_shape=(
+            jax.ShapeDtypeStruct((steps * DROWS, atoms), f32),
+            jax.ShapeDtypeStruct((8, atoms), f32),
+            jax.ShapeDtypeStruct((8, quantum), f32),
+        ),
+        grid=(steps,),
+        in_specs=[
+            pl.BlockSpec((depth, atoms), lambda i: (0, 0), pipeline_mode=pl.Buffered(1)),
+            whole_spec(coefficient.shape),
+            whole_spec(ordered.shape),
+            pl.BlockSpec(memory_space=pl.ANY),
+        ],
+        out_specs=(
+            pl.BlockSpec((DROWS, atoms), lambda i: (i, 0)),
+            whole_spec((8, atoms)),
+            whole_spec((8, quantum)),
+        ),
+        scratch_shapes=[
+            pltpu.VMEM((factors, steps * DROWS, quantum), bf16),
+            pltpu.VMEM((factors, quantum, atoms), f32),
+            pltpu.VMEM((factors, quantum, atoms), bf16),
+            pltpu.VMEM((QB, atoms), f32),
+            pltpu.VMEM((24, quantum), bf16),
+            pltpu.SemaphoreType.DMA((factors,)),
+        ],
+        compiler_params=pltpu.CompilerParams(vmem_limit_bytes=48 << 20),
+        name="contract_2",
+    )(dens, coefficient, ordered, coupling)
+
+
+def contract_back_kernel(coup_ref, coef_ref, mix_ref, site_ref, gfeat_ref, aux_ref, factor_ref, out_ref,
+                         grad_ref, f_ref, g_ref, ch_ref, row_ref, sem):
+    step = pl.program_id(0)
+    factors, quantum, atoms = f_ref.shape
+    chunks = quantum // QB
+
+    def load(chunk):
+        rows = pl.ds(pl.multiple_of(chunk * QB, QB), QB)
+        return pltpu.make_async_copy(factor_ref.at[:, rows, :], f_ref.at[:, rows, :], sem.at[chunk])
+
+    @pl.when(step == 0)
+    def _():
+        for chunk in range(chunks):
+            load(chunk).start()
+        onehot = onehot_rows(site_ref[3:4, :])
+        scale = aux_ref[8:9, :]
+        gfeat = gfeat_ref[...]
+        dot = jnp.sum(aux_ref[0:8, :] * gfeat, axis=0, keepdims=True)
+        shrink = jnp.broadcast_to(scale * scale * scale * dot * (1.0 / quantum), (8, atoms))
+        scaled = split3(scale * gfeat)
+        high, middle, low = scaled[0:8], scaled[8:16], scaled[16:24]
+        mix = split3(mix_ref[...])
+        row_ref[0:24, :] = split3(padded_rows(coef_ref[...]))
+        for at, piece in enumerate((0, 0, 0, 1, 1, 2)):
+            row_ref[24 + 8 * at : 32 + 8 * at, :] = mix[8 * piece : 8 * piece + 8]
+        right = jnp.concatenate([onehot] * 3 + [high, middle, low, high, middle, high], axis=0)
+
+        def chunk_body(chunk, carry):
+            load(chunk).wait()
+            cols = pl.ds(pl.multiple_of(chunk * QB, QB), QB)
+            ch_ref[...] = tn_dot(row_ref[:, cols], right)
+
+            def rows_body(small, inner):
+                at = pl.multiple_of(small * 16, 16)
+                rows = pl.ds(pl.multiple_of(chunk * QB + small * 16, 16), 16)
+                values = [f_ref[v, rows, :] for v in range(factors)]
+                product = values[0] * values[1] * values[2] * values[3]
+                both = jnp.concatenate([shrink, shrink], axis=0)
+                upstream = ch_ref[pl.ds(at, 16), :] - both * product
+                grads = factor_grads(values, upstream)
+                for v in range(factors):
+                    g_ref[v, rows, :] = grads[v].astype(bf16)
+                f_ref[0, rows, :] = product
+                return inner
+
+            lax.fori_loop(0, QB // 16, rows_body, 0)
+            grad_ref[:, cols] = combine(by_atoms(scaled, f_ref[0, cols, :]))
+            return carry
+
+        lax.fori_loop(0, chunks, chunk_body, 0)
+
+    total = None
+    for at in range(factors):
+        part = jnp.dot(coup_ref[at], g_ref[at], preferred_element_type=f32)
+        total = part if total is None else total + part
+    out_ref[...] = total
+
+
+def contract_back_call(coupling, coefficient, mixing_rows, ordered, gfeat, aux, factor):
+    factors, depth, quantum = coupling.shape
+    atoms = ordered.shape[1]
+    rows = depth // 5
+    return pl.pallas_call(
+        contract_back_kernel,
+        out_shape=(
+            jax.ShapeDtypeStruct((depth, atoms), f32),
+            jax.ShapeDtypeStruct((8, quantum), f32),
+        ),
+        grid=(5,),
+        in_specs=[
+            pl.BlockSpec((factors, rows, quantum), lambda i: (0, i, 0)),
+            whole_spec(coefficient.shape),
+            whole_spec(mixing_rows.shape),
+            whole_spec(ordered.shape),
+            whole_spec(gfeat.shape),
+            whole_spec(aux.shape),
+            pl.BlockSpec(memory_space=pl.ANY),
+        ],
+        out_specs=(pl.BlockSpec((rows, atoms), lambda i: (i, 0)), whole_spec((8, quantum))),
+        scratch_shapes=[
+            pltpu.VMEM((factors, quantum, atoms), f32),
+            pltpu.VMEM((factors, quantum, atoms), bf16),
+            pltpu.VMEM((QB, atoms), f32),
+            pltpu.VMEM((72, quantum), bf16),
+            pltpu.SemaphoreType.DMA((quantum // QB,)),
+        ],
+        compiler_params=pltpu.CompilerParams(vmem_limit_bytes=48 << 20),
+        name="contract_back_1",
+    )(coupling, coefficient, mixing_rows, ordered, gfeat, aux, factor)
 
 
 def per_device(
@@ -995,18 +1284,18 @@
     first = ((lax.axis_index("dom") - 1) * atoms).astype(jnp.int32).reshape(1)
     index, weight, ordered, perm, info = prepare_call(first, slot_counts, neighbours[:, 0, :], site)
     onehot = (ordered[3:4] == jnp.arange(SPECIES, dtype=f32)[:, None]).astype(f32)
+    mixing_rows = jnp.pad(mixing.T, ((0, 8 - SPECIES), (0, 0)))
 
     dens_one, geo = density_call(1, info, radial_one, table_one, ordered, index, weight)
-    factors_one, invariants_one = contract(dens_one, coupling_one)
-    chosen_one = jnp.dot(coefficient_one.T, onehot, precision=highest)
-    energy_one = jnp.sum(invariants_one * chosen_one, axis=0)
-    features, features_back = jax.vjp(feature_map, invariants_one, mixing)
-    features8 = jnp.pad(features, ((0, 8 - SPECIES), (0, 0)))
-    table_two = spread_call(1, SPECIES, features8, perm)
+    factors_one, energy_one, features, aux, coefficient_first = contract_one_call(
+        dens_one, coupling_one, coefficient_one, mixing_rows, ordered
+    )
+    table_two = spread_call(1, SPECIES, features, perm)
     dens_two, feat = density_call(2, info, radial_two, table_two, ordered, index, weight, geo)
-    factors_two, invariants_two = contract(dens_two, coupling_two)
-    chosen_two = jnp.dot(coefficient_two.T, onehot, precision=highest)
-    site_energy = energy_one + jnp.sum(invariants_two * chosen_two, axis=0)
+    grad_dens_two, energy_two, coefficient_second = contract_two_call(
+        dens_two, coupling_two, coefficient_two, ordered
+    )
+    site_energy = energy_one[0] + energy_two[0]
     structures = target_energy.shape[1]
     members = (ordered[4][:, None] == jnp.arange(structures, dtype=f32)[None, :]).astype(f32)
     per_structure = jnp.dot(
@@ -1015,22 +1304,18 @@
     target = jnp.where(lax.axis_index("dom") == 0, target_energy, 0.0)
     per_structure = jnp.concatenate([per_structure, target], axis=0)
 
-    grad_dens_two = contract_back(factors_two, chosen_two, coupling_two)
     blank_window = jnp.zeros((8, TILE), f32)
     blank_own = jnp.zeros((8, atoms), f32)
     window_two, own_two, rgr_two = backward_call(
         2, info, radial_two, geo, feat, index, weight, grad_dens_two, blank_window, blank_own
     )
-    grad_features = collect_call(
-        2, tiles, 3, window_two.reshape(NVAL, WSTEP, TILE), perm
-    )[:SPECIES]
-    coefficient_second = jnp.dot(onehot, invariants_two.T, precision=highest)
-    grad_invariants, mixing_gradient = features_back(grad_features)
-    grad_dens_one = contract_back(factors_one, chosen_one + grad_invariants, coupling_one)
+    grad_features = collect_call(2, tiles, 3, window_two.reshape(NVAL, WSTEP, TILE), perm)
+    grad_dens_one, mixing_gradient = contract_back_call(
+        coupling_one, coefficient_one, mixing_rows, ordered, grad_features, aux, factors_one
+    )
     window_one, own_one, rgr_one = backward_call(
         1, info, radial_one, geo, blank_own, index, weight, grad_dens_one, window_two, own_two
     )
-    coefficient_first = jnp.dot(onehot, invariants_one.T, precision=highest)
 
     def radial_sum(partial_grad):
         return jnp.sum(partial_grad.reshape(NMAX * NRAD, 8 * TILE), axis=1)
@@ -1046,9 +1331,9 @@
     payload = jnp.concatenate(
         [
             radials,
-            coefficient_first.reshape(-1),
-            coefficient_second.reshape(-1),
-            mixing_gradient.T.reshape(-1),
+            coefficient_first[:SPECIES].reshape(-1),
+            coefficient_second[:SPECIES].reshape(-1),
+            mixing_gradient[:SPECIES].reshape(-1),
             slots.reshape(-1),
         ]
     )

time: 287 us -> 280 us (0.976)
  matrix products: 75.7 us -> 0.76 us
  Pallas kernels: 184 us -> 246 us
  local copies, waits for them, and re-layouts: 21.4 us -> 28.2 us
    dot_general x11 -> x0, matrix products: 74.9 us -> none  [the longest x2 26.9 us: contract_back(): jnp.einsum('vdq,vqa->da', coupling, rounded, preferred_element_type=f32)]
    pallas_call x0 -> x3, Pallas kernels: none -> 60 us  [the longest x1 25.2 us: contract_two_call(): pl.pallas_call(contract_two_kernel, out_shape=(jax.ShapeDtypeStruct((step...]
    unnamed x65 -> x80, local copies, waits for them, and re-layouts: 13.8 us -> 19.8 us
    pallas_call x1, Pallas kernels: 17.8 us -> 21 us  [finish_call(): pl.pallas_call(partial(finish_kernel, rows, sums_at, per_group), out_shap...]
    pallas_call x2, Pallas kernels: 81.8 us -> 78.6 us  [backward_call(): pl.pallas_call(partial(backward_kernel, layer), out_shape=(jax.ShapeDtype...]
where the time goes in v2:
time: 280 us; the launch traced here: 279 us
  Pallas kernels  246 us (88%)
  local copies, waits for them, and re-layouts  28.2 us (10%)
    pallas_call x2, Pallas kernels, backward_call(): pl.pallas_call(partial(backward_kernel, layer), out_shape=(jax.ShapeDtype...  78.6 us
    pallas_call x2, Pallas kernels, density_call(): pl.pallas_call(partial(density_kernel, layer), out_shape=(jax.ShapeDtypeS...  58.5 us
    pallas_call x1, Pallas kernels, contract_two_call(): pl.pallas_call(contract_two_kernel, out_shape=(jax.ShapeDtypeStruct((step...  25.2 us
    pallas_call x1, Pallas kernels, finish_call(): pl.pallas_call(partial(finish_kernel, rows, sums_at, per_group), out_shap...  21 us
    unnamed x80, local copies, waits for them, and re-layouts  19.8 us
    pallas_call x1, Pallas kernels, contract_back_call(): pl.pallas_call(contract_back_kernel, out_shape=(jax.ShapeDtypeStruct((dep...  17.7 us
    pallas_call x1, Pallas kernels, contract_one_call(): pl.pallas_call(contract_one_kernel, out_shape=(jax.ShapeDtypeStruct((fact...  17.2 us
    pallas_call x2, Pallas kernels, spread_call(): pl.pallas_call(partial(spread_kernel, values, perm is None), out_shape=ja...  12.5 us

profile of v2, /device:TPU:0, one launch (start us, length us, event | category | flops | bytes accessed | tf_op | source)
XLA Modules:
  0.0 278.9 jit_solution(10110996976486609456)
XLA Ops:
  0.6 0.7 copy.31
  1.4 0.7 convert_element_type.12
  2.0 0.7 convert_element_type.13
  2.7 0.1 pad.17.clone
  2.8 0.7 maximum_maximum_fusion.site_ref.refs_0_
  3.5 1.6 copy.30
  5.1 6.0 %prepare.1 = (s32[64,1024]{1,0:T(8,128)}, f32[64,1024]{1,0:T(8,128)}, f32[8,1024]{1,0:T(8,128)}, bf16[1024,1024]{1,0:T(8,128)(2,1)}, s32[3,8]{1,0:T(4,128)}) custom-call(s32[1]{0:T(128)} %bitcast.first_ref, s32[1,1024]{1,0:T(1,128)} %cnt_ref.1, s32[48,1024]{1,0:T(8,128)} %bitcast.28, f32[8,1024]{1,0:T(8,128)} %maximum_maximum_fusion.site_ref.refs_0_), custom_call_target="tpu_custom_call" | custom-call | tf_op jit(solution)/shard_map/prepare/pallas_call | solution.py:470
  11.2 5.2 %spread_0.1.tab_ref = f32[96,128]{1,0:T(8,128)} custom-call(f32[8,1024]{1,0:T(8,128)} %maximum_maximum_fusion.site_ref.refs_0_), custom_call_target="tpu_custom_call" | custom-call | tf_op jit(solution)/shard_map/spread_0/pallas_call | solution.py:158
  16.4 0.0 copy-start
  16.4 0.9 copy-done
  17.3 0.9 copy-done.2
  18.3 0.8 copy-done.5
  19.0 0.8 copy-done.9
  19.8 0.7 copy-done.19
  20.5 0.7 copy-done.21
  21.2 29.5 %density_1.1 = (bf16[1960,1024]{1,0:T(8,128)(2,1)S(1)}, f32[320,1024]{1,0:T(8,128)S(1)}) custom-call(s32[3,8]{1,0:T(4,128)S(1)} %copy-done.21, f32[10,12]{1,0:T(8,128)S(1)} %copy-done.19, f32[96,128]{1,0:T(8,128)S(1)} %copy-done.9, f32[8,1024]{1,0:T(8,128)S(1)} %copy-done.5, s32[64,1024]{1,0:T(8,128)S(1)} %copy-done, f32[64,1024]{1,0:T(8,128)S(1)} %copy-done.2), custom_call_target="tpu_custom_call" | custom-call | tf_op jit(solution)/shard_map/density_1/pallas_call | solution.py:667
  50.7 0.7 pad.9.mix_ref
  51.4 0.7 copy-done.17
  52.1 0.0 copy-start.22
  52.1 17.2 %contract_1.1 = (f32[4,512,1024]{2,1,0:T(8,128)}, f32[8,1024]{1,0:T(8,128)S(1)}, f32[8,1024]{1,0:T(8,128)S(1)}, f32[16,1024]{1,0:T(8,128)S(1)}, f32[8,512]{1,0:T(8,128)S(1)}) custom-call(bf16[1960,1024]{1,0:T(8,128)(2,1)S(1)} %get-tuple-element.66.dens_ref, bf16[4,1960,512]{2,1,0:T(8,128)(2,1)} %coup_ref.5, f32[4,512]{1,0:T(4,128)S(1)} %copy-done.17, ...), custom_call_target="tpu_custom_call" | custom-call | tf_op jit(solution)/shard_map/contract_1/pallas_call | solution.py:1030
  69.3 0.6 copy-done.14
  69.9 0.6 copy-done.26
  70.5 7.3 %spread_1.1.tab_ref = f32[96,128]{1,0:T(8,128)} custom-call(f32[8,1024]{1,0:T(8,128)} %copy-done.14, bf16[1024,1024]{1,0:T(8,128)(2,1)} %get-tuple-element.68.refs_1_.perm_ref), custom_call_target="tpu_custom_call" | custom-call | tf_op jit(solution)/shard_map/spread_1/pallas_call | solution.py:158
  77.8 0.0 copy-done.1
  77.8 0.8 copy-done.10
  78.6 29.0 %density_2.1 = (bf16[1960,1024]{1,0:T(8,128)(2,1)}, f32[256,1024]{1,0:T(8,128)S(1)}) custom-call(s32[3,8]{1,0:T(4,128)S(1)} %copy-done.22, f32[10,12]{1,0:T(8,128)S(1)} %copy-done.15, f32[96,128]{1,0:T(8,128)S(1)} %copy-done.10, f32[8,1024]{1,0:T(8,128)S(1)} %copy-done.6, s32[64,1024]{1,0:T(8,128)S(1)} %copy-done.1, f32[64,1024]{1,0:T(8,128)S(1)} %copy-done.3, ...), custom_call_target="tpu_custom_call" | custom-call | tf_op jit(solution)/shard_map/density_2/pallas_call | solution.py:667
  107.6 2.1 copy-done.4
  109.8 25.2 %contract_2.1 = (f32[2000,1024]{1,0:T(8,128)}, f32[8,1024]{1,0:T(8,128)S(1)}, f32[8,512]{1,0:T(8,128)S(1)}) custom-call(bf16[1960,1024]{1,0:T(8,128)(2,1)S(1)} %copy-done.4, f32[4,512]{1,0:T(4,128)S(1)} %copy-done.25, f32[8,1024]{1,0:T(8,128)S(1)} %copy-done.6, bf16[4,1960,512]{2,1,0:T(8,128)(2,1)} %coup_ref.4), custom_call_target="tpu_custom_call" | custom-call | tf_op jit(solution)/shard_map/contract_2/pallas_call | solution.py:1134
  134.9 0.6 copy-done.28
  135.5 0.8 fusion
  136.4 0.1 broadcast_select_fusion
  136.4 0.6 select_n.19
  137.1 0.7 copy-done.16
  137.8 0.7 copy-done.23
  138.4 47.1 %backward_2.1 = (f32[280,128]{1,0:T(8,128)S(1)}, f32[8,1024]{1,0:T(8,128)S(1)}, f32[960,128]{1,0:T(8,128)S(1)}) custom-call(s32[3,8]{1,0:T(4,128)S(1)} %copy-done.23, f32[10,12]{1,0:T(8,128)S(1)} %copy-done.16, f32[320,1024]{1,0:T(8,128)S(1)} %get-tuple-element.65.refs_0_.geo_ref, f32[256,1024]{1,0:T(8,128)S(1)} %get-tuple-element.69.feat_ref, ...), custom_call_target="tpu_custom_call" | custom-call | tf_op jit(solution)/shard_map/backward_2/pallas_call | solution.py:907
  185.5 0.6 copy-done.7
  186.2 9.5 %collect_2.1.gfeat_ref = f32[8,1024]{1,0:T(8,128)} custom-call(f32[7,40,128]{2,1,0:T(8,128)} %bitcast.26, bf16[1024,1024]{1,0:T(8,128)(2,1)} %get-tuple-element.68.refs_1_.perm_ref), custom_call_target="tpu_custom_call" | custom-call | tf_op jit(solution)/shard_map/collect_2/pallas_call | solution.py:199
  195.7 0.0 copy-start.11
  195.7 0.7 copy-done.11
  196.5 0.7 copy-done.18
  197.2 17.7 %contract_back_1.1 = (f32[1960,1024]{1,0:T(8,128)}, f32[8,512]{1,0:T(8,128)S(1)}) custom-call(bf16[4,1960,512]{2,1,0:T(8,128)(2,1)} %coup_ref.5, f32[4,512]{1,0:T(4,128)S(1)} %copy-done.18, f32[8,512]{1,0:T(8,128)S(1)} %pad.9.mix_ref, f32[8,1024]{1,0:T(8,128)S(1)} %copy-done.6, f32[8,1024]{1,0:T(8,128)S(1)} %copy-done.11, ...), custom_call_target="tpu_custom_call" | custom-call | tf_op jit(solution)/shard_map/contract_back_1/pallas_call | solution.py:1228
  214.9 31.5 %backward_1.1 = (f32[120,128]{1,0:T(8,128)S(1)}, f32[8,1024]{1,0:T(8,128)S(1)}, f32[960,128]{1,0:T(8,128)S(1)}) custom-call(s32[3,8]{1,0:T(4,128)S(1)} %copy-done.24, f32[10,12]{1,0:T(8,128)S(1)} %copy-done.20, f32[320,1024]{1,0:T(8,128)S(1)} %get-tuple-element.65.refs_0_.geo_ref, f32[8,1024]{1,0:T(8,128)S(1)} %broadcast_in_dim.40.own_in_ref.feat_ref, ...), custom_call_target="tpu_custom_call" | custom-call | tf_op jit(solution)/shard_map/backward_1/pallas_call | solution.py:907
  246.5 0.6 copy-done.12
  247.1 0.6 copy-done.13
  247.7 0.2 reduce_sum.23
  247.9 0.1 reduce_sum.24
  248.0 0.1 reduce_sum.25
  248.1 0.2 reduce_sum.29
  248.3 0.1 reduce_sum.36
  248.4 0.1 reduce_sum.37
  248.7 0.0 copy-done.30
  248.7 0.6 copy-done.31
  249.3 21.0 %finish_3.1 = (f32[8,1024]{1,0:T(8,128)}, f32[104,128]{1,0:T(8,128)}, f32[4,128]{1,0:T(4,128)}, f32[8,128]{1,0:T(8,128)}) custom-call(f32[3,40,128]{2,1,0:T(8,128)} %bitcast.27, f32[8,1024]{1,0:T(8,128)} %copy-done.13, bf16[1024,1024]{1,0:T(8,128)(2,1)} %get-tuple-element.68.refs_1_.perm_ref, f32[104,128]{1,0:T(8,128)} %bitcast.30), custom_call_target="tpu_custom_call" | custom-call | tf_op jit(solution)/shard_map/finish_3/pallas_call | solution.py:297
  270.3 0.7 fusion.7
  271.0 0.6 squeeze.24
  271.7 0.6 squeeze.23
  272.3 0.6 squeeze.25
  272.9 0.8 slice_bitcast_fusion
  273.6 0.6 copy.22
  274.2 0.8 slice_reduce_fusion.1
  275.0 0.7 reshape_squeeze.6
  275.7 0.7 reshape_squeeze.7
  276.4 1.3 slice_reduce_fusion
  277.7 1.2 copy.38
  (63 shorter events, 0.2 us)
Async XLA Ops:
  16.4 1.0 copy-start
  17.3 0.9 copy-start.2
  18.3 0.8 copy-start.5
  19.0 0.8 copy-start.9
  19.8 0.7 copy-start.19
  20.5 0.7 copy-start.21
  51.4 0.7 copy-start.17
  52.1 25.7 %copy-start.1 = (s32[64,1024]{1,0:T(8,128)S(1)}, s32[64,1024]{1,0:T(8,128)}, u32[]{:S(2)}) copy-start(s32[64,1024]{1,0:T(8,128)} %get-tuple-element.63.idx_ref) | copy-start | bytes 786436
  52.1 25.7 %copy-start.3 = (f32[64,1024]{1,0:T(8,128)S(1)}, f32[64,1024]{1,0:T(8,128)}, u32[]{:S(2)}) copy-start(f32[64,1024]{1,0:T(8,128)} %get-tuple-element.64.wt_ref) | copy-start | bytes 786436
  52.1 25.7 %copy-start.6 = (f32[8,1024]{1,0:T(8,128)S(1)}, f32[8,1024]{1,0:T(8,128)}, u32[]{:S(2)}) copy-start(f32[8,1024]{1,0:T(8,128)} %get-tuple-element.62.cen_ref.site_ref) | copy-start | bytes 98308
  52.1 25.7 %copy-start.15 = (f32[10,12]{1,0:T(8,128)S(1)}, f32[10,12]{1,0:T(8,128)}, u32[]{:S(2)}) copy-start(f32[10,12]{1,0:T(8,128)} %rad_ref.6) | copy-start | bytes 1444
  52.1 25.7 %copy-start.22 = (s32[3,8]{1,0:T(4,128)S(1)}, s32[3,8]{1,0:T(4,128)}, u32[]{:S(2)}) copy-start(s32[3,8]{1,0:T(4,128)} %get-tuple-element.61.info_ref) | copy-start | bytes 292
  69.3 0.6 copy-start.14
  69.9 0.6 copy-start.26
  70.5 37.1 %copy-start.25 = (f32[4,512]{1,0:T(4,128)S(1)}, f32[4,512]{1,0:T(4,128)}, u32[]{:S(2)}) copy-start(f32[4,512]{1,0:T(4,128)} %coef_ref.4) | copy-start | bytes 24580
  77.8 0.8 copy-start.10
  107.6 2.1 copy-start.4
  109.8 26.6 %copy-start.32 = (f32[1,512]{1,0:T(1,128)S(1)}, f32[1,512]{1,0:T(1,128)}, u32[]{:S(2)}) copy-start(f32[1,512]{1,0:T(1,128)} %param.22) | copy-start | bytes 6148
  134.9 0.6 copy-start.28
  137.1 0.7 copy-start.16
  137.7 0.7 copy-start.23
  185.5 0.7 copy-start.7
  195.7 0.8 copy-start.11
  196.5 0.7 copy-start.18
  197.2 17.7 %copy-start.8 = (f32[280,128]{1,0:T(8,128)S(1)}, f32[280,128]{1,0:T(8,128)}, u32[]{:S(2)}) copy-start(f32[280,128]{1,0:T(8,128)} %copy-done.7) | copy-start | bytes 430084
  197.2 17.7 %copy-start.20 = (f32[10,12]{1,0:T(8,128)S(1)}, f32[10,12]{1,0:T(8,128)}, u32[]{:S(2)}) copy-start(f32[10,12]{1,0:T(8,128)} %rad_ref.7) | copy-start | bytes 1444
  197.2 17.7 %copy-start.24 = (s32[3,8]{1,0:T(4,128)S(1)}, s32[3,8]{1,0:T(4,128)}, u32[]{:S(2)}) copy-start(s32[3,8]{1,0:T(4,128)} %get-tuple-element.61.info_ref) | copy-start | bytes 292
  214.9 33.7 %copy-start.27 = (f32[8,512]{1,0:T(8,128)S(1)}, f32[8,512]{1,0:T(8,128)}, u32[]{:S(2)}) copy-start(f32[8,512]{1,0:T(8,128)} %copy-done.26) | copy-start | bytes 49156
  214.9 33.7 %copy-start.29 = (f32[8,512]{1,0:T(8,128)S(1)}, f32[8,512]{1,0:T(8,128)}, u32[]{:S(2)}) copy-start(f32[8,512]{1,0:T(8,128)} %copy-done.28) | copy-start | bytes 49156
  214.9 33.8 %copy-start.30 = (f32[6144]{0:T(1024)S(1)}, f32[6144]{0:T(1024)}, u32[]{:S(2)}) copy-start(f32[6144]{0:T(1024)} %select_n.19) | copy-start | bytes 73732
  246.5 0.6 copy-start.12
  247.1 0.6 copy-start.13
  248.7 0.6 copy-start.31

commit v3 on v2

--- a/solution.py
+++ b/solution.py
@@ -23,6 +23,7 @@
 WSTEP = 40
 GEO = 5
 QB = 128
+VMEM_ALL = 67043328
 DROWS = 400
 NVAL = 7
 SLOTS = 4
@@ -117,10 +118,17 @@
     return out[:count] + (out[count : 2 * count] + out[2 * count :])
 
 
+def site_rows(pos_ref, kind_ref, part_ref):
+    atoms = kind_ref.shape[1]
+    rows = [pos_ref[axis] for axis in range(3)]
+    rows = rows + [kind_ref[...].astype(f32), part_ref[...].astype(f32)]
+    return jnp.concatenate(rows + [jnp.zeros((3, atoms), f32)], axis=0)
+
+
 def spread_kernel(values, ordered, *refs):
     if ordered:
-        x_ref, out_ref, mine_ref, got_ref, send_sem, recv_sem = refs
-        flat = x_ref[...]
+        pos_ref, kind_ref, part_ref, out_ref, mine_ref, got_ref, send_sem, recv_sem = refs
+        flat = site_rows(pos_ref, kind_ref, part_ref)
     else:
         x_ref, perm_ref, out_ref, mine_ref, got_ref, send_sem, recv_sem = refs
         flat = reorder(x_ref[...], perm_ref, 0)
@@ -145,18 +153,17 @@
 
 
 def comm_params(which):
-    return pltpu.CompilerParams(collective_id=which, has_side_effects=True)
+    return pltpu.CompilerParams(collective_id=which, has_side_effects=True, vmem_limit_bytes=VMEM_ALL)
 
 
 def vmem_spec():
     return pl.BlockSpec(memory_space=pltpu.VMEM)
 
 
-def spread_call(which, values, cells, perm=None):
-    rows = values * cells.shape[1] // TILE
-    operands = (cells,) if perm is None else (cells, perm)
+def spread_call(which, values, raw, operands):
+    rows = values * operands[-1].shape[1] // TILE
     return pl.pallas_call(
-        partial(spread_kernel, values, perm is None),
+        partial(spread_kernel, values, raw),
         out_shape=jax.ShapeDtypeStruct((rows * 3, TILE), f32),
         in_specs=[vmem_spec()] * len(operands),
         out_specs=vmem_spec(),
@@ -211,8 +218,16 @@
     )(window, perm)
 
 
-def finish_kernel(rows, sums_at, per_group, win_ref, own_ref, perm_ref, pay_ref, force_ref, sum_ref, energy_ref,
-                  offset_ref, got_ref, came_ref, send_sem, recv_sem, step_send, step_recv):
+def lane_sums(value):
+    wide = nt_dot(jnp.ones((8, TILE), bf16), split3(value))
+    rows = value.shape[0]
+    total = wide[0:1, 2 * rows :] + wide[0:1, rows : 2 * rows] + wide[0:1, :rows]
+    return jnp.concatenate([total, jnp.zeros((1, TILE - rows), f32)], axis=1)
+
+
+def finish_kernel(rows, win_ref, own_ref, perm_ref, first_ref, second_ref, mix_ref, one_ref, two_ref, part_ref,
+                  target_ref, force_ref, sum_ref, group_ref, got_ref, pay_ref, pay_group_ref, came_ref,
+                  came_group_ref, send_sem, recv_sem, step_send, step_recv, group_send, group_recv):
     pair = SidePair(
         win_ref.at[:, 0:rows], win_ref.at[:, 2 * rows : 3 * rows], got_ref, send_sem, recv_sem
     )
@@ -222,52 +237,111 @@
         for bit in range(log2_of(lax.axis_size(axis))):
             half = 1 << bit
             partners.append({axis: me + half - 2 * half * lax.rem(lax.div(me, half), 2)})
+    width = pay_ref.shape[1]
+    for at, ref in enumerate((first_ref, second_ref, mix_ref)):
+        pay_ref[4 * at : 4 * at + 4, :] = ref[0:4, :]
+    tail = [lane_sums(one_ref[...]), lane_sums(two_ref[...]), jnp.zeros((1, width - 2 * TILE), f32)]
+    pay_ref[12:13, :] = jnp.concatenate(tail, axis=1)
+    pay_ref[13:16, :] = jnp.zeros((3, width), f32)
+    lead = lax.axis_index("dom") == 0
+    mine = lax.axis_index("grp")
+    target = jnp.where(lead, target_ref[...], 0.0)
+    block = part_ref[...]
+    block = jnp.concatenate([block[0:5], target, block[6:8]], axis=0)
+    for group in range(lax.axis_size("grp")):
+        pay_group_ref[8 * group : 8 * group + 8, :] = jnp.where(mine == group, block, 0.0)
     greet(list(pair.partners) + partners, list(pair.flags) + [None] * len(partners))
     pair.start()
     force_ref[...] = reorder(own_ref[...], perm_ref, 0)
     for step, partner in enumerate(partners):
-        source = pay_ref if step == 0 else sum_ref
-        copy = pltpu.make_async_remote_copy(
-            src_ref=source,
-            dst_ref=came_ref.at[step],
-            send_sem=step_send.at[step],
-            recv_sem=step_recv.at[step],
-            device_id=partner,
-            device_id_type=MESH,
-        )
-        copy.start()
-        copy.wait()
-        sum_ref[...] = source[...] + came_ref[step]
+        copies = []
+        for source, total, came, send, recv in (
+            (pay_ref, sum_ref, came_ref, step_send, step_recv),
+            (pay_group_ref, group_ref, came_group_ref, group_send, group_recv),
+        ):
+            now = source if step == 0 else total
+            copy = pltpu.make_async_remote_copy(
+                src_ref=now,
+                dst_ref=came.at[step],
+                send_sem=send.at[step],
+                recv_sem=recv.at[step],
+                device_id=partner,
+                device_id_type=MESH,
+            )
+            copy.start()
+            copies.append((copy, now, total, came))
+        for copy, now, total, came in copies:
+            copy.wait()
+            total[...] = now[...] + came[step]
     pair.wait()
     total = win_ref[:, rows : 2 * rows] + pair.received(0) + pair.received(1)
     force_ref[...] = force_ref[...] - in_lanes(total)
 
-    groups = lax.axis_size("grp")
+
+def finish_call(which, mesh_steps, groups, rows, operands):
+    width, structures = operands[3].shape[1], operands[9].shape[1]
+    return pl.pallas_call(
+        partial(finish_kernel, rows),
+        out_shape=(
+            jax.ShapeDtypeStruct((8, rows * TILE), f32),
+            jax.ShapeDtypeStruct((16, width), f32),
+            jax.ShapeDtypeStruct((8 * groups, structures), f32),
+        ),
+        in_specs=[vmem_spec()] * 10,
+        out_specs=(vmem_spec(),) * 3,
+        scratch_shapes=[
+            pltpu.VMEM((2, 3, rows, TILE), f32),
+            pltpu.VMEM((16, width), f32),
+            pltpu.VMEM((8 * groups, structures), f32),
+            pltpu.VMEM((mesh_steps, 16, width), f32),
+            pltpu.VMEM((mesh_steps, 8 * groups, structures), f32),
+            pltpu.SemaphoreType.DMA((2,)),
+            pltpu.SemaphoreType.DMA((2,)),
+            pltpu.SemaphoreType.DMA((mesh_steps,)),
+            pltpu.SemaphoreType.DMA((mesh_steps,)),
+            pltpu.SemaphoreType.DMA((mesh_steps,)),
+            pltpu.SemaphoreType.DMA((mesh_steps,)),
+        ],
+        compiler_params=comm_params(which),
+        name="finish_%d" % which,
+    )(*operands)
+
+
+def tail_kernel(mine_ref, all_force_ref, sum_ref, group_ref, energy_ref, offset_ref, force_ref, one_ref,
+                first_ref, mix_ref, two_ref, second_ref):
+    groups = group_ref.shape[0] // 8
+
+    def fractions(rows):
+        counts = [rows[1 + c : 2 + c, :] for c in range(SPECIES)]
+        size = jnp.maximum(counts[0] + counts[1] + counts[2] + counts[3], 1.0)
+        return [count / size for count in counts], size
+
     gram = [[None] * SPECIES for _ in range(SPECIES)]
     right = [None] * SPECIES
-
-    def fractions(base):
-        counts = [
-            sum_ref[pl.ds(base + (1 + c) * per_group, per_group), :] for c in range(SPECIES)
-        ]
-        size = jnp.maximum(counts[0] + counts[1] + counts[2] + counts[3], 1.0)
-        return [count / size for count in counts], size
-
-    def gather_sum(total, value):
-        part = jnp.sum(jnp.sum(value, axis=0, keepdims=True), axis=1, keepdims=True)
-        return part if total is None else total + part
-
-    stride = (SPECIES + 2) * per_group
+    energy = None
+    own_frac = [None] * SPECIES
+
+    def plus(total, value):
+        return value if total is None else total + value
+
     for group in range(groups):
-        base = sums_at + group * stride
-        frac, _ = fractions(base)
-        target = sum_ref[pl.ds(base + (1 + SPECIES) * per_group, per_group), :]
+        rows = group_ref[8 * group : 8 * group + 8, :]
+        frac, size = fractions(rows)
+        mine = jnp.where(mine_ref[0] == group, 1.0, 0.0)
+        energy = plus(energy, mine * (rows[0:1] / size))
         for c in range(SPECIES):
-            right[c] = gather_sum(right[c], frac[c] * target)
+            own_frac[c] = plus(own_frac[c], mine * frac[c])
+            right[c] = plus(right[c], frac[c] * rows[5:6])
             for d in range(c, SPECIES):
-                gram[c][d] = gather_sum(gram[c][d], frac[c] * frac[d])
+                gram[c][d] = plus(gram[c][d], frac[c] * frac[d])
+
+    def whole(value):
+        return jnp.sum(value, axis=1, keepdims=True)
+
+    right = [whole(value) for value in right]
+    upper = [[None if value is None else whole(value) for value in row] for row in gram]
     matrix = [
-        [gram[min(c, d)][max(c, d)] + (ridge_weight if c == d else 0.0) for d in range(SPECIES)]
+        [upper[min(c, d)][max(c, d)] + (ridge_weight if c == d else 0.0) for d in range(SPECIES)]
         for c in range(SPECIES)
     ]
     for pivot in range(SPECIES):
@@ -281,40 +355,40 @@
         for later in range(row + 1, SPECIES):
             running = running - matrix[row][later] * answer[later]
         answer[row] = running / matrix[row][row]
-    mine = sums_at + lax.axis_index("grp") * stride
-    frac, size = fractions(mine)
-    energy = sum_ref[pl.ds(mine, per_group), :] / size
     for c in range(SPECIES):
-        energy = energy + frac[c] * answer[c]
+        energy = energy + own_frac[c] * answer[c]
     energy_ref[...] = energy
-    offset_ref[...] = jnp.concatenate(
-        [jnp.broadcast_to(value, (1, TILE)) for value in answer] + [jnp.zeros((4, TILE), f32)], axis=0
-    )
-
-
-def finish_call(which, mesh_steps, rows, sums_at, per_group, window, own, perm, payload):
-    size = payload.shape[0]
+    offset_ref[...] = jnp.concatenate(answer, axis=1)
+    for axis in range(3):
+        force_ref[axis] = all_force_ref[axis : axis + 1, :]
+    first_ref[...] = sum_ref[0:4, :]
+    second_ref[...] = sum_ref[4:8, :]
+    mix_ref[...] = sum_ref[8:12, :]
+    for n in range(NMAX):
+        one_ref[n : n + 1, :] = sum_ref[12:13, n * NRAD : (n + 1) * NRAD]
+        two_ref[n : n + 1, :] = sum_ref[12:13, TILE + n * NRAD : TILE + (n + 1) * NRAD]
+
+
+def tail_call(mine, forces, sums, groups):
+    width, structures, atoms = sums.shape[1], groups.shape[1], forces.shape[1]
+    shapes = (
+        (1, structures),
+        (1, SPECIES),
+        (3, 1, atoms),
+        (NMAX, NRAD),
+        (SPECIES, width),
+        (SPECIES, width),
+        (NMAX, NRAD),
+        (SPECIES, width),
+    )
     return pl.pallas_call(
-        partial(finish_kernel, rows, sums_at, per_group),
-        out_shape=(
-            jax.ShapeDtypeStruct((8, rows * TILE), f32),
-            jax.ShapeDtypeStruct((size, TILE), f32),
-            jax.ShapeDtypeStruct((per_group, TILE), f32),
-            jax.ShapeDtypeStruct((8, TILE), f32),
-        ),
-        in_specs=[vmem_spec()] * 4,
-        out_specs=(vmem_spec(),) * 4,
-        scratch_shapes=[
-            pltpu.VMEM((2, 3, rows, TILE), f32),
-            pltpu.VMEM((mesh_steps, size, TILE), f32),
-            pltpu.SemaphoreType.DMA((2,)),
-            pltpu.SemaphoreType.DMA((2,)),
-            pltpu.SemaphoreType.DMA((mesh_steps,)),
-            pltpu.SemaphoreType.DMA((mesh_steps,)),
-        ],
-        compiler_params=comm_params(which),
-        name="finish_%d" % which,
-    )(window, own, perm, payload)
+        tail_kernel,
+        out_shape=tuple(jax.ShapeDtypeStruct(shape, f32) for shape in shapes),
+        in_specs=[smem_spec()] + [vmem_spec()] * 3,
+        out_specs=(vmem_spec(),) * len(shapes),
+        compiler_params=pltpu.CompilerParams(vmem_limit_bytes=VMEM_ALL),
+        name="tail",
+    )(mine, forces, sums, groups)
 
 
 def double_factorial(number):
@@ -384,9 +458,9 @@
     )
 
 
-def prepare_kernel(first_ref, cnt_ref, nbr_ref, site_ref, idx_ref, wt_ref, sorted_ref, perm_ref, info_ref,
+def prepare_kernel(first_ref, cnt_ref, nbr_ref, spot_ref, kind_ref, part_ref, idx_ref, wt_ref, sorted_ref, perm_ref, info_ref,
                    key_ref, pos_ref, word_ref, rank_ref):
-    atoms = nbr_ref.shape[1]
+    atoms = nbr_ref.shape[2]
     tiles = atoms // TILE
     blocks = NBR // 8
     sub = lax.broadcasted_iota(jnp.int32, (8, TILE), 0)
@@ -396,7 +470,7 @@
         cols = pl.ds(pl.multiple_of(tile * TILE, TILE), TILE)
         limit = cnt_ref[:, cols]
         iota = lax.broadcasted_iota(jnp.int32, (NBR, TILE), 0)
-        key = jnp.where(iota < limit, nbr_ref[:, cols] - first_ref[0], -1 - iota)
+        key = jnp.where(iota < limit, nbr_ref[:, 0, cols] - first_ref[0], -1 - iota)
         key_ref[...] = key
         keys = [key[8 * b : 8 * b + 8] for b in range(blocks)]
         total = [jnp.zeros((8, TILE), jnp.int32) for _ in range(blocks)]
@@ -444,7 +518,7 @@
     for tile in range(tiles):
         line = jnp.broadcast_to(ranks[tile], (atoms, TILE))
         perm_ref[:, tile * TILE : (tile + 1) * TILE] = jnp.where(line == place, 1.0, 0.0).astype(bf16)
-    word_ref[NBR : NBR + 8, :] = site_ref[...]
+    word_ref[NBR : NBR + 8, :] = site_rows(spot_ref, kind_ref, part_ref)
     moved = reorder(word_ref[...], perm_ref, 1)
     sorted_ref[...] = moved[NBR:]
     word = moved[:NBR].astype(jnp.int32)
@@ -465,8 +539,8 @@
         info_ref[2, tile] = high
 
 
-def prepare_call(first, limits, neighbours, site):
-    atoms = neighbours.shape[1]
+def prepare_call(first, limits, neighbours, positions, species, structure):
+    atoms = neighbours.shape[2]
     return pl.pallas_call(
         prepare_kernel,
         out_shape=(
@@ -476,7 +550,7 @@
             jax.ShapeDtypeStruct((atoms, atoms), bf16),
             jax.ShapeDtypeStruct((3, atoms // TILE), jnp.int32),
         ),
-        in_specs=[smem_spec(), vmem_spec(), vmem_spec(), vmem_spec()],
+        in_specs=[smem_spec()] + [vmem_spec()] * 5,
         out_specs=(vmem_spec(), vmem_spec(), vmem_spec(), vmem_spec(), smem_spec()),
         scratch_shapes=[
             pltpu.VMEM((NBR, TILE), jnp.int32),
@@ -484,8 +558,9 @@
             pltpu.VMEM((NBR + 8, atoms), f32),
             pltpu.VMEM((atoms // TILE, TILE), f32),
         ],
+        compiler_params=pltpu.CompilerParams(vmem_limit_bytes=VMEM_ALL),
         name="prepare",
-    )(first, limits, neighbours, site)
+    )(first, limits, neighbours, positions, species, structure)
 
 
 def fetch(tab_ref, values, idx_ref, put_ref, chunk, row_low, row_high):
@@ -686,13 +761,13 @@
             pltpu.VMEM((LM * NPAD, TILE), f32),
             pltpu.VMEM((DENS, TILE), f32),
         ],
-        compiler_params=pltpu.CompilerParams(vmem_limit_bytes=48 << 20),
+        compiler_params=pltpu.CompilerParams(vmem_limit_bytes=VMEM_ALL),
         name="density_%d" % layer,
     )(info, radial, table, centres, index, weight, *extra)
 
 
 def backward_kernel(layer, info_ref, rad_ref, geo_ref, feat_ref, idx_ref, wt_ref, dd_ref, win_in_ref,
-                    own_in_ref, win_ref, own_ref, rgr_ref, x_ref, y_ref, gx_ref, gy_ref, val_ref,
+                    own_in_ref, win_ref, own_ref, rad_out_ref, rgr_ref, x_ref, y_ref, gx_ref, gy_ref, val_ref,
                     left_ref):
     tile = pl.program_id(0)
     count = info_ref[0, tile]
@@ -900,6 +975,11 @@
 
     lax.fori_loop(0, windows, window, 0)
 
+    @pl.when(tile == pl.num_programs(0) - 1)
+    def _():
+        for at in range(NMAX * NRAD):
+            rad_out_ref[at : at + 1, :] = jnp.sum(rgr_ref[8 * at : 8 * at + 8, :], axis=0, keepdims=True)
+
 
 def backward_call(layer, info, radial, geo, feat, index, weight, grad_dens, window_in, own_in):
     atoms = index.shape[1]
@@ -909,7 +989,7 @@
         out_shape=(
             jax.ShapeDtypeStruct((values * WSTEP, TILE), f32),
             jax.ShapeDtypeStruct((8, atoms), f32),
-            jax.ShapeDtypeStruct((NMAX * NRAD * 8, TILE), f32),
+            jax.ShapeDtypeStruct((NMAX * NRAD, TILE), f32),
         ),
         grid=(atoms // TILE,),
         in_specs=[
@@ -926,9 +1006,10 @@
         out_specs=(
             whole_spec((values * WSTEP, TILE)),
             tile_spec(8),
-            whole_spec((NMAX * NRAD * 8, TILE)),
+            whole_spec((NMAX * NRAD, TILE)),
         ),
         scratch_shapes=[
+            pltpu.VMEM((NMAX * NRAD * 8, TILE), f32),
             pltpu.VMEM((CH * 8, TILE), f32),
             pltpu.VMEM((LM * 8, TILE), f32),
             pltpu.VMEM((CH * 8, TILE), f32),
@@ -936,7 +1017,7 @@
             pltpu.VMEM((NVAL * NPAD, TILE), f32),
             pltpu.VMEM((8 * (NVAL * WROWS + 1), TILE), f32),
         ],
-        compiler_params=pltpu.CompilerParams(vmem_limit_bytes=48 << 20),
+        compiler_params=pltpu.CompilerParams(vmem_limit_bytes=VMEM_ALL),
         name="backward_%d" % layer,
     )(info, radial, geo, feat, index, weight, grad_dens, window_in, own_in)
 
@@ -992,7 +1073,7 @@
     def _():
         onehot = onehot_rows(site_ref[3:4, :])
         row_ref[0:24, :] = split3(padded_rows(coef_ref[...]))
-        row_ref[24:48, :] = split3(mix_ref[...])
+        row_ref[24:48, :] = split3(padded_rows(mix_ref[...]))
         triple = jnp.concatenate([onehot] * 3, axis=0)
 
         def chunk_body(chunk, mixed):
@@ -1056,7 +1137,7 @@
             pltpu.VMEM((QB, atoms), f32),
             pltpu.VMEM((48, quantum), bf16),
         ],
-        compiler_params=pltpu.CompilerParams(vmem_limit_bytes=48 << 20),
+        compiler_params=pltpu.CompilerParams(vmem_limit_bytes=VMEM_ALL),
         name="contract_1",
     )(dens, coupling, coefficient, mixing_rows, ordered)
 
@@ -1067,7 +1148,7 @@
     return first * values[1], first * values[0], second * values[3], second * values[2]
 
 
-def contract_two_kernel(dens_ref, coef_ref, site_ref, coup_ref, out_ref, energy_ref, grad_ref,
+def contract_two_kernel(dens_ref, coef_ref, site_ref, before_ref, coup_ref, out_ref, part_ref, grad_ref,
                         cv_ref, f_ref, g_ref, ch_ref, row_ref, sem):
     step = pl.program_id(0)
     factors, quantum, atoms = f_ref.shape
@@ -1117,7 +1198,20 @@
             return energy
 
         energy = lax.fori_loop(0, quantum // QB, chunk_body, jnp.zeros((8, atoms), f32))
-        energy_ref[...] = jnp.broadcast_to(jnp.sum(energy, axis=0, keepdims=True), (8, atoms))
+        energy = jnp.sum(energy, axis=0, keepdims=True) + before_ref[0:1, :]
+        kinds = [jnp.where(site_ref[3:4, :] == float(c), 1.0, 0.0) for c in range(SPECIES)]
+        rows8 = split3(jnp.concatenate([energy] + kinds + [jnp.zeros((3, atoms), f32)], axis=0))
+        owner = site_ref[4:5, :]
+
+        def structure_body(chunk, carry):
+            cols = pl.ds(pl.multiple_of(chunk * TILE, TILE), TILE)
+            ids = lax.broadcasted_iota(jnp.int32, (TILE, atoms), 0) + chunk * TILE
+            members = jnp.where(ids.astype(f32) == owner, 1.0, 0.0).astype(bf16)
+            wide = nt_dot(rows8, members)
+            part_ref[:, cols] = wide[16:24] + wide[8:16] + wide[0:8]
+            return carry
+
+        lax.fori_loop(0, part_ref.shape[1] // TILE, structure_body, 0)
 
     rows = pl.ds(pl.multiple_of(step * DROWS, 16), DROWS)
     total = None
@@ -1127,7 +1221,7 @@
     out_ref[...] = total
 
 
-def contract_two_call(dens, coupling, coefficient, ordered):
+def contract_two_call(dens, coupling, coefficient, ordered, energy_one, structures):
     factors, depth, quantum = coupling.shape
     atoms = dens.shape[1]
     steps = pl.cdiv(depth, DROWS)
@@ -1135,7 +1229,7 @@
         contract_two_kernel,
         out_shape=(
             jax.ShapeDtypeStruct((steps * DROWS, atoms), f32),
-            jax.ShapeDtypeStruct((8, atoms), f32),
+            jax.ShapeDtypeStruct((8, structures), f32),
             jax.ShapeDtypeStruct((8, quantum), f32),
         ),
         grid=(steps,),
@@ -1143,11 +1237,12 @@
             pl.BlockSpec((depth, atoms), lambda i: (0, 0), pipeline_mode=pl.Buffered(1)),
             whole_spec(coefficient.shape),
             whole_spec(ordered.shape),
+            whole_spec(energy_one.shape),
             pl.BlockSpec(memory_space=pl.ANY),
         ],
         out_specs=(
             pl.BlockSpec((DROWS, atoms), lambda i: (i, 0)),
-            whole_spec((8, atoms)),
+            whole_spec((8, structures)),
             whole_spec((8, quantum)),
         ),
         scratch_shapes=[
@@ -1158,9 +1253,9 @@
             pltpu.VMEM((24, quantum), bf16),
             pltpu.SemaphoreType.DMA((factors,)),
         ],
-        compiler_params=pltpu.CompilerParams(vmem_limit_bytes=48 << 20),
+        compiler_params=pltpu.CompilerParams(vmem_limit_bytes=VMEM_ALL),
         name="contract_2",
-    )(dens, coefficient, ordered, coupling)
+    )(dens, coefficient, ordered, energy_one, coupling)
 
 
 def contract_back_kernel(coup_ref, coef_ref, mix_ref, site_ref, gfeat_ref, aux_ref, factor_ref, out_ref,
@@ -1184,7 +1279,7 @@
         shrink = jnp.broadcast_to(scale * scale * scale * dot * (1.0 / quantum), (8, atoms))
         scaled = split3(scale * gfeat)
         high, middle, low = scaled[0:8], scaled[8:16], scaled[16:24]
-        mix = split3(mix_ref[...])
+        mix = split3(padded_rows(mix_ref[...]))
         row_ref[0:24, :] = split3(padded_rows(coef_ref[...]))
         for at, piece in enumerate((0, 0, 0, 1, 1, 2)):
             row_ref[24 + 8 * at : 32 + 8 * at, :] = mix[8 * piece : 8 * piece + 8]
@@ -1249,7 +1344,7 @@
             pltpu.VMEM((72, quantum), bf16),
             pltpu.SemaphoreType.DMA((quantum // QB,)),
         ],
-        compiler_params=pltpu.CompilerParams(vmem_limit_bytes=48 << 20),
+        compiler_params=pltpu.CompilerParams(vmem_limit_bytes=VMEM_ALL),
         name="contract_back_1",
     )(coupling, coefficient, mixing_rows, ordered, gfeat, aux, factor)
 
@@ -1271,96 +1366,58 @@
 ):
     atoms = positions.shape[2]
     tiles = atoms // TILE
-    site = jnp.concatenate(
-        [
-            positions[:, 0, :],
-            species.astype(f32),
-            structure.astype(f32),
-            jnp.zeros((3, atoms), f32),
-        ],
-        axis=0,
-    )
-    table_one = spread_call(0, 4, site)
+    structures = target_energy.shape[1]
+    table_one = spread_call(0, 4, True, (positions, species, structure))
     first = ((lax.axis_index("dom") - 1) * atoms).astype(jnp.int32).reshape(1)
-    index, weight, ordered, perm, info = prepare_call(first, slot_counts, neighbours[:, 0, :], site)
-    onehot = (ordered[3:4] == jnp.arange(SPECIES, dtype=f32)[:, None]).astype(f32)
-    mixing_rows = jnp.pad(mixing.T, ((0, 8 - SPECIES), (0, 0)))
+    index, weight, ordered, perm, info = prepare_call(
+        first, slot_counts, neighbours, positions, species, structure
+    )
+    mixing_rows = mixing.T
 
     dens_one, geo = density_call(1, info, radial_one, table_one, ordered, index, weight)
     factors_one, energy_one, features, aux, coefficient_first = contract_one_call(
         dens_one, coupling_one, coefficient_one, mixing_rows, ordered
     )
-    table_two = spread_call(1, SPECIES, features, perm)
+    table_two = spread_call(1, SPECIES, False, (features, perm))
     dens_two, feat = density_call(2, info, radial_two, table_two, ordered, index, weight, geo)
-    grad_dens_two, energy_two, coefficient_second = contract_two_call(
-        dens_two, coupling_two, coefficient_two, ordered
-    )
-    site_energy = energy_one[0] + energy_two[0]
-    structures = target_energy.shape[1]
-    members = (ordered[4][:, None] == jnp.arange(structures, dtype=f32)[None, :]).astype(f32)
-    per_structure = jnp.dot(
-        jnp.concatenate([site_energy[None, :], onehot], axis=0), members, precision=highest
-    )
-    target = jnp.where(lax.axis_index("dom") == 0, target_energy, 0.0)
-    per_structure = jnp.concatenate([per_structure, target], axis=0)
-
-    blank_window = jnp.zeros((8, TILE), f32)
-    blank_own = jnp.zeros((8, atoms), f32)
-    window_two, own_two, rgr_two = backward_call(
-        2, info, radial_two, geo, feat, index, weight, grad_dens_two, blank_window, blank_own
+    grad_dens_two, per_structure, coefficient_second = contract_two_call(
+        dens_two, coupling_two, coefficient_two, ordered, energy_one, structures
+    )
+    window_two, own_two, radial_second = backward_call(
+        2, info, radial_two, geo, feat, index, weight, grad_dens_two, table_two, ordered
     )
     grad_features = collect_call(2, tiles, 3, window_two.reshape(NVAL, WSTEP, TILE), perm)
     grad_dens_one, mixing_gradient = contract_back_call(
         coupling_one, coefficient_one, mixing_rows, ordered, grad_features, aux, factors_one
     )
-    window_one, own_one, rgr_one = backward_call(
-        1, info, radial_one, geo, blank_own, index, weight, grad_dens_one, window_two, own_two
-    )
-
-    def radial_sum(partial_grad):
-        return jnp.sum(partial_grad.reshape(NMAX * NRAD, 8 * TILE), axis=1)
-
+    window_one, own_one, radial_first = backward_call(
+        1, info, radial_one, geo, ordered, index, weight, grad_dens_one, window_two, own_two
+    )
     groups = lax.axis_size("grp")
-    mine = lax.axis_index("grp") == jnp.arange(groups, dtype=jnp.int32)
-    slots = jnp.where(mine[:, None, None], per_structure[None], 0.0)
-    quantum = coefficient_first.shape[1]
-    wide = SPECIES * quantum
-    radials = jnp.zeros((8 * TILE,), f32)
-    radials = radials.at[: NMAX * NRAD].set(radial_sum(rgr_one))
-    radials = radials.at[TILE : TILE + NMAX * NRAD].set(radial_sum(rgr_two))
-    payload = jnp.concatenate(
-        [
-            radials,
-            coefficient_first[:SPECIES].reshape(-1),
-            coefficient_second[:SPECIES].reshape(-1),
-            mixing_gradient[:SPECIES].reshape(-1),
-            slots.reshape(-1),
-        ]
-    )
-    sums_at = 8 + 3 * wide // TILE
     steps = log2_of(lax.axis_size("dom")) + log2_of(groups)
-    forces, sums, energies, offsets = finish_call(
+    forces, sums, group_sums = finish_call(
         3,
         steps,
+        groups,
         tiles,
-        sums_at,
-        structures // TILE,
-        window_one.reshape(3, WSTEP, TILE),
-        own_one,
-        perm,
-        payload.reshape(-1, TILE),
-    )
-    parts = sums[8:sums_at].reshape(3, SPECIES, quantum)
-    return (
-        energies.reshape(1, structures),
-        offsets[:SPECIES, 0],
-        forces[:3].reshape(3, 1, atoms),
-        sums[0, : NMAX * NRAD].reshape(NMAX, NRAD),
-        parts[0],
-        parts[2].T,
-        sums[1, : NMAX * NRAD].reshape(NMAX, NRAD),
-        parts[1],
-    )
+        (
+            window_one.reshape(3, WSTEP, TILE),
+            own_one,
+            perm,
+            coefficient_first,
+            coefficient_second,
+            mixing_gradient,
+            radial_first,
+            radial_second,
+            per_structure,
+            target_energy,
+        ),
+    )
+    mine = lax.axis_index("grp").astype(jnp.int32).reshape(1)
+    outputs = list(tail_call(mine, forces, sums, group_sums))
+    outputs[1] = outputs[1].reshape(SPECIES)
+    outputs[5] = outputs[5].T
+    return tuple(outputs)
 
 
 def solution(mesh):

time: 280 us -> 256 us (0.914)
  local copies, waits for them, and re-layouts: 28.2 us -> 0 us
  Pallas kernels: 246 us -> 255 us
    unnamed x80 -> x0, local copies, waits for them, and re-layouts: 19.8 us -> none
    pallas_call x1, Pallas kernels: 25.2 us -> 28.3 us  [contract_two_call(): pl.pallas_call(contract_two_kernel, out_shape=(jax.ShapeDtypeStruct((step...]
    slice x4 -> x0, local copies, waits for them, and re-layouts: 2.82 us -> none  [the longest x1 1.31 us: per_device(): offsets[:SPECIES, 0]]
    pallas_call x3 -> x4, Pallas kernels: 33.4 us -> 36.2 us  [the longest x1 22.1 us: finish_call(): pl.pallas_call(partial(finish_kernel, rows), out_shape=(jax.ShapeDtypeStr...]
where the time goes in v3:
time: 256 us
  Pallas kernels  255 us (100%)
    pallas_call x2, Pallas kernels, backward_call(): pl.pallas_call(partial(backward_kernel, layer), out_shape=(jax.ShapeDtype...  80.5 us
    pallas_call x2, Pallas kernels, density_call(): pl.pallas_call(partial(density_kernel, layer), out_shape=(jax.ShapeDtypeS...  58.4 us
    pallas_call x1, Pallas kernels, contract_two_call(): pl.pallas_call(contract_two_kernel, out_shape=(jax.ShapeDtypeStruct((step...  28.3 us
    pallas_call x1, Pallas kernels, finish_call(): pl.pallas_call(partial(finish_kernel, rows), out_shape=(jax.ShapeDtypeStr...  22.1 us
    pallas_call x1, Pallas kernels, contract_one_call(): pl.pallas_call(contract_one_kernel, out_shape=(jax.ShapeDtypeStruct((fact...  18.4 us
    pallas_call x1, Pallas kernels, contract_back_call(): pl.pallas_call(contract_back_kernel, out_shape=(jax.ShapeDtypeStruct((dep...  17.7 us
    pallas_call x2, Pallas kernels, spread_call(): pl.pallas_call(partial(spread_kernel, values, raw), out_shape=jax.ShapeDt...  12.4 us
    pallas_call x1, Pallas kernels, collect_call(): pl.pallas_call(partial(collect_kernel, rows, values_at), out_shape=jax.Sh...  9.52 us

profile of v3, /device:TPU:0, one launch (start us, length us, event | category | flops | bytes accessed | tf_op | source)
XLA Modules:
  0.0 255.9 jit_solution(8093265535067471991)
XLA Ops:
  0.6 5.2 %spread_0.1.tab_ref = f32[96,128]{1,0:T(8,128)} custom-call(f32[3,1,1024]{2,1,0:T(1,128)} %refs_0_.1, s32[1,1024]{1,0:T(1,128)} %refs_1_.1, s32[1,1024]{1,0:T(1,128)} %refs_2_.1), custom_call_target="tpu_custom_call" | custom-call | tf_op jit(solution)/shard_map/spread_0/pallas_call | solution.py:165
  5.8 6.1 %prepare.1 = (s32[64,1024]{1,0:T(8,128)}, f32[64,1024]{1,0:T(8,128)}, f32[8,1024]{1,0:T(8,128)}, bf16[1024,1024]{1,0:T(8,128)(2,1)}, s32[3,8]{1,0:T(4,128)}) custom-call(s32[1]{0:T(128)} %bitcast.1.first_ref, s32[1,1024]{1,0:T(1,128)} %cnt_ref.1, s32[48,1,1024]{2,1,0:T(1,128)} %nbr_ref.1, f32[3,1,1024]{2,1,0:T(1,128)} %refs_0_.1, s32[1,1024]{1,0:T(1,128)} %refs_1_.1, ...), custom_call_target="tpu_custom_call" | custom-call | tf_op jit(solution)/shard_map/prepare/pallas_call | solution.py:544
  12.0 29.4 %density_1.1 = (bf16[1960,1024]{1,0:T(8,128)(2,1)}, f32[320,1024]{1,0:T(8,128)}) custom-call(s32[3,8]{1,0:T(4,128)} %get-tuple-element.44.info_ref, f32[10,12]{1,0:T(8,128)} %rad_ref.7, f32[96,128]{1,0:T(8,128)} %spread_0.1.tab_ref, f32[8,1024]{1,0:T(8,128)} %get-tuple-element.45.cen_ref.site_ref.own_in_ref.feat_ref, s32[64,1024]{1,0:T(8,128)} %get-tuple-element.46.idx_ref, ...), custom_call_target="tpu_custom_call" | custom-call | tf_op jit(solution)/shard_map/density_1/pallas_call | solution.py:742
  41.3 18.4 %contract_1.1 = (f32[4,512,1024]{2,1,0:T(8,128)}, f32[8,1024]{1,0:T(8,128)}, f32[8,1024]{1,0:T(8,128)}, f32[16,1024]{1,0:T(8,128)}, f32[8,512]{1,0:T(8,128)}) custom-call(bf16[1960,1024]{1,0:T(8,128)(2,1)} %get-tuple-element.49.dens_ref, bf16[4,1960,512]{2,1,0:T(8,128)(2,1)} %coup_ref.5, f32[4,512]{1,0:T(4,128)} %coef_ref.5, f32[4,512]{1,0:T(4,128)} %bitcast.9, ...), custom_call_target="tpu_custom_call" | custom-call | tf_op jit(solution)/shard_map/contract_1/pallas_call | solution.py:1111
  59.8 7.2 %spread_1.1.tab_ref.win_in_ref = f32[96,128]{1,0:T(8,128)} custom-call(f32[8,1024]{1,0:T(8,128)} %get-tuple-element.50.refs_0_, bf16[1024,1024]{1,0:T(8,128)(2,1)} %get-tuple-element.51.refs_1_.perm_ref), custom_call_target="tpu_custom_call" | custom-call | tf_op jit(solution)/shard_map/spread_1/pallas_call | solution.py:165
  67.0 29.1 %density_2.1 = (bf16[1960,1024]{1,0:T(8,128)(2,1)}, f32[256,1024]{1,0:T(8,128)}) custom-call(s32[3,8]{1,0:T(4,128)} %get-tuple-element.44.info_ref, f32[10,12]{1,0:T(8,128)} %rad_ref.6, f32[96,128]{1,0:T(8,128)} %spread_1.1.tab_ref.win_in_ref, f32[8,1024]{1,0:T(8,128)} %get-tuple-element.45.cen_ref.site_ref.own_in_ref.feat_ref, ...), custom_call_target="tpu_custom_call" | custom-call | tf_op jit(solution)/shard_map/density_2/pallas_call | solution.py:742
  96.1 28.3 %contract_2.1 = (f32[2000,1024]{1,0:T(8,128)}, f32[8,512]{1,0:T(8,128)}, f32[8,512]{1,0:T(8,128)}) custom-call(bf16[1960,1024]{1,0:T(8,128)(2,1)} %get-tuple-element.53.dens_ref, f32[4,512]{1,0:T(4,128)} %coef_ref.4, f32[8,1024]{1,0:T(8,128)} %get-tuple-element.45.cen_ref.site_ref.own_in_ref.feat_ref, f32[8,1024]{1,0:T(8,128)} %get-tuple-element.54.before_ref, ...), custom_call_target="tpu_custom_call" | custom-call | tf_op jit(solution)/shard_map/contract_2/pallas_call | solution.py:1228
  124.4 48.1 %backward_2.1 = (f32[280,128]{1,0:T(8,128)}, f32[8,1024]{1,0:T(8,128)}, f32[120,128]{1,0:T(8,128)}) custom-call(s32[3,8]{1,0:T(4,128)} %get-tuple-element.44.info_ref, f32[10,12]{1,0:T(8,128)} %rad_ref.6, f32[320,1024]{1,0:T(8,128)} %get-tuple-element.48.refs_0_.geo_ref, f32[256,1024]{1,0:T(8,128)} %get-tuple-element.52.feat_ref, ...), custom_call_target="tpu_custom_call" | custom-call | tf_op jit(solution)/shard_map/backward_2/pallas_call | solution.py:987
  172.5 9.5 %collect_2.1.gfeat_ref = f32[8,1024]{1,0:T(8,128)} custom-call(f32[7,40,128]{2,1,0:T(8,128)} %bitcast.7, bf16[1024,1024]{1,0:T(8,128)(2,1)} %get-tuple-element.51.refs_1_.perm_ref), custom_call_target="tpu_custom_call" | custom-call | tf_op jit(solution)/shard_map/collect_2/pallas_call | solution.py:206
  182.0 17.7 %contract_back_1.1 = (f32[1960,1024]{1,0:T(8,128)}, f32[8,512]{1,0:T(8,128)}) custom-call(bf16[4,1960,512]{2,1,0:T(8,128)(2,1)} %coup_ref.5, f32[4,512]{1,0:T(4,128)} %coef_ref.5, f32[4,512]{1,0:T(4,128)} %bitcast.10, f32[8,1024]{1,0:T(8,128)} %get-tuple-element.45.cen_ref.site_ref.own_in_ref.feat_ref, f32[8,1024]{1,0:T(8,128)} %collect_2.1.gfeat_ref, ...), custom_call_target="tpu_custom_call" | custom-call | tf_op jit(solution)/shard_map/contract_back_1/pallas_call | solution.py:1323
  199.7 32.4 %backward_1.1 = (f32[120,128]{1,0:T(8,128)}, f32[8,1024]{1,0:T(8,128)}, f32[120,128]{1,0:T(8,128)}) custom-call(s32[3,8]{1,0:T(4,128)} %get-tuple-element.44.info_ref, f32[10,12]{1,0:T(8,128)} %rad_ref.7, f32[320,1024]{1,0:T(8,128)} %get-tuple-element.48.refs_0_.geo_ref, f32[8,1024]{1,0:T(8,128)} %get-tuple-element.45.cen_ref.site_ref.own_in_ref.feat_ref, ...), custom_call_target="tpu_custom_call" | custom-call | tf_op jit(solution)/shard_map/backward_1/pallas_call | solution.py:987
  232.1 22.1 %finish_3.1 = (f32[8,1024]{1,0:T(8,128)}, f32[16,512]{1,0:T(8,128)}, f32[16,512]{1,0:T(8,128)}) custom-call(f32[3,40,128]{2,1,0:T(8,128)} %bitcast.8, f32[8,1024]{1,0:T(8,128)} %get-tuple-element.62.own_ref, bf16[1024,1024]{1,0:T(8,128)(2,1)} %get-tuple-element.51.refs_1_.perm_ref, f32[8,512]{1,0:T(8,128)} %get-tuple-element.63.first_ref, ...), custom_call_target="tpu_custom_call" | custom-call | tf_op jit(solution)/shard_map/finish_3/pallas_call | solution.py:283
  254.2 1.7 tail.1

commit v4 on v3

--- a/solution.py
+++ b/solution.py
@@ -23,6 +23,7 @@
 WSTEP = 40
 GEO = 5
 QB = 128
+FROWS = 16
 VMEM_ALL = 67043328
 DROWS = 400
 NVAL = 7
@@ -225,18 +226,35 @@
     return jnp.concatenate([total, jnp.zeros((1, TILE - rows), f32)], axis=1)
 
 
+def exchange_rounds():
+    rounds = []
+    for axis in ("dom", "grp"):
+        me = lax.axis_index(axis)
+        bits = log2_of(lax.axis_size(axis))
+
+        def flip(places):
+            other = me
+            for bit in places:
+                half = 1 << bit
+                other = other + half - 2 * half * lax.rem(lax.div(me, half), 2)
+            return {axis: other}
+
+        for bit in range(0, bits, 2):
+            if bit + 1 < bits:
+                rounds.append([flip((bit,)), flip((bit + 1,)), flip((bit, bit + 1))])
+            else:
+                rounds.append([flip((bit,))])
+    return rounds
+
+
 def finish_kernel(rows, win_ref, own_ref, perm_ref, first_ref, second_ref, mix_ref, one_ref, two_ref, part_ref,
                   target_ref, force_ref, sum_ref, group_ref, got_ref, pay_ref, pay_group_ref, came_ref,
                   came_group_ref, send_sem, recv_sem, step_send, step_recv, group_send, group_recv):
     pair = SidePair(
         win_ref.at[:, 0:rows], win_ref.at[:, 2 * rows : 3 * rows], got_ref, send_sem, recv_sem
     )
-    partners = []
-    for axis in ("dom", "grp"):
-        me = lax.axis_index(axis)
-        for bit in range(log2_of(lax.axis_size(axis))):
-            half = 1 << bit
-            partners.append({axis: me + half - 2 * half * lax.rem(lax.div(me, half), 2)})
+    rounds = exchange_rounds()
+    partners = [partner for group in rounds for partner in group]
     width = pay_ref.shape[1]
     for at, ref in enumerate((first_ref, second_ref, mix_ref)):
         pay_ref[4 * at : 4 * at + 4, :] = ref[0:4, :]
@@ -252,27 +270,37 @@
         pay_group_ref[8 * group : 8 * group + 8, :] = jnp.where(mine == group, block, 0.0)
     greet(list(pair.partners) + partners, list(pair.flags) + [None] * len(partners))
     pair.start()
-    force_ref[...] = reorder(own_ref[...], perm_ref, 0)
-    for step, partner in enumerate(partners):
+    at = 0
+    for turn, group in enumerate(rounds):
         copies = []
-        for source, total, came, send, recv in (
-            (pay_ref, sum_ref, came_ref, step_send, step_recv),
-            (pay_group_ref, group_ref, came_group_ref, group_send, group_recv),
+        for partner in group:
+            for source, total, came, send, recv in (
+                (pay_ref, sum_ref, came_ref, step_send, step_recv),
+                (pay_group_ref, group_ref, came_group_ref, group_send, group_recv),
+            ):
+                copy = pltpu.make_async_remote_copy(
+                    src_ref=source if turn == 0 else total,
+                    dst_ref=came.at[at],
+                    send_sem=send.at[at],
+                    recv_sem=recv.at[at],
+                    device_id=partner,
+                    device_id_type=MESH,
+                )
+                copy.start()
+                copies.append(copy)
+            at = at + 1
+        if turn == 0:
+            force_ref[...] = reorder(own_ref[...], perm_ref, 0)
+        for copy in copies:
+            copy.wait()
+        for source, total, came in (
+            (pay_ref, sum_ref, came_ref),
+            (pay_group_ref, group_ref, came_group_ref),
         ):
-            now = source if step == 0 else total
-            copy = pltpu.make_async_remote_copy(
-                src_ref=now,
-                dst_ref=came.at[step],
-                send_sem=send.at[step],
-                recv_sem=recv.at[step],
-                device_id=partner,
-                device_id_type=MESH,
-            )
-            copy.start()
-            copies.append((copy, now, total, came))
-        for copy, now, total, came in copies:
-            copy.wait()
-            total[...] = now[...] + came[step]
+            value = (source if turn == 0 else total)[...] + came[at - len(group)]
+            if len(group) == 3:
+                value = value + (came[at - 2] + came[at - 1])
+            total[...] = value
     pair.wait()
     total = win_ref[:, rows : 2 * rows] + pair.received(0) + pair.received(1)
     force_ref[...] = force_ref[...] - in_lanes(total)
@@ -563,27 +591,52 @@
     )(first, limits, neighbours, positions, species, structure)
 
 
-def fetch(tab_ref, values, idx_ref, put_ref, chunk, row_low, row_high):
-    start = pl.multiple_of(chunk * 32, 32)
-    index = [idx_ref[pl.ds(start + 8 * kb, 8), :] for kb in range(4)]
-    hi = [lax.shift_right_logical(word, 7) for word in index]
-    lo = [lax.bitwise_and(word, 127) for word in index]
-
-    def body(row, found):
-        found = list(found)
-        hits = [word == row for word in hi]
+def window_starts(row_low, row_high):
+    start = jnp.minimum(row_low, 24 - FROWS)
+    return start, lax.div(row_high - start, FROWS) + 1
+
+
+def load_window(tab_ref, left_ref, values, exact, start):
+    for value in range(values):
+        pieces = split3(tab_ref[pl.ds(value * 24 + start, FROWS), :])
+        for piece in range(3 if exact else 2):
+            at = (piece * values + value) * FROWS
+            left_ref[at : at + FROWS, :] = pieces[piece * FROWS : (piece + 1) * FROWS]
+
+
+def fetch(left_ref, values, exact, idx_ref, put_ref, base, start):
+    index = idx_ref[pl.ds(base, 8), :]
+    hi = lax.shift_right_logical(index, 7) - start
+    lo = lax.bitwise_and(index, 127)
+    sub = lax.broadcasted_iota(jnp.int32, (TILE, TILE), 0)
+    hits = []
+    for part in range(8):
+        line = jnp.broadcast_to(lo[part : part + 1, :], (TILE, TILE))
+        hits.append(jnp.where(line == sub, 1.0, 0.0).astype(bf16))
+    one = jnp.concatenate(hits, axis=1)
+    height = values * FROWS
+    pieces = 3 if exact else 2
+    wide = jnp.dot(left_ref[0 : pieces * height, :], one, preferred_element_type=f32)
+    got = wide[0:height] + wide[height : 2 * height]
+    if exact:
+        got = got + wide[2 * height :]
+    line8 = lax.broadcasted_iota(jnp.int32, (8, TILE), 0)
+    found = [jnp.zeros((8, TILE), f32) for _ in range(values)]
+    for part in range(8):
+        place = jnp.broadcast_to(hi[part : part + 1, :], (8, TILE))
+        masks = [place == line8 + 8 * r for r in range(FROWS // 8)]
         for value in range(values):
-            line = jnp.broadcast_to(tab_ref[pl.ds(value * 24 + row, 1), :], (8, TILE))
-            for kb in range(4):
-                at = value * 4 + kb
-                found[at] = jnp.where(hits[kb], lane_gather(line, lo[kb]), found[at])
-        return tuple(found)
-
-    zero = jnp.zeros((8, TILE), f32)
-    found = lax.fori_loop(row_low, row_high + 1, body, tuple(zero for _ in range(4 * values)))
+            total = None
+            for r, mask in enumerate(masks):
+                at = value * FROWS + 8 * r
+                term = jnp.where(mask, got[at : at + 8, part * TILE : (part + 1) * TILE], 0.0)
+                total = term if total is None else total + term
+            row = jnp.sum(total, axis=0, keepdims=True)
+            found[value] = jnp.where(line8 == part, jnp.broadcast_to(row, (8, TILE)), found[value])
+    inside = (hi >= 0) & (hi < FROWS)
     for value in range(values):
-        for kb in range(4):
-            put_ref[pl.ds(pl.multiple_of(value * NPAD + start + 8 * kb, 8), 8), :] = found[value * 4 + kb]
+        rows = slot_rows(value, base)
+        put_ref[rows, :] = jnp.where(inside, found[value], put_ref[rows, :])
 
 
 def slot_rows(which, base):
@@ -653,21 +706,33 @@
 
 def density_kernel(layer, info_ref, rad_ref, tab_ref, cen_ref, idx_ref, wt_ref, *refs):
     if layer == 1:
-        out_ref, geo_ref, x_ref, y_ref, d_ref = refs
+        out_ref, geo_ref, x_ref, y_ref, d_ref, left_ref = refs
         feat_ref, put_ref = None, geo_ref
     else:
-        geo_ref, out_ref, feat_ref, x_ref, y_ref, d_ref = refs
+        geo_ref, out_ref, feat_ref, x_ref, y_ref, d_ref, left_ref = refs
         put_ref = feat_ref
     tile = pl.program_id(0)
     count = info_ref[0, tile]
     row_low, row_high = info_ref[1, tile], info_ref[2, tile]
     blocks = lax.div(count + 7, 8)
 
-    def gather_chunk(chunk, carry):
-        fetch(tab_ref, 4, idx_ref, put_ref, chunk, row_low, row_high)
-        return carry
-
-    lax.fori_loop(0, lax.div(count + 31, 32), gather_chunk, 0)
+    start, windows = window_starts(row_low, row_high)
+
+    def gather_window(window_at, carry):
+        first_row = jnp.minimum(start + window_at * FROWS, 24 - FROWS)
+
+        @pl.when((tile == 0) | (windows > 1))
+        def _():
+            load_window(tab_ref, left_ref, SPECIES, layer == 1, first_row)
+
+        def gather_block(block_at, inner):
+            base = pl.multiple_of(block_at * 8, 8)
+            fetch(left_ref, SPECIES, layer == 1, idx_ref, put_ref, base, first_row)
+            return inner
+
+        return lax.fori_loop(0, blocks, gather_block, carry)
+
+    lax.fori_loop(0, windows, gather_window, 0)
 
     def edges(block_at, carry):
         base = pl.multiple_of(block_at * 8, 8)
@@ -760,6 +825,7 @@
             pltpu.VMEM((NPAD * XROW + 8, TILE), f32),
             pltpu.VMEM((LM * NPAD, TILE), f32),
             pltpu.VMEM((DENS, TILE), f32),
+            pltpu.VMEM((3 * SPECIES * FROWS, TILE), bf16),
         ],
         compiler_params=pltpu.CompilerParams(vmem_limit_bytes=VMEM_ALL),
         name="density_%d" % layer,
@@ -1394,7 +1460,7 @@
         1, info, radial_one, geo, ordered, index, weight, grad_dens_one, window_two, own_two
     )
     groups = lax.axis_size("grp")
-    steps = log2_of(lax.axis_size("dom")) + log2_of(groups)
+    steps = sum(len(group) for group in exchange_rounds())
     forces, sums, group_sums = finish_call(
         3,
         steps,

time: 256 us -> 251 us (0.980)
  Pallas kernels: 255 us -> 249 us
    pallas_call x1, Pallas kernels: 9.52 us -> 4.24 us  [collect_call(): pl.pallas_call(partial(collect_kernel, rows, values_at), out_shape=jax.Sh...]
    pallas_call x2, Pallas kernels: 80.5 us -> 83.7 us  [backward_call(): pl.pallas_call(partial(backward_kernel, layer), out_shape=(jax.ShapeDtype...]
where the time goes in v4:
time: 251 us; the launch traced here: 250 us
  Pallas kernels  249 us (99%)
    pallas_call x2, Pallas kernels, backward_call(): pl.pallas_call(partial(backward_kernel, layer), out_shape=(jax.ShapeDtype...  83.7 us
    pallas_call x2, Pallas kernels, density_call(): pl.pallas_call(partial(density_kernel, layer), out_shape=(jax.ShapeDtypeS...  56 us
    pallas_call x1, Pallas kernels, contract_two_call(): pl.pallas_call(contract_two_kernel, out_shape=(jax.ShapeDtypeStruct((step...  28.3 us
    pallas_call x1, Pallas kernels, finish_call(): pl.pallas_call(partial(finish_kernel, rows), out_shape=(jax.ShapeDtypeStr...  22.7 us
    pallas_call x1, Pallas kernels, contract_one_call(): pl.pallas_call(contract_one_kernel, out_shape=(jax.ShapeDtypeStruct((fact...  18.4 us
    pallas_call x1, Pallas kernels, contract_back_call(): pl.pallas_call(contract_back_kernel, out_shape=(jax.ShapeDtypeStruct((dep...  17.7 us
    pallas_call x2, Pallas kernels, spread_call(): pl.pallas_call(partial(spread_kernel, values, raw), out_shape=jax.ShapeDt...  10.3 us
    pallas_call x1, Pallas kernels, prepare_call(): pl.pallas_call(prepare_kernel, out_shape=(jax.ShapeDtypeStruct((NPAD, ato...  6.15 us

profile of v4, /device:TPU:0, one launch (start us, length us, event | category | flops | bytes accessed | tf_op | source)
XLA Modules:
  0.0 249.9 jit_solution(18002465380653106928)
XLA Ops:
  0.6 5.2 %spread_0.1.tab_ref = f32[96,128]{1,0:T(8,128)} custom-call(f32[3,1,1024]{2,1,0:T(1,128)} %refs_0_.1, s32[1,1024]{1,0:T(1,128)} %refs_1_.1, s32[1,1024]{1,0:T(1,128)} %refs_2_.1), custom_call_target="tpu_custom_call" | custom-call | tf_op jit(solution)/shard_map/spread_0/pallas_call | solution.py:166
  5.8 6.1 %prepare.1 = (s32[64,1024]{1,0:T(8,128)}, f32[64,1024]{1,0:T(8,128)}, f32[8,1024]{1,0:T(8,128)}, bf16[1024,1024]{1,0:T(8,128)(2,1)}, s32[3,8]{1,0:T(4,128)}) custom-call(s32[1]{0:T(128)} %bitcast.1.first_ref, s32[1,1024]{1,0:T(1,128)} %cnt_ref.1, s32[48,1,1024]{2,1,0:T(1,128)} %nbr_ref.1, f32[3,1,1024]{2,1,0:T(1,128)} %refs_0_.1, s32[1,1024]{1,0:T(1,128)} %refs_1_.1, ...), custom_call_target="tpu_custom_call" | custom-call | tf_op jit(solution)/shard_map/prepare/pallas_call | solution.py:572
  12.0 28.5 %density_1.1 = (bf16[1960,1024]{1,0:T(8,128)(2,1)}, f32[320,1024]{1,0:T(8,128)}) custom-call(s32[3,8]{1,0:T(4,128)} %get-tuple-element.44.info_ref, f32[10,12]{1,0:T(8,128)} %rad_ref.7, f32[96,128]{1,0:T(8,128)} %spread_0.1.tab_ref, f32[8,1024]{1,0:T(8,128)} %get-tuple-element.45.cen_ref.site_ref.own_in_ref.feat_ref, s32[64,1024]{1,0:T(8,128)} %get-tuple-element.46.idx_ref, ...), custom_call_target="tpu_custom_call" | custom-call | tf_op jit(solution)/shard_map/density_1/pallas_call | solution.py:807
  40.5 18.4 %contract_1.1 = (f32[4,512,1024]{2,1,0:T(8,128)}, f32[8,1024]{1,0:T(8,128)}, f32[8,1024]{1,0:T(8,128)}, f32[16,1024]{1,0:T(8,128)}, f32[8,512]{1,0:T(8,128)}) custom-call(bf16[1960,1024]{1,0:T(8,128)(2,1)} %get-tuple-element.49.dens_ref, bf16[4,1960,512]{2,1,0:T(8,128)(2,1)} %coup_ref.5, f32[4,512]{1,0:T(4,128)} %coef_ref.5, f32[4,512]{1,0:T(4,128)} %bitcast.9, ...), custom_call_target="tpu_custom_call" | custom-call | tf_op jit(solution)/shard_map/contract_1/pallas_call | solution.py:1177
  58.9 5.2 %spread_1.1.tab_ref.win_in_ref = f32[96,128]{1,0:T(8,128)} custom-call(f32[8,1024]{1,0:T(8,128)} %get-tuple-element.50.refs_0_, bf16[1024,1024]{1,0:T(8,128)(2,1)} %get-tuple-element.51.refs_1_.perm_ref), custom_call_target="tpu_custom_call" | custom-call | tf_op jit(solution)/shard_map/spread_1/pallas_call | solution.py:166
  64.1 27.4 %density_2.1 = (bf16[1960,1024]{1,0:T(8,128)(2,1)}, f32[256,1024]{1,0:T(8,128)}) custom-call(s32[3,8]{1,0:T(4,128)} %get-tuple-element.44.info_ref, f32[10,12]{1,0:T(8,128)} %rad_ref.6, f32[96,128]{1,0:T(8,128)} %spread_1.1.tab_ref.win_in_ref, f32[8,1024]{1,0:T(8,128)} %get-tuple-element.45.cen_ref.site_ref.own_in_ref.feat_ref, ...), custom_call_target="tpu_custom_call" | custom-call | tf_op jit(solution)/shard_map/density_2/pallas_call | solution.py:807
  91.5 28.3 %contract_2.1 = (f32[2000,1024]{1,0:T(8,128)}, f32[8,512]{1,0:T(8,128)}, f32[8,512]{1,0:T(8,128)}) custom-call(bf16[1960,1024]{1,0:T(8,128)(2,1)} %get-tuple-element.53.dens_ref, f32[4,512]{1,0:T(4,128)} %coef_ref.4, f32[8,1024]{1,0:T(8,128)} %get-tuple-element.45.cen_ref.site_ref.own_in_ref.feat_ref, f32[8,1024]{1,0:T(8,128)} %get-tuple-element.54.before_ref, ...), custom_call_target="tpu_custom_call" | custom-call | tf_op jit(solution)/shard_map/contract_2/pallas_call | solution.py:1294
  119.9 50.0 %backward_2.1 = (f32[280,128]{1,0:T(8,128)}, f32[8,1024]{1,0:T(8,128)}, f32[120,128]{1,0:T(8,128)}) custom-call(s32[3,8]{1,0:T(4,128)} %get-tuple-element.44.info_ref, f32[10,12]{1,0:T(8,128)} %rad_ref.6, f32[320,1024]{1,0:T(8,128)} %get-tuple-element.48.refs_0_.geo_ref, f32[256,1024]{1,0:T(8,128)} %get-tuple-element.52.feat_ref, ...), custom_call_target="tpu_custom_call" | custom-call | tf_op jit(solution)/shard_map/backward_2/pallas_call | solution.py:1053
  169.9 4.2 %collect_2.1.gfeat_ref = f32[8,1024]{1,0:T(8,128)} custom-call(f32[7,40,128]{2,1,0:T(8,128)} %bitcast.7, bf16[1024,1024]{1,0:T(8,128)(2,1)} %get-tuple-element.51.refs_1_.perm_ref), custom_call_target="tpu_custom_call" | custom-call | tf_op jit(solution)/shard_map/collect_2/pallas_call | solution.py:207
  174.1 17.7 %contract_back_1.1 = (f32[1960,1024]{1,0:T(8,128)}, f32[8,512]{1,0:T(8,128)}) custom-call(bf16[4,1960,512]{2,1,0:T(8,128)(2,1)} %coup_ref.5, f32[4,512]{1,0:T(4,128)} %coef_ref.5, f32[4,512]{1,0:T(4,128)} %bitcast.10, f32[8,1024]{1,0:T(8,128)} %get-tuple-element.45.cen_ref.site_ref.own_in_ref.feat_ref, f32[8,1024]{1,0:T(8,128)} %collect_2.1.gfeat_ref, ...), custom_call_target="tpu_custom_call" | custom-call | tf_op jit(solution)/shard_map/contract_back_1/pallas_call | solution.py:1389
  191.8 33.6 %backward_1.1 = (f32[120,128]{1,0:T(8,128)}, f32[8,1024]{1,0:T(8,128)}, f32[120,128]{1,0:T(8,128)}) custom-call(s32[3,8]{1,0:T(4,128)} %get-tuple-element.44.info_ref, f32[10,12]{1,0:T(8,128)} %rad_ref.7, f32[320,1024]{1,0:T(8,128)} %get-tuple-element.48.refs_0_.geo_ref, f32[8,1024]{1,0:T(8,128)} %get-tuple-element.45.cen_ref.site_ref.own_in_ref.feat_ref, ...), custom_call_target="tpu_custom_call" | custom-call | tf_op jit(solution)/shard_map/backward_1/pallas_call | solution.py:1053
  225.5 22.7 %finish_3.1 = (f32[8,1024]{1,0:T(8,128)}, f32[16,512]{1,0:T(8,128)}, f32[16,512]{1,0:T(8,128)}) custom-call(f32[3,40,128]{2,1,0:T(8,128)} %bitcast.8, f32[8,1024]{1,0:T(8,128)} %get-tuple-element.62.own_ref, bf16[1024,1024]{1,0:T(8,128)(2,1)} %get-tuple-element.51.refs_1_.perm_ref, f32[8,512]{1,0:T(8,128)} %get-tuple-element.63.first_ref, ...), custom_call_target="tpu_custom_call" | custom-call | tf_op jit(solution)/shard_map/finish_3/pallas_call | solution.py:311
  248.2 1.7 tail.1

commit v5 on v4

--- a/solution.py
+++ b/solution.py
@@ -126,13 +126,7 @@
     return jnp.concatenate(rows + [jnp.zeros((3, atoms), f32)], axis=0)
 
 
-def spread_kernel(values, ordered, *refs):
-    if ordered:
-        pos_ref, kind_ref, part_ref, out_ref, mine_ref, got_ref, send_sem, recv_sem = refs
-        flat = site_rows(pos_ref, kind_ref, part_ref)
-    else:
-        x_ref, perm_ref, out_ref, mine_ref, got_ref, send_sem, recv_sem = refs
-        flat = reorder(x_ref[...], perm_ref, 0)
+def begin_spread(values, flat, mine_ref, got_ref, send_sem, recv_sem):
     rows = flat.shape[1] // TILE
     for value in range(values):
         for row in range(rows):
@@ -142,6 +136,11 @@
     pair = SidePair(mine_ref, mine_ref, got_ref, send_sem, recv_sem)
     greet(pair.partners, pair.flags)
     pair.start()
+    return pair
+
+
+def end_spread(values, pair, out_ref, mine_ref):
+    rows = mine_ref.shape[0] // values
     for value in range(values):
         at = value * 3 * rows
         out_ref[at + rows : at + 2 * rows, :] = mine_ref[value * rows : (value + 1) * rows, :]
@@ -153,6 +152,12 @@
             out_ref[at : at + rows, :] = block[value * rows : (value + 1) * rows]
 
 
+def spread_kernel(values, x_ref, perm_ref, out_ref, mine_ref, got_ref, send_sem, recv_sem):
+    flat = reorder(x_ref[...], perm_ref, 0)
+    pair = begin_spread(values, flat, mine_ref, got_ref, send_sem, recv_sem)
+    end_spread(values, pair, out_ref, mine_ref)
+
+
 def comm_params(which):
     return pltpu.CompilerParams(collective_id=which, has_side_effects=True, vmem_limit_bytes=VMEM_ALL)
 
@@ -161,10 +166,10 @@
     return pl.BlockSpec(memory_space=pltpu.VMEM)
 
 
-def spread_call(which, values, raw, operands):
+def spread_call(which, values, operands):
     rows = values * operands[-1].shape[1] // TILE
     return pl.pallas_call(
-        partial(spread_kernel, values, raw),
+        partial(spread_kernel, values),
         out_shape=jax.ShapeDtypeStruct((rows * 3, TILE), f32),
         in_specs=[vmem_spec()] * len(operands),
         out_specs=vmem_spec(),
@@ -486,13 +491,16 @@
     )
 
 
-def prepare_kernel(first_ref, cnt_ref, nbr_ref, spot_ref, kind_ref, part_ref, idx_ref, wt_ref, sorted_ref, perm_ref, info_ref,
-                   key_ref, pos_ref, word_ref, rank_ref):
+def prepare_kernel(first_ref, cnt_ref, nbr_ref, spot_ref, kind_ref, part_ref, table_ref, idx_ref, wt_ref,
+                   sorted_ref, perm_ref, info_ref, mine_ref, got_ref, send_sem, recv_sem, key_ref, pos_ref,
+                   word_ref, rank_ref):
     atoms = nbr_ref.shape[2]
     tiles = atoms // TILE
     blocks = NBR // 8
     sub = lax.broadcasted_iota(jnp.int32, (8, TILE), 0)
     lane = lax.broadcasted_iota(jnp.int32, (1, TILE), 1)
+    site = site_rows(spot_ref, kind_ref, part_ref)
+    pair = begin_spread(SPECIES, site, mine_ref, got_ref, send_sem, recv_sem)
 
     def merge(tile, carry):
         cols = pl.ds(pl.multiple_of(tile * TILE, TILE), TILE)
@@ -546,7 +554,7 @@
     for tile in range(tiles):
         line = jnp.broadcast_to(ranks[tile], (atoms, TILE))
         perm_ref[:, tile * TILE : (tile + 1) * TILE] = jnp.where(line == place, 1.0, 0.0).astype(bf16)
-    word_ref[NBR : NBR + 8, :] = site_rows(spot_ref, kind_ref, part_ref)
+    word_ref[NBR : NBR + 8, :] = site
     moved = reorder(word_ref[...], perm_ref, 1)
     sorted_ref[...] = moved[NBR:]
     word = moved[:NBR].astype(jnp.int32)
@@ -565,13 +573,15 @@
         info_ref[0, tile] = lax.div(jnp.max(jnp.where(used, slots, 0)) + SLOTS - 1, SLOTS) * SLOTS
         info_ref[1, tile] = low
         info_ref[2, tile] = high
-
-
-def prepare_call(first, limits, neighbours, positions, species, structure):
+    end_spread(SPECIES, pair, table_ref, mine_ref)
+
+
+def prepare_call(which, first, limits, neighbours, positions, species, structure):
     atoms = neighbours.shape[2]
     return pl.pallas_call(
         prepare_kernel,
         out_shape=(
+            jax.ShapeDtypeStruct((SPECIES * 3 * atoms // TILE, TILE), f32),
             jax.ShapeDtypeStruct((NPAD, atoms), jnp.int32),
             jax.ShapeDtypeStruct((NPAD, atoms), f32),
             jax.ShapeDtypeStruct((8, atoms), f32),
@@ -579,14 +589,18 @@
             jax.ShapeDtypeStruct((3, atoms // TILE), jnp.int32),
         ),
         in_specs=[smem_spec()] + [vmem_spec()] * 5,
-        out_specs=(vmem_spec(), vmem_spec(), vmem_spec(), vmem_spec(), smem_spec()),
+        out_specs=(vmem_spec(),) * 5 + (smem_spec(),),
         scratch_shapes=[
+            pltpu.VMEM((SPECIES * atoms // TILE, TILE), f32),
+            pltpu.VMEM((2, SPECIES * atoms // TILE, TILE), f32),
+            pltpu.SemaphoreType.DMA((2,)),
+            pltpu.SemaphoreType.DMA((2,)),
             pltpu.VMEM((NBR, TILE), jnp.int32),
             pltpu.VMEM((NBR, TILE), jnp.int32),
             pltpu.VMEM((NBR + 8, atoms), f32),
             pltpu.VMEM((atoms // TILE, TILE), f32),
         ],
-        compiler_params=pltpu.CompilerParams(vmem_limit_bytes=VMEM_ALL),
+        compiler_params=comm_params(which),
         name="prepare",
     )(first, limits, neighbours, positions, species, structure)
 
@@ -857,12 +871,14 @@
             acc = list(acc)
             for part in range(LBLK):
                 lm = step * LBLK + part
-                col = y_ref[pl.ds(pl.multiple_of(lm * 8, 8), 8), :]
+                col = y_ref[pl.ds(lm * 8, 8), :]
                 for m in range(CH):
                     acc[m] = acc[m] + line_of(m * LM + lm) * col
             return tuple(acc)
 
-        acc = lax.fori_loop(0, LM // LBLK, over_lm, tuple(zero for _ in range(CH)))
+        acc = tuple(zero for _ in range(CH))
+        for step in range(LM // LBLK):
+            acc = over_lm(step, acc)
         for m in range(CH):
             gx_ref[8 * m : 8 * m + 8, :] = acc[m]
 
@@ -870,12 +886,14 @@
             acc = list(acc)
             for part in range(4):
                 m = step * 4 + part
-                col = x_ref[pl.ds(pl.multiple_of(m * 8, 8), 8), :]
+                col = x_ref[pl.ds(m * 8, 8), :]
                 for lm in range(LM):
                     acc[lm] = acc[lm] + line_of(m * LM + lm) * col
             return tuple(acc)
 
-        acc = lax.fori_loop(0, CH // 4, over_m, tuple(zero for _ in range(LM)))
+        acc = tuple(zero for _ in range(LM))
+        for step in range(CH // 4):
+            acc = over_m(step, acc)
         for lm in range(LM):
             gy_ref[8 * lm : 8 * lm + 8, :] = acc[lm]
 
@@ -887,7 +905,7 @@
             acc = list(acc)
             for part in range(2):
                 n = step * 2 + part
-                at = pl.multiple_of(n * 8, 8)
+                at = n * 8
                 scaled = x_ref[pl.ds(at, 8), :]
                 sums = [None, None]
                 for lm in range(LM):
@@ -901,7 +919,9 @@
                 gx_ref[pl.ds(at, 8), :] = sums[0] + sums[1]
             return tuple(acc)
 
-        acc = lax.fori_loop(0, NMAX // 2, over_n, tuple(zero for _ in range(LM)))
+        acc = tuple(zero for _ in range(LM))
+        for step in range(NMAX // 2):
+            acc = over_n(step, acc)
         for lm in range(LM):
             gy_ref[8 * lm : 8 * lm + 8, :] = acc[lm]
 
@@ -1433,10 +1453,9 @@
     atoms = positions.shape[2]
     tiles = atoms // TILE
     structures = target_energy.shape[1]
-    table_one = spread_call(0, 4, True, (positions, species, structure))
     first = ((lax.axis_index("dom") - 1) * atoms).astype(jnp.int32).reshape(1)
-    index, weight, ordered, perm, info = prepare_call(
-        first, slot_counts, neighbours, positions, species, structure
+    table_one, index, weight, ordered, perm, info = prepare_call(
+        0, first, slot_counts, neighbours, positions, species, structure
     )
     mixing_rows = mixing.T
 
@@ -1444,7 +1463,7 @@
     factors_one, energy_one, features, aux, coefficient_first = contract_one_call(
         dens_one, coupling_one, coefficient_one, mixing_rows, ordered
     )
-    table_two = spread_call(1, SPECIES, False, (features, perm))
+    table_two = spread_call(1, SPECIES, (features, perm))
     dens_two, feat = density_call(2, info, radial_two, table_two, ordered, index, weight, geo)
     grad_dens_two, per_structure, coefficient_second = contract_two_call(
         dens_two, coupling_two, coefficient_two, ordered, energy_one, structures

time: 251 us -> 246 us (0.980)
  Pallas kernels: 249 us -> 244 us
    pallas_call x2, Pallas kernels: 83.7 us -> 78.4 us  [backward_call(): pl.pallas_call(partial(backward_kernel, layer), out_shape=(jax.ShapeDtype...]
    pallas_call x1, Pallas kernels: 4.24 us -> 8.85 us  [collect_call(): pl.pallas_call(partial(collect_kernel, rows, values_at), out_shape=jax.Sh...]
    pallas_call x3 -> x2, Pallas kernels: 16.5 us -> 13.9 us  [the longest x1 7.16 us: prepare_call(): pl.pallas_call(prepare_kernel, out_shape=(jax.ShapeDtypeStruct((SPECIES *...]
where the time goes in v5:
time: 246 us; the launch traced here: 245 us
  Pallas kernels  244 us (99%)
    pallas_call x2, Pallas kernels, backward_call(): pl.pallas_call(partial(backward_kernel, layer), out_shape=(jax.ShapeDtype...  78.4 us
    pallas_call x2, Pallas kernels, density_call(): pl.pallas_call(partial(density_kernel, layer), out_shape=(jax.ShapeDtypeS...  54.5 us
    pallas_call x1, Pallas kernels, contract_two_call(): pl.pallas_call(contract_two_kernel, out_shape=(jax.ShapeDtypeStruct((step...  28.3 us
    pallas_call x1, Pallas kernels, finish_call(): pl.pallas_call(partial(finish_kernel, rows), out_shape=(jax.ShapeDtypeStr...  22.1 us
    pallas_call x1, Pallas kernels, contract_one_call(): pl.pallas_call(contract_one_kernel, out_shape=(jax.ShapeDtypeStruct((fact...  18.4 us
    pallas_call x1, Pallas kernels, contract_back_call(): pl.pallas_call(contract_back_kernel, out_shape=(jax.ShapeDtypeStruct((dep...  17.7 us
    pallas_call x1, Pallas kernels, collect_call(): pl.pallas_call(partial(collect_kernel, rows, values_at), out_shape=jax.Sh...  8.85 us
    pallas_call x1, Pallas kernels, prepare_call(): pl.pallas_call(prepare_kernel, out_shape=(jax.ShapeDtypeStruct((SPECIES *...  7.16 us

profile of v5, /device:TPU:0, one launch (start us, length us, event | category | flops | bytes accessed | tf_op | source)
XLA Modules:
  0.0 244.6 jit_solution(14838316437750209649)
XLA Ops:
  0.6 7.2 %prepare.1 = (f32[96,128]{1,0:T(8,128)}, s32[64,1024]{1,0:T(8,128)}, f32[64,1024]{1,0:T(8,128)}, f32[8,1024]{1,0:T(8,128)}, bf16[1024,1024]{1,0:T(8,128)(2,1)}, /*index=5*/s32[3,8]{1,0:T(4,128)}) custom-call(s32[1]{0:T(128)} %bitcast.1.first_ref, s32[1,1024]{1,0:T(1,128)} %cnt_ref.1, s32[48,1,1024]{2,1,0:T(1,128)} %nbr_ref.1, f32[3,1,1024]{2,1,0:T(1,128)} %spot_ref.1, ...), custom_call_target="tpu_custom_call" | custom-call | tf_op jit(solution)/shard_map/prepare/pallas_call | solution.py:581
  7.8 27.8 %density_1.1 = (bf16[1960,1024]{1,0:T(8,128)(2,1)}, f32[320,1024]{1,0:T(8,128)}) custom-call(s32[3,8]{1,0:T(4,128)} %get-tuple-element.45.info_ref, f32[10,12]{1,0:T(8,128)} %rad_ref.7, f32[96,128]{1,0:T(8,128)} %get-tuple-element.46.tab_ref, f32[8,1024]{1,0:T(8,128)} %get-tuple-element.47.cen_ref.site_ref.own_in_ref.feat_ref, ...), custom_call_target="tpu_custom_call" | custom-call | tf_op jit(solution)/shard_map/density_1/pallas_call | solution.py:821
  35.6 18.4 %contract_1.1 = (f32[4,512,1024]{2,1,0:T(8,128)}, f32[8,1024]{1,0:T(8,128)}, f32[8,1024]{1,0:T(8,128)}, f32[16,1024]{1,0:T(8,128)}, f32[8,512]{1,0:T(8,128)}) custom-call(bf16[1960,1024]{1,0:T(8,128)(2,1)} %get-tuple-element.51.dens_ref, bf16[4,1960,512]{2,1,0:T(8,128)(2,1)} %coup_ref.5, f32[4,512]{1,0:T(4,128)} %coef_ref.5, f32[4,512]{1,0:T(4,128)} %bitcast.9, ...), custom_call_target="tpu_custom_call" | custom-call | tf_op jit(solution)/shard_map/contract_1/pallas_call | solution.py:1197
  54.0 6.8 %spread_1.1.tab_ref.win_in_ref = f32[96,128]{1,0:T(8,128)} custom-call(f32[8,1024]{1,0:T(8,128)} %get-tuple-element.52.x_ref, bf16[1024,1024]{1,0:T(8,128)(2,1)} %get-tuple-element.53.perm_ref), custom_call_target="tpu_custom_call" | custom-call | tf_op jit(solution)/shard_map/spread_1/pallas_call | solution.py:171
  60.8 26.7 %density_2.1 = (bf16[1960,1024]{1,0:T(8,128)(2,1)}, f32[256,1024]{1,0:T(8,128)}) custom-call(s32[3,8]{1,0:T(4,128)} %get-tuple-element.45.info_ref, f32[10,12]{1,0:T(8,128)} %rad_ref.6, f32[96,128]{1,0:T(8,128)} %spread_1.1.tab_ref.win_in_ref, f32[8,1024]{1,0:T(8,128)} %get-tuple-element.47.cen_ref.site_ref.own_in_ref.feat_ref, ...), custom_call_target="tpu_custom_call" | custom-call | tf_op jit(solution)/shard_map/density_2/pallas_call | solution.py:821
  87.6 28.3 %contract_2.1 = (f32[2000,1024]{1,0:T(8,128)}, f32[8,512]{1,0:T(8,128)}, f32[8,512]{1,0:T(8,128)}) custom-call(bf16[1960,1024]{1,0:T(8,128)(2,1)} %get-tuple-element.55.dens_ref, f32[4,512]{1,0:T(4,128)} %coef_ref.4, f32[8,1024]{1,0:T(8,128)} %get-tuple-element.47.cen_ref.site_ref.own_in_ref.feat_ref, f32[8,1024]{1,0:T(8,128)} %get-tuple-element.56.before_ref, ...), custom_call_target="tpu_custom_call" | custom-call | tf_op jit(solution)/shard_map/contract_2/pallas_call | solution.py:1314
  115.9 47.4 %backward_2.1 = (f32[280,128]{1,0:T(8,128)}, f32[8,1024]{1,0:T(8,128)}, f32[120,128]{1,0:T(8,128)}) custom-call(s32[3,8]{1,0:T(4,128)} %get-tuple-element.45.info_ref, f32[10,12]{1,0:T(8,128)} %rad_ref.6, f32[320,1024]{1,0:T(8,128)} %get-tuple-element.50.refs_0_.geo_ref, f32[256,1024]{1,0:T(8,128)} %get-tuple-element.54.feat_ref, ...), custom_call_target="tpu_custom_call" | custom-call | tf_op jit(solution)/shard_map/backward_2/pallas_call | solution.py:1073
  163.2 8.8 %collect_2.1.gfeat_ref = f32[8,1024]{1,0:T(8,128)} custom-call(f32[7,40,128]{2,1,0:T(8,128)} %bitcast.7, bf16[1024,1024]{1,0:T(8,128)(2,1)} %get-tuple-element.53.perm_ref), custom_call_target="tpu_custom_call" | custom-call | tf_op jit(solution)/shard_map/collect_2/pallas_call | solution.py:212
  172.1 17.7 %contract_back_1.1 = (f32[1960,1024]{1,0:T(8,128)}, f32[8,512]{1,0:T(8,128)}) custom-call(bf16[4,1960,512]{2,1,0:T(8,128)(2,1)} %coup_ref.5, f32[4,512]{1,0:T(4,128)} %coef_ref.5, f32[4,512]{1,0:T(4,128)} %bitcast.10, f32[8,1024]{1,0:T(8,128)} %get-tuple-element.47.cen_ref.site_ref.own_in_ref.feat_ref, f32[8,1024]{1,0:T(8,128)} %collect_2.1.gfeat_ref, ...), custom_call_target="tpu_custom_call" | custom-call | tf_op jit(solution)/shard_map/contract_back_1/pallas_call | solution.py:1409
  189.8 31.0 %backward_1.1 = (f32[120,128]{1,0:T(8,128)}, f32[8,1024]{1,0:T(8,128)}, f32[120,128]{1,0:T(8,128)}) custom-call(s32[3,8]{1,0:T(4,128)} %get-tuple-element.45.info_ref, f32[10,12]{1,0:T(8,128)} %rad_ref.7, f32[320,1024]{1,0:T(8,128)} %get-tuple-element.50.refs_0_.geo_ref, f32[8,1024]{1,0:T(8,128)} %get-tuple-element.47.cen_ref.site_ref.own_in_ref.feat_ref, ...), custom_call_target="tpu_custom_call" | custom-call | tf_op jit(solution)/shard_map/backward_1/pallas_call | solution.py:1073
  220.8 22.1 %finish_3.1 = (f32[8,1024]{1,0:T(8,128)}, f32[16,512]{1,0:T(8,128)}, f32[16,512]{1,0:T(8,128)}) custom-call(f32[3,40,128]{2,1,0:T(8,128)} %bitcast.8, f32[8,1024]{1,0:T(8,128)} %get-tuple-element.64.own_ref, bf16[1024,1024]{1,0:T(8,128)(2,1)} %get-tuple-element.53.perm_ref, f32[8,512]{1,0:T(8,128)} %get-tuple-element.65.first_ref, ...), custom_call_target="tpu_custom_call" | custom-call | tf_op jit(solution)/shard_map/finish_3/pallas_call | solution.py:316
  243.0 1.7 tail.1

commit v6 on v5

--- a/solution.py
+++ b/solution.py
@@ -190,38 +190,6 @@
         jnp.concatenate([blocks[v, r : r + 1, :] for r in range(rows)], axis=1) for v in range(values)
     ]
     return jnp.concatenate(flat + [jnp.zeros((8 - values, rows * TILE), f32)], axis=0)
-
-
-def collect_kernel(rows, values_at, win_ref, perm_ref, out_ref, got_ref, send_sem, recv_sem):
-    pair = SidePair(
-        win_ref.at[values_at:, 0:rows],
-        win_ref.at[values_at:, 2 * rows : 3 * rows],
-        got_ref,
-        send_sem,
-        recv_sem,
-    )
-    greet(pair.partners, pair.flags)
-    pair.start()
-    pair.wait()
-    total = win_ref[values_at:, rows : 2 * rows] + pair.received(0) + pair.received(1)
-    out_ref[...] = reorder(in_lanes(total), perm_ref, 1)
-
-
-def collect_call(which, rows, values_at, window, perm):
-    values = window.shape[0] - values_at
-    return pl.pallas_call(
-        partial(collect_kernel, rows, values_at),
-        out_shape=jax.ShapeDtypeStruct((8, rows * TILE), f32),
-        in_specs=[vmem_spec()] * 2,
-        out_specs=vmem_spec(),
-        scratch_shapes=[
-            pltpu.VMEM((2, values, rows, TILE), f32),
-            pltpu.SemaphoreType.DMA((2,)),
-            pltpu.SemaphoreType.DMA((2,)),
-        ],
-        compiler_params=comm_params(which),
-        name="collect_%d" % which,
-    )(window, perm)
 
 
 def lane_sums(value):
@@ -1344,8 +1312,8 @@
     )(dens, coefficient, ordered, energy_one, coupling)
 
 
-def contract_back_kernel(coup_ref, coef_ref, mix_ref, site_ref, gfeat_ref, aux_ref, factor_ref, out_ref,
-                         grad_ref, f_ref, g_ref, ch_ref, row_ref, sem):
+def contract_back_kernel(values_at, coup_ref, coef_ref, mix_ref, site_ref, win_ref, perm_ref, aux_ref, factor_ref,
+                         out_ref, grad_ref, f_ref, g_ref, ch_ref, row_ref, got_ref, sem, send_sem, recv_sem):
     step = pl.program_id(0)
     factors, quantum, atoms = f_ref.shape
     chunks = quantum // QB
@@ -1356,11 +1324,23 @@
 
     @pl.when(step == 0)
     def _():
+        tiles = got_ref.shape[2]
+        pair = SidePair(
+            win_ref.at[values_at:, 0:tiles],
+            win_ref.at[values_at:, 2 * tiles : 3 * tiles],
+            got_ref,
+            send_sem,
+            recv_sem,
+        )
+        greet(pair.partners, pair.flags)
+        pair.start()
         for chunk in range(chunks):
             load(chunk).start()
         onehot = onehot_rows(site_ref[3:4, :])
         scale = aux_ref[8:9, :]
-        gfeat = gfeat_ref[...]
+        pair.wait()
+        total = win_ref[values_at:, tiles : 2 * tiles] + pair.received(0) + pair.received(1)
+        gfeat = reorder(in_lanes(total), perm_ref, 1)
         dot = jnp.sum(aux_ref[0:8, :] * gfeat, axis=0, keepdims=True)
         shrink = jnp.broadcast_to(scale * scale * scale * dot * (1.0 / quantum), (8, atoms))
         scaled = split3(scale * gfeat)
@@ -1402,12 +1382,12 @@
     out_ref[...] = total
 
 
-def contract_back_call(coupling, coefficient, mixing_rows, ordered, gfeat, aux, factor):
+def contract_back_call(which, values_at, coupling, coefficient, mixing_rows, ordered, window, perm, aux, factor):
     factors, depth, quantum = coupling.shape
     atoms = ordered.shape[1]
     rows = depth // 5
     return pl.pallas_call(
-        contract_back_kernel,
+        partial(contract_back_kernel, values_at),
         out_shape=(
             jax.ShapeDtypeStruct((depth, atoms), f32),
             jax.ShapeDtypeStruct((8, quantum), f32),
@@ -1418,7 +1398,8 @@
             whole_spec(coefficient.shape),
             whole_spec(mixing_rows.shape),
             whole_spec(ordered.shape),
-            whole_spec(gfeat.shape),
+            whole_spec(window.shape),
+            whole_spec(perm.shape),
             whole_spec(aux.shape),
             pl.BlockSpec(memory_space=pl.ANY),
         ],
@@ -1428,11 +1409,14 @@
             pltpu.VMEM((factors, quantum, atoms), bf16),
             pltpu.VMEM((QB, atoms), f32),
             pltpu.VMEM((72, quantum), bf16),
+            pltpu.VMEM((2, window.shape[0] - values_at, atoms // TILE, TILE), f32),
             pltpu.SemaphoreType.DMA((quantum // QB,)),
+            pltpu.SemaphoreType.DMA((2,)),
+            pltpu.SemaphoreType.DMA((2,)),
         ],
-        compiler_params=pltpu.CompilerParams(vmem_limit_bytes=VMEM_ALL),
+        compiler_params=comm_params(which),
         name="contract_back_1",
-    )(coupling, coefficient, mixing_rows, ordered, gfeat, aux, factor)
+    )(coupling, coefficient, mixing_rows, ordered, window, perm, aux, factor)
 
 
 def per_device(
@@ -1471,9 +1455,17 @@
     window_two, own_two, radial_second = backward_call(
         2, info, radial_two, geo, feat, index, weight, grad_dens_two, table_two, ordered
     )
-    grad_features = collect_call(2, tiles, 3, window_two.reshape(NVAL, WSTEP, TILE), perm)
     grad_dens_one, mixing_gradient = contract_back_call(
-        coupling_one, coefficient_one, mixing_rows, ordered, grad_features, aux, factors_one
+        2,
+        3,
+        coupling_one,
+        coefficient_one,
+        mixing_rows,
+        ordered,
+        window_two.reshape(NVAL, WSTEP, TILE),
+        perm,
+        aux,
+        factors_one,
     )
     window_one, own_one, radial_first = backward_call(
         1, info, radial_one, geo, ordered, index, weight, grad_dens_one, window_two, own_two

time: 246 us -> 244 us (level)
    pallas_call x2 -> x1, Pallas kernels: 26.5 us -> 20.7 us  [contract_back_call(): pl.pallas_call(partial(contract_back_kernel, values_at), out_shape=(jax.S...]
    pallas_call x2, Pallas kernels: 78.4 us -> 81.6 us  [backward_call(): pl.pallas_call(partial(backward_kernel, layer), out_shape=(jax.ShapeDtype...]
where the time goes in v6:
time: 244 us; the launch traced here: 243 us
  Pallas kernels  243 us (100%)
    pallas_call x2, Pallas kernels, backward_call(): pl.pallas_call(partial(backward_kernel, layer), out_shape=(jax.ShapeDtype...  81.6 us
    pallas_call x2, Pallas kernels, density_call(): pl.pallas_call(partial(density_kernel, layer), out_shape=(jax.ShapeDtypeS...  56 us
    pallas_call x1, Pallas kernels, contract_two_call(): pl.pallas_call(contract_two_kernel, out_shape=(jax.ShapeDtypeStruct((step...  28.3 us
    pallas_call x1, Pallas kernels, finish_call(): pl.pallas_call(partial(finish_kernel, rows), out_shape=(jax.ShapeDtypeStr...  22.6 us
    pallas_call x1, Pallas kernels, contract_back_call(): pl.pallas_call(partial(contract_back_kernel, values_at), out_shape=(jax.S...  20.7 us
    pallas_call x1, Pallas kernels, contract_one_call(): pl.pallas_call(contract_one_kernel, out_shape=(jax.ShapeDtypeStruct((fact...  18.4 us
    pallas_call x1, Pallas kernels, prepare_call(): pl.pallas_call(prepare_kernel, out_shape=(jax.ShapeDtypeStruct((SPECIES *...  7.16 us
    pallas_call x1, Pallas kernels, spread_call(): pl.pallas_call(partial(spread_kernel, values), out_shape=jax.ShapeDtypeSt...  6.17 us

profile of v6, /device:TPU:0, one launch (start us, length us, event | category | flops | bytes accessed | tf_op | source)
XLA Modules:
  0.0 243.3 jit_solution(3357626524854211341)
XLA Ops:
  0.6 7.2 %prepare.1 = (f32[96,128]{1,0:T(8,128)}, s32[64,1024]{1,0:T(8,128)}, f32[64,1024]{1,0:T(8,128)}, f32[8,1024]{1,0:T(8,128)}, bf16[1024,1024]{1,0:T(8,128)(2,1)}, /*index=5*/s32[3,8]{1,0:T(4,128)}) custom-call(s32[1]{0:T(128)} %bitcast.1.first_ref, s32[1,1024]{1,0:T(1,128)} %cnt_ref.1, s32[48,1,1024]{2,1,0:T(1,128)} %nbr_ref.1, f32[3,1,1024]{2,1,0:T(1,128)} %spot_ref.1, ...), custom_call_target="tpu_custom_call" | custom-call | tf_op jit(solution)/shard_map/prepare/pallas_call | solution.py:549
  7.8 28.5 %density_1.1 = (bf16[1960,1024]{1,0:T(8,128)(2,1)}, f32[320,1024]{1,0:T(8,128)}) custom-call(s32[3,8]{1,0:T(4,128)} %get-tuple-element.45.info_ref, f32[10,12]{1,0:T(8,128)} %rad_ref.7, f32[96,128]{1,0:T(8,128)} %get-tuple-element.46.tab_ref, f32[8,1024]{1,0:T(8,128)} %get-tuple-element.47.cen_ref.site_ref.own_in_ref.feat_ref, ...), custom_call_target="tpu_custom_call" | custom-call | tf_op jit(solution)/shard_map/density_1/pallas_call | solution.py:789
  36.3 18.4 %contract_1.1 = (f32[4,512,1024]{2,1,0:T(8,128)}, f32[8,1024]{1,0:T(8,128)}, f32[8,1024]{1,0:T(8,128)}, f32[16,1024]{1,0:T(8,128)}, f32[8,512]{1,0:T(8,128)}) custom-call(bf16[1960,1024]{1,0:T(8,128)(2,1)} %get-tuple-element.51.dens_ref, bf16[4,1960,512]{2,1,0:T(8,128)(2,1)} %coup_ref.5, f32[4,512]{1,0:T(4,128)} %coef_ref.5, f32[4,512]{1,0:T(4,128)} %bitcast.9, ...), custom_call_target="tpu_custom_call" | custom-call | tf_op jit(solution)/shard_map/contract_1/pallas_call | solution.py:1165
  54.8 6.2 %spread_1.1.tab_ref.win_in_ref = f32[96,128]{1,0:T(8,128)} custom-call(f32[8,1024]{1,0:T(8,128)} %get-tuple-element.52.x_ref, bf16[1024,1024]{1,0:T(8,128)(2,1)} %get-tuple-element.53.perm_ref), custom_call_target="tpu_custom_call" | custom-call | tf_op jit(solution)/shard_map/spread_1/pallas_call | solution.py:171
  60.9 27.4 %density_2.1 = (bf16[1960,1024]{1,0:T(8,128)(2,1)}, f32[256,1024]{1,0:T(8,128)}) custom-call(s32[3,8]{1,0:T(4,128)} %get-tuple-element.45.info_ref, f32[10,12]{1,0:T(8,128)} %rad_ref.6, f32[96,128]{1,0:T(8,128)} %spread_1.1.tab_ref.win_in_ref, f32[8,1024]{1,0:T(8,128)} %get-tuple-element.47.cen_ref.site_ref.own_in_ref.feat_ref, ...), custom_call_target="tpu_custom_call" | custom-call | tf_op jit(solution)/shard_map/density_2/pallas_call | solution.py:789
  88.4 28.3 %contract_2.1 = (f32[2000,1024]{1,0:T(8,128)}, f32[8,512]{1,0:T(8,128)}, f32[8,512]{1,0:T(8,128)}) custom-call(bf16[1960,1024]{1,0:T(8,128)(2,1)} %get-tuple-element.55.dens_ref, f32[4,512]{1,0:T(4,128)} %coef_ref.4, f32[8,1024]{1,0:T(8,128)} %get-tuple-element.47.cen_ref.site_ref.own_in_ref.feat_ref, f32[8,1024]{1,0:T(8,128)} %get-tuple-element.56.before_ref, ...), custom_call_target="tpu_custom_call" | custom-call | tf_op jit(solution)/shard_map/contract_2/pallas_call | solution.py:1282
  116.7 49.3 %backward_2.1 = (f32[280,128]{1,0:T(8,128)}, f32[8,1024]{1,0:T(8,128)}, f32[120,128]{1,0:T(8,128)}) custom-call(s32[3,8]{1,0:T(4,128)} %get-tuple-element.45.info_ref, f32[10,12]{1,0:T(8,128)} %rad_ref.6, f32[320,1024]{1,0:T(8,128)} %get-tuple-element.50.refs_0_.geo_ref, f32[256,1024]{1,0:T(8,128)} %get-tuple-element.54.feat_ref, ...), custom_call_target="tpu_custom_call" | custom-call | tf_op jit(solution)/shard_map/backward_2/pallas_call | solution.py:1041
  166.0 20.7 %contract_back_1.1 = (f32[1960,1024]{1,0:T(8,128)}, f32[8,512]{1,0:T(8,128)}) custom-call(bf16[4,1960,512]{2,1,0:T(8,128)(2,1)} %coup_ref.5, f32[4,512]{1,0:T(4,128)} %coef_ref.5, f32[4,512]{1,0:T(4,128)} %bitcast.10, f32[8,1024]{1,0:T(8,128)} %get-tuple-element.47.cen_ref.site_ref.own_in_ref.feat_ref, f32[7,40,128]{2,1,0:T(8,128)} %bitcast.7, ...), custom_call_target="tpu_custom_call" | custom-call | tf_op jit(solution)/shard_map/contract_back_1/pallas_call | solution.py:1389
  186.7 32.3 %backward_1.1 = (f32[120,128]{1,0:T(8,128)}, f32[8,1024]{1,0:T(8,128)}, f32[120,128]{1,0:T(8,128)}) custom-call(s32[3,8]{1,0:T(4,128)} %get-tuple-element.45.info_ref, f32[10,12]{1,0:T(8,128)} %rad_ref.7, f32[320,1024]{1,0:T(8,128)} %get-tuple-element.50.refs_0_.geo_ref, f32[8,1024]{1,0:T(8,128)} %get-tuple-element.47.cen_ref.site_ref.own_in_ref.feat_ref, ...), custom_call_target="tpu_custom_call" | custom-call | tf_op jit(solution)/shard_map/backward_1/pallas_call | solution.py:1041
  219.0 22.6 %finish_3.1 = (f32[8,1024]{1,0:T(8,128)}, f32[16,512]{1,0:T(8,128)}, f32[16,512]{1,0:T(8,128)}) custom-call(f32[3,40,128]{2,1,0:T(8,128)} %bitcast.8, f32[8,1024]{1,0:T(8,128)} %get-tuple-element.64.own_ref, bf16[1024,1024]{1,0:T(8,128)(2,1)} %get-tuple-element.53.perm_ref, f32[8,512]{1,0:T(8,128)} %get-tuple-element.65.first_ref, ...), custom_call_target="tpu_custom_call" | custom-call | tf_op jit(solution)/shard_map/finish_3/pallas_call | solution.py:284
  241.6 1.7 tail.1
